TPU v7x, 512 devices: a 8x2x16 block of a 8x16x16 slice. The times are simulated.
512 devices in a mesh: groups: 2 (over y), expert: 32 (over z, core), dp: 8 (over x).
Axes of the slice: x: 8, y: 2, z: 16, core: 2. Of those that a mesh axis runs over, the one named last changes fastest.
The devices are a block of a 8x16x16 slice.
Arguments:
- tokens: bfloat16 [4096, 2048], P(('groups', 'expert'), 'dp'), parts along dimension 0, may hold values from -6 to 6
- expert_ids: int32 [4096, 8], P(('groups', 'expert')), parts along dimension 0, may hold values from 0 to 63, all different within a row; in each aligned block of 64 rows (0 to 63, 64 to 127, ...) at most 16 rows name the same one
- gate_levels: int32 [4096, 8], P(('groups', 'expert')), parts along dimension 0, may hold values from 1 to 255
- gate_weight: bfloat16 [64, 2048, 1536], P('expert', None, 'dp'), may hold values from -0.125 to 0.125
- up_weight: bfloat16 [64, 2048, 1536], P('expert', None, 'dp'), may hold values from -0.125 to 0.125
- down_weight: bfloat16 [64, 1536, 2048], P('expert', None, 'dp'), may hold values from -0.15625 to 0.15625
Outputs:
- mixed: bfloat16 [4096, 2048], P(('groups', 'expert'), 'dp'), parts along dimension 0
There are 2 independent parts, one for each index of `groups`. A program takes and returns all parts, laid end to end along the dimension named above; an argument that names none is the same for every part. Nothing has to cross between parts.
Inputs may be any that keep to these rules, and one draw needn't show every extreme that they name: `expert_ids`: each row names 8 different experts. Among the rows of one index of the expert axis no expert is named more than 16 times, a bound that some block reaches.
All inputs are finite; a program needn't handle non-finite values.
Results may differ from a plain program's by a relative error of at most 0.0057.
Values may be sent and summed in bfloat16 or wider, within the bound.
No kernel may reach another device: no remote copies, remote signals or barrier semaphores. Data moves between devices by JAX's collectives and lax.ppermute only.
A program may use at most 64 MiB of HBM per device.

v0:
```python
import jax
import jax.numpy as jnp
from jax import lax
from jax.experimental import pallas as pl
from jax.experimental.pallas import tpu as pltpu
from jax.sharding import Mesh, PartitionSpec as P


CORES = 2


def swap(block):
    return lax.ppermute(block, "core", [(0, 1), (1, 0)])


def onward(block):
    count = lax.axis_size("dp")
    up = [(i, (i + 1) % count) for i in range(count)]
    down = [(count + i, count + (i - 1) % count) for i in range(count)]
    return lax.ppermute(block, ("core", "dp"), up + down)


def positions(member):
    count = member.shape[-1]
    row = lax.broadcasted_iota(jnp.int32, (count, count), 0)
    col = lax.broadcasted_iota(jnp.int32, (count, count), 1)
    before = (row < col).astype(jnp.bfloat16)
    return jnp.einsum(
        "...i,ij->...j", member.astype(jnp.bfloat16), before, preferred_element_type=jnp.float32
    ).astype(jnp.int32)


def weighted_sum(parts, steps, weights, table, kind, extra=(), finish=None, out=None):
    chip_experts = parts[0].shape[0]
    hid, rows = None, None
    exp_dev = weights[0][0].shape[0]
    last = table.shape[0] - 1
    n_parts, n_kinds = len(parts), len(weights)

    def place(core):
        return lambda e, t: jnp.clip(e - exp_dev * core(t), 0, exp_dev - 1)

    ours = place(lambda t: t[last])
    theirs = place(lambda t: 1 - t[last])
    if kind == "in":
        hid, width = weights[0][0].shape[1], parts[0].shape[2]
        block = (1, hid, width)
        where = lambda pick, k: lambda e, t: (pick(e, t), 0, t[k])
        rows = parts[0].shape[1]
        sum_shape = (n_kinds * hid, rows)
        dims = (((1,), (1,)), ((), ()))
    else:
        hid, width = parts[0].shape[1], weights[0][0].shape[2]
        block = (1, hid, width)
        where = lambda pick, k: lambda e, t: (pick(e, t), t[k], 0)
        rows = parts[0].shape[2]
        sum_shape = (rows, width)
        dims = (((0,), (0,)), ((), ()))

    in_specs = [pl.BlockSpec((1, *p.shape[1:]), lambda e, t: (e, 0, 0)) for p in parts]
    operands = list(parts)
    for k in steps:
        for first, second in weights:
            in_specs += [pl.BlockSpec(block, where(ours, k)), pl.BlockSpec(block, where(theirs, k))]
            operands += [first, second]
    for more in extra:
        in_specs.append(pl.BlockSpec((1, *sum_shape), lambda e, t: (e, 0, 0)))
        operands.append(more)
    if out is None:
        out_shape = jax.ShapeDtypeStruct((chip_experts, *sum_shape), jnp.float32)
        out_spec = pl.BlockSpec((1, *sum_shape), lambda e, t: (e, 0, 0))
    else:
        out_shape, out_spec = out

    def body(table_ref, *refs):
        part_refs, rest = refs[:n_parts], refs[n_parts:]
        weight_refs, rest = rest[: 2 * n_parts * n_kinds], rest[2 * n_parts * n_kinds :]
        extra_refs, out_ref = rest[:-1], rest[-1]
        mine = pl.program_id(0) // exp_dev == table_ref[last]
        sums = []
        for kind_at in range(n_kinds):
            total = None
            for k in range(n_parts):
                at = 2 * (k * n_kinds + kind_at)
                weight = jnp.where(mine, weight_refs[at][0], weight_refs[at + 1][0])
                pair = (weight, part_refs[k][0]) if kind == "in" else (part_refs[k][0], weight)
                term = lax.dot_general(*pair, dims, preferred_element_type=jnp.float32)
                total = term if total is None else total + term
            if kind == "in":
                for ref in extra_refs:
                    total = total + ref[0, kind_at * hid : (kind_at + 1) * hid]
            else:
                for ref in extra_refs:
                    total = total + ref[0]
            sums.append(total)
        if finish is not None:
            finish(out_ref, *sums)
        elif kind == "in":
            for kind_at, total in enumerate(sums):
                out_ref[0, kind_at * hid : (kind_at + 1) * hid] = total
        else:
            out_ref[0] = sums[0]

    flops = 2 * chip_experts * n_parts * n_kinds * rows * hid * width
    moved = n_parts * chip_experts * (n_kinds * hid * width + parts[0].size // chip_experts) * 2
    return pl.pallas_call(
        body,
        grid_spec=pltpu.PrefetchScalarGridSpec(
            num_scalar_prefetch=1, grid=(chip_experts,), in_specs=in_specs, out_specs=out_spec
        ),
        out_shape=out_shape,
        compiler_params=pltpu.CompilerParams(vmem_limit_bytes=16 * 2**20),
        cost_estimate=pl.CostEstimate(flops=flops, bytes_accessed=moved, transcendentals=0),
    )(table, *operands)


def gather_sum(own, weights, table, kind, finish, out):
    half = lax.axis_size("dp") // 2
    mine = [own]
    for _ in range(1, half + 1):
        mine.append(onward(mine[-1]))
    other = [swap(own)]
    for _ in range(1, half):
        other.append(onward(other[-1]))
    early = weighted_sum(mine[:half], range(half), weights, table, kind)
    aside = weighted_sum(other[1:], range(1, half), weights, table, kind)
    back = swap(aside)
    return weighted_sum(mine[half:], [half], weights, table, kind, (early, back), finish, out)


def layer(tokens, expert_ids, gate_levels, gate_weight, up_weight, down_weight):
    tok_dev, width = tokens.shape
    picks = expert_ids.shape[1]
    exp_dev = gate_weight.shape[0]
    hid = gate_weight.shape[2]
    n_z = lax.axis_size("z")
    chip_experts = exp_dev * CORES
    experts = chip_experts * n_z
    capacity = min(tok_dev, max(2, 2 * tok_dev * picks // experts))
    core = lax.axis_index("core")
    z = lax.axis_index("z")

    ids_rows = jnp.zeros((2 * picks, width), jnp.bfloat16)
    ids_rows = ids_rows.at[:picks, :tok_dev].set(expert_ids.T.astype(jnp.bfloat16))
    gathered = lax.all_gather(jnp.concatenate([tokens, ids_rows], axis=0), "z", axis=0)
    all_tokens = gathered[:, :tok_dev]
    all_ids = gathered[:, tok_dev : tok_dev + picks, :tok_dev].astype(jnp.int32)

    names = z * chip_experts + jnp.arange(chip_experts, dtype=jnp.int32)
    member = jnp.any(all_ids[:, None, :, :] == names[None, :, None, None], axis=2)
    spot = jnp.where(member, positions(member), -1)
    chosen = spot[:, :, None, :] == jnp.arange(capacity, dtype=jnp.int32)[None, None, :, None]
    rows = jnp.einsum(
        "sepj,sjd->espd",
        chosen.astype(jnp.bfloat16),
        all_tokens,
        preferred_element_type=jnp.float32,
    ).astype(jnp.bfloat16)
    count = n_z * capacity
    rows = rows.reshape(chip_experts, count, width)

    pairs = []
    for weights in (jnp.swapaxes(gate_weight, 1, 2), jnp.swapaxes(up_weight, 1, 2), down_weight):
        pairs.append((weights, swap(weights)))

    n_dp = lax.axis_size("dp")
    step = jnp.arange(n_dp, dtype=jnp.int32)
    owners = (lax.axis_index("dp") + jnp.where(core == 0, -step, step)) % n_dp
    table = jnp.where(step == n_dp - 1, core, owners)

    def gated(out_ref, gate_sum, up_sum):
        out_ref[0] = (gate_sum / (1.0 + jnp.exp(-gate_sum)) * up_sum).astype(jnp.bfloat16)

    hidden = gather_sum(
        rows,
        pairs[:2],
        table,
        "in",
        gated,
        (
            jax.ShapeDtypeStruct((chip_experts, hid, count), jnp.bfloat16),
            pl.BlockSpec((1, hid, count), lambda e, t: (e, 0, 0)),
        ),
    )

    out_features = down_weight.shape[2]

    def returning(out_ref, total):
        out_ref[:, 0] = total.astype(jnp.bfloat16).reshape(n_z, capacity, out_features)

    result = gather_sum(
        hidden,
        pairs[2:],
        table,
        "out",
        returning,
        (
            jax.ShapeDtypeStruct((n_z, chip_experts, capacity, out_features), jnp.bfloat16),
            pl.BlockSpec((n_z, 1, capacity, out_features), lambda e, t: (0, e, 0, 0)),
        ),
    )
    returned = lax.all_to_all(result, "z", split_axis=0, concat_axis=0, tiled=True)
    slot_count = experts * capacity
    returned = returned.reshape(slot_count, out_features)

    own_ids = expert_ids.T
    names = jnp.arange(experts, dtype=jnp.int32)
    named = own_ids[None, :, :] == names[:, None, None]
    own_spot = positions(jnp.any(named, axis=1))
    shares = gate_levels.astype(jnp.float32) / 256.0
    factor = jnp.sum(jnp.where(named, shares.T[None, :, :], 0.0), axis=1)
    weighting = jnp.where(
        own_spot[:, None, :] == jnp.arange(capacity, dtype=jnp.int32)[None, :, None],
        factor[:, None, :],
        0.0,
    ).astype(jnp.bfloat16)
    weighting = weighting.reshape(slot_count, tok_dev)
    combined = jnp.einsum("sj,sd->jd", weighting, returned, preferred_element_type=jnp.float32)
    return combined.astype(jnp.bfloat16)


def solution(mesh):
    groups, expert, dp = (mesh.shape[name] for name in ("groups", "expert", "dp"))
    split = Mesh(
        mesh.devices.reshape(groups, expert // CORES, CORES, dp), ("groups", "z", "core", "dp")
    )
    rows, held = ("groups", "z", "core"), ("z", "core")
    in_specs = (
        P(rows, "dp"),
        P(rows, None),
        P(rows, None),
        P(held, None, "dp"),
        P(held, None, "dp"),
        P(held, None, "dp"),
    )
    return jax.shard_map(
        layer, mesh=split, in_specs=in_specs, out_specs=P(rows, "dp"), check_vma=False
    )
```

profile of v0, /device:TPU:70, one launch (start us, length us, event | category | flops | bytes accessed | tf_op | source)
XLA Modules:
  0.0 249.3 jit_solution(2449974530626640146)
XLA Ops:
  1.6 71.7 %all-gather = bf16[1280,256]{1,0:T(8,128)(2,1)S(1)} all-gather(bf16[80,256]{1,0:T(8,128)(2,1)S(1)} %fusion.4), channel_id=2, replica_groups=mesh['groups'=2,'z'=16,'core'=2,'dp'=8] {'z'}, dimensions={0}, use_global_device_ids=true | all-gather | bytes 696320 | tf_op jit(solution)/shard_map/all_gather | solution.py:145
  79.1 4.8 %collective-permute-start.7 = (bf16[4,256,256]{2,1,0:T(8,128)(2,1)S(1)}, bf16[4,256,256]{2,1,0:T(8,128)(2,1)S(1)}, u32[]{:S(2)}, u32[]{:S(2)}) collective-permute-start(bf16[4,256,256]{2,1,0:T(8,128)(2,1)S(1)} %collective-permute-done.6), channel_id=1, source_target_pairs={{0,1},{1,2},{2,3},{3,4},{4,5},{5,6},{6,7},{7,0},{8,15},{9,8},{10,9... | collective-permute-start | bytes 1572872 | tf_op jit(solution)/shard_map/ppermute | solution.py:20
  85.9 4.7 %collective-permute-done.7.refs_0_ = bf16[4,256,256]{2,1,0:T(8,128)(2,1)S(1)} collective-permute-done((bf16[4,256,256]{2,1,0:T(8,128)(2,1)S(1)}, bf16[4,256,256]{2,1,0:T(8,128)(2,1)S(1)}, u32[]{:S(2)}, u32[]{:S(2)}) %collective-permute-start.7) | collective-permute-done | bytes 524320 | tf_op jit(solution)/shard_map/ppermute | solution.py:20
  90.6 5.6 %collective-permute-start.8 = (bf16[4,256,256]{2,1,0:T(8,128)(2,1)S(1)}, bf16[4,256,256]{2,1,0:T(8,128)(2,1)}, u32[]{:S(2)}, u32[]{:S(2)}) collective-permute-start(bf16[4,256,256]{2,1,0:T(8,128)(2,1)S(1)} %collective-permute-done.7.refs_0_), channel_id=1, source_target_pairs={{0,1},{1,2},{2,3},{3,4},{4,5},{5,6},{6,7},{7,0},{8,15},{9,8},{10,9... | collective-permute-start | bytes 1572872 | tf_op jit(solution)/shard_map/ppermute | solution.py:20
  99.0 3.9 %collective-permute-done.8.refs_1_ = bf16[4,256,256]{2,1,0:T(8,128)(2,1)} collective-permute-done((bf16[4,256,256]{2,1,0:T(8,128)(2,1)S(1)}, bf16[4,256,256]{2,1,0:T(8,128)(2,1)}, u32[]{:S(2)}, u32[]{:S(2)}) %collective-permute-start.8) | collective-permute-done | bytes 524320 | tf_op jit(solution)/shard_map/ppermute | solution.py:20
  102.9 5.7 %collective-permute-start.9 = (bf16[4,256,256]{2,1,0:T(8,128)(2,1)}, bf16[4,256,256]{2,1,0:T(8,128)(2,1)}, u32[]{:S(2)}, u32[]{:S(2)}) collective-permute-start(bf16[4,256,256]{2,1,0:T(8,128)(2,1)} %collective-permute-done.8.refs_1_), channel_id=1, source_target_pairs={{0,1},{1,2},{2,3},{3,4},{4,5},{5,6},{6,7},{7,0},{8,15},{9,8},{10,9... | collective-permute-start | bytes 1572872 | tf_op jit(solution)/shard_map/ppermute | solution.py:20
  108.7 5.6 %collective-permute-start.1 = (bf16[4,256,256]{2,1,0:T(8,128)(2,1)}, bf16[4,256,256]{2,1,0:T(8,128)(2,1)S(1)}, u32[]{:S(2)}, u32[]{:S(2)}) collective-permute-start(bf16[4,256,256]{2,1,0:T(8,128)(2,1)} %collective-permute-done.refs_1_), channel_id=1, source_target_pairs={{0,1},{1,2},{2,3},{3,4},{4,5},{5,6},{6,7},{7,0},{8,15},{9,8},{10,9... | collective-permute-start | bytes 1572872 | tf_op jit(solution)/shard_map/ppermute | solution.py:20
  116.7 4.7 %shard_map.65 = f32[4,384,256]{2,1,0:T(8,128)S(1)} custom-call(s32[8]{0:T(128)S(1)} %compare_select_fusion.2.table_ref, bf16[4,256,256]{2,1,0:T(8,128)(2,1)S(1)} %copy-done.4, bf16[4,256,256]{2,1,0:T(8,128)(2,1)} %collective-permute-done.8.refs_1_, bf16[4,256,256]{2,1,0:T(8,128)(2,1)} %collective-permute-done.9.refs_2_, bf16[2,192,2048]{2,1,0:T(8,128)(2,1)S(1)} %bitcast.24, ...), custom_call_target="tpu_custom_call" | custom-call | flops 603979776 | bytes 3932160 | tf_op jit(solution)/shard_map/pallas_call | solution.py:106
  123.3 5.6 %collective-permute-start.2 = (bf16[4,256,256]{2,1,0:T(8,128)(2,1)S(1)}, bf16[4,256,256]{2,1,0:T(8,128)(2,1)S(1)}, u32[]{:S(2)}, u32[]{:S(2)}) collective-permute-start(bf16[4,256,256]{2,1,0:T(8,128)(2,1)S(1)} %collective-permute-done.1.refs_2_), channel_id=1, source_target_pairs={{0,1},{1,2},{2,3},{3,4},{4,5},{5,6},{6,7},{7,0},{8,15},{9,8},{10,9... | collective-permute-start | bytes 1572872 | tf_op jit(solution)/shard_map/ppermute | solution.py:20
  129.0 6.7 %collective-permute-done.2.refs_3_ = bf16[4,256,256]{2,1,0:T(8,128)(2,1)S(1)} collective-permute-done((bf16[4,256,256]{2,1,0:T(8,128)(2,1)S(1)}, bf16[4,256,256]{2,1,0:T(8,128)(2,1)S(1)}, u32[]{:S(2)}, u32[]{:S(2)}) %collective-permute-start.2) | collective-permute-done | bytes 524320 | tf_op jit(solution)/shard_map/ppermute | solution.py:20
  135.7 5.6 %collective-permute-start.3 = (bf16[4,256,256]{2,1,0:T(8,128)(2,1)S(1)}, bf16[4,256,256]{2,1,0:T(8,128)(2,1)S(1)}, u32[]{:S(2)}, u32[]{:S(2)}) collective-permute-start(bf16[4,256,256]{2,1,0:T(8,128)(2,1)S(1)} %collective-permute-done.2.refs_3_), channel_id=1, source_target_pairs={{0,1},{1,2},{2,3},{3,4},{4,5},{5,6},{6,7},{7,0},{8,15},{9,8},{10,9... | collective-permute-start | bytes 1572872 | tf_op jit(solution)/shard_map/ppermute | solution.py:20
  141.3 5.3 %shard_map.64.refs_5_ = f32[4,384,256]{2,1,0:T(8,128)S(1)} custom-call(s32[8]{0:T(128)S(1)} %compare_select_fusion.2.table_ref, bf16[4,256,256]{2,1,0:T(8,128)(2,1)} %bitcast.8.refs_0_, bf16[4,256,256]{2,1,0:T(8,128)(2,1)} %collective-permute-done.refs_1_, bf16[4,256,256]{2,1,0:T(8,128)(2,1)S(1)} %collective-permute-done.1.refs_2_, ...), custom_call_target="tpu_custom_call" | custom-call | flops 805306368 | bytes 5242880 | tf_op jit(solution)/shard_map/pallas_call | solution.py:106
  148.0 3.5 %shard_map.66.refs_0_ = bf16[4,192,256]{2,1,0:T(8,128)(2,1)S(1)} custom-call(s32[8]{0:T(128)S(1)} %compare_select_fusion.2.table_ref, bf16[4,256,256]{2,1,0:T(8,128)(2,1)S(1)} %collective-permute-done.3.refs_0_, bf16[2,192,2048]{2,1,0:T(8,128)(2,1)S(1)} %bitcast.31, ...), custom_call_target="tpu_custom_call" | custom-call | flops 201326592 | bytes 1310720 | tf_op jit(solution)/shard_map/pallas_call | solution.py:106
  155.9 5.6 %collective-permute-start.17 = (bf16[4,192,256]{2,1,0:T(8,128)(2,1)S(1)}, bf16[4,192,256]{2,1,0:T(8,128)(2,1)S(1)}, u32[]{:S(2)}, u32[]{:S(2)}) collective-permute-start(bf16[4,192,256]{2,1,0:T(8,128)(2,1)S(1)} %collective-permute-done.16), channel_id=1, source_target_pairs={{0,1},{1,2},{2,3},{3,4},{4,5},{5,6},{6,7},{7,0},{8,15},{9,8},{10,9... | collective-permute-start | bytes 1179656 | tf_op jit(solution)/shard_map/ppermute | solution.py:20
  161.5 5.3 %collective-permute-done.17.refs_0_ = bf16[4,192,256]{2,1,0:T(8,128)(2,1)S(1)} collective-permute-done((bf16[4,192,256]{2,1,0:T(8,128)(2,1)S(1)}, bf16[4,192,256]{2,1,0:T(8,128)(2,1)S(1)}, u32[]{:S(2)}, u32[]{:S(2)}) %collective-permute-start.17) | collective-permute-done | bytes 393248 | tf_op jit(solution)/shard_map/ppermute | solution.py:20
  166.8 5.6 %collective-permute-start.18 = (bf16[4,192,256]{2,1,0:T(8,128)(2,1)S(1)}, bf16[4,192,256]{2,1,0:T(8,128)(2,1)S(1)}, u32[]{:S(2)}, u32[]{:S(2)}) collective-permute-start(bf16[4,192,256]{2,1,0:T(8,128)(2,1)S(1)} %collective-permute-done.17.refs_0_), channel_id=1, source_target_pairs={{0,1},{1,2},{2,3},{3,4},{4,5},{5,6},{6,7},{7,0},{8,15},{9,8},{10,9... | collective-permute-start | bytes 1179656 | tf_op jit(solution)/shard_map/ppermute | solution.py:20
  174.4 3.3 %collective-permute-done.18.refs_1_ = bf16[4,192,256]{2,1,0:T(8,128)(2,1)S(1)} collective-permute-done((bf16[4,192,256]{2,1,0:T(8,128)(2,1)S(1)}, bf16[4,192,256]{2,1,0:T(8,128)(2,1)S(1)}, u32[]{:S(2)}, u32[]{:S(2)}) %collective-permute-start.18) | collective-permute-done | bytes 393248 | tf_op jit(solution)/shard_map/ppermute | solution.py:20
  177.7 5.6 %collective-permute-start.19 = (bf16[4,192,256]{2,1,0:T(8,128)(2,1)S(1)}, bf16[4,192,256]{2,1,0:T(8,128)(2,1)S(1)}, u32[]{:S(2)}, u32[]{:S(2)}) collective-permute-start(bf16[4,192,256]{2,1,0:T(8,128)(2,1)S(1)} %collective-permute-done.18.refs_1_), channel_id=1, source_target_pairs={{0,1},{1,2},{2,3},{3,4},{4,5},{5,6},{6,7},{7,0},{8,15},{9,8},{10,9... | collective-permute-start | bytes 1179656 | tf_op jit(solution)/shard_map/ppermute | solution.py:20
  183.3 4.2 %collective-permute-start.12 = (bf16[4,192,256]{2,1,0:T(8,128)(2,1)S(1)}, bf16[4,192,256]{2,1,0:T(8,128)(2,1)S(1)}, u32[]{:S(2)}, u32[]{:S(2)}) collective-permute-start(bf16[4,192,256]{2,1,0:T(8,128)(2,1)S(1)} %collective-permute-done.11.refs_1_), channel_id=1, source_target_pairs={{0,1},{1,2},{2,3},{3,4},{4,5},{5,6},{6,7},{7,0},{8,15},{9,8},{10,9... | collective-permute-start | bytes 1179656 | tf_op jit(solution)/shard_map/ppermute | solution.py:20
  193.0 5.4 %collective-permute-start.13 = (bf16[4,192,256]{2,1,0:T(8,128)(2,1)S(1)}, bf16[4,192,256]{2,1,0:T(8,128)(2,1)S(1)}, u32[]{:S(2)}, u32[]{:S(2)}) collective-permute-start(bf16[4,192,256]{2,1,0:T(8,128)(2,1)S(1)} %collective-permute-done.12.refs_2_), channel_id=1, source_target_pairs={{0,1},{1,2},{2,3},{3,4},{4,5},{5,6},{6,7},{7,0},{8,15},{9,8},{10,9... | collective-permute-start | bytes 1179656 | tf_op jit(solution)/shard_map/ppermute | solution.py:20
  198.4 5.3 %collective-permute-done.13.refs_3_ = bf16[4,192,256]{2,1,0:T(8,128)(2,1)S(1)} collective-permute-done((bf16[4,192,256]{2,1,0:T(8,128)(2,1)S(1)}, bf16[4,192,256]{2,1,0:T(8,128)(2,1)S(1)}, u32[]{:S(2)}, u32[]{:S(2)}) %collective-permute-start.13) | collective-permute-done | bytes 393248 | tf_op jit(solution)/shard_map/ppermute | solution.py:20
  203.7 5.6 %collective-permute-start.14 = (bf16[4,192,256]{2,1,0:T(8,128)(2,1)S(1)}, bf16[4,192,256]{2,1,0:T(8,128)(2,1)S(1)}, u32[]{:S(2)}, u32[]{:S(2)}) collective-permute-start(bf16[4,192,256]{2,1,0:T(8,128)(2,1)S(1)} %collective-permute-done.13.refs_3_), channel_id=1, source_target_pairs={{0,1},{1,2},{2,3},{3,4},{4,5},{5,6},{6,7},{7,0},{8,15},{9,8},{10,9... | collective-permute-start | bytes 1179656 | tf_op jit(solution)/shard_map/ppermute | solution.py:20
  217.2 4.0 %all-to-all-start = ((bf16[16,4,16,256]{3,2,1,0:T(8,128)(2,1)}), bf16[16,4,16,256]{3,2,1,0:T(8,128)(2,1)S(1)}, u32[]{:S(2)}, u32[]{:S(2)}) async-start(bf16[16,4,16,256]{3,2,1,0:T(8,128)(2,1)} %shard_map.69), calls=%async_computation | async-start | bytes 1048576 | tf_op jit(solution)/shard_map/all_to_all | solution.py:202
  221.7 26.8 %all-to-all-done = bf16[16,4,16,256]{3,2,1,0:T(8,128)(2,1)S(1)} async-done(((bf16[16,4,16,256]{3,2,1,0:T(8,128)(2,1)}), bf16[16,4,16,256]{3,2,1,0:T(8,128)(2,1)S(1)}, u32[]{:S(2)}, u32[]{:S(2)}) %all-to-all-start) | async-done | bytes 524320 | tf_op jit(solution)/shard_map/all_to_all | solution.py:202
  (57 shorter events, 38.8 us)
Async XLA Ops:
  0.7 83.2 %copy-start.2 = (bf16[2,2048,192]{1,2,0:T(8,128)(2,1)S(1)}, bf16[2,2048,192]{1,2,0:T(8,128)(2,1)}, u32[]{:S(2)}) copy-start(bf16[2,2048,192]{1,2,0:T(8,128)(2,1)} %param.12) | copy-start | bytes 4718596
  1.6 75.1 %copy-start.1 = (bf16[2,2048,192]{1,2,0:T(8,128)(2,1)S(1)}, bf16[2,2048,192]{1,2,0:T(8,128)(2,1)}, u32[]{:S(2)}) copy-start(bf16[2,2048,192]{1,2,0:T(8,128)(2,1)} %param.11) | copy-start | bytes 4718596
  74.7 4.4 %collective-permute-start.6 = (bf16[4,256,256]{2,1,0:T(8,128)(2,1)}, bf16[4,256,256]{2,1,0:T(8,128)(2,1)S(1)}, u32[]{:S(2)}, u32[]{:S(2)}) collective-permute-start(bf16[4,256,256]{2,1,0:T(8,128)(2,1)} %bitcast.8.refs_0_), channel_id=1, source_target_pairs={{0,8},{8,0},{1,9},{9,1},{2,10},{10,2},{3,11},{11,3},{4,12},{12,4},... | collective-permute-start | bytes 1572872 | tf_op jit(solution)/shard_map/ppermute | solution.py:13
  76.7 37.6 %collective-permute-start.4 = (bf16[2,192,2048]{2,1,0:T(8,128)(2,1)S(1)}, bf16[2,192,2048]{2,1,0:T(8,128)(2,1)}, u32[]{:S(2)}, u32[]{:S(2)}) collective-permute-start(bf16[2,192,2048]{2,1,0:T(8,128)(2,1)S(1)} %bitcast.23), channel_id=1, source_target_pairs={{0,8},{8,0},{1,9},{9,1},{2,10},{10,2},{3,11},{11,3},{4,12},{12,4},... | collective-permute-start | bytes 4718600 | tf_op jit(solution)/shard_map/ppermute | solution.py:13
  79.1 11.5 %collective-permute-start.7 = (bf16[4,256,256]{2,1,0:T(8,128)(2,1)S(1)}, bf16[4,256,256]{2,1,0:T(8,128)(2,1)S(1)}, u32[]{:S(2)}, u32[]{:S(2)}) collective-permute-start(bf16[4,256,256]{2,1,0:T(8,128)(2,1)S(1)} %collective-permute-done.6), channel_id=1, source_target_pairs={{0,1},{1,2},{2,3},{3,4},{4,5},{5,6},{6,7},{7,0},{8,15},{9,8},{10,9... | collective-permute-start | bytes 1572872 | tf_op jit(solution)/shard_map/ppermute | solution.py:20
  83.9 30.3 %collective-permute-start.5 = (bf16[2,192,2048]{2,1,0:T(8,128)(2,1)S(1)}, bf16[2,192,2048]{2,1,0:T(8,128)(2,1)}, u32[]{:S(2)}, u32[]{:S(2)}) collective-permute-start(bf16[2,192,2048]{2,1,0:T(8,128)(2,1)S(1)} %bitcast.32), channel_id=1, source_target_pairs={{0,8},{8,0},{1,9},{9,1},{2,10},{10,2},{3,11},{11,3},{4,12},{12,4},... | collective-permute-start | bytes 4718600 | tf_op jit(solution)/shard_map/ppermute | solution.py:13
  90.6 12.3 %collective-permute-start.8 = (bf16[4,256,256]{2,1,0:T(8,128)(2,1)S(1)}, bf16[4,256,256]{2,1,0:T(8,128)(2,1)}, u32[]{:S(2)}, u32[]{:S(2)}) collective-permute-start(bf16[4,256,256]{2,1,0:T(8,128)(2,1)S(1)} %collective-permute-done.7.refs_0_), channel_id=1, source_target_pairs={{0,1},{1,2},{2,3},{3,4},{4,5},{5,6},{6,7},{7,0},{8,15},{9,8},{10,9... | collective-permute-start | bytes 1572872 | tf_op jit(solution)/shard_map/ppermute | solution.py:20
  97.0 11.7 %collective-permute-start = (bf16[4,256,256]{2,1,0:T(8,128)(2,1)}, bf16[4,256,256]{2,1,0:T(8,128)(2,1)}, u32[]{:S(2)}, u32[]{:S(2)}) collective-permute-start(bf16[4,256,256]{2,1,0:T(8,128)(2,1)} %bitcast.8.refs_0_), channel_id=1, source_target_pairs={{0,1},{1,2},{2,3},{3,4},{4,5},{5,6},{6,7},{7,0},{8,15},{9,8},{10,9... | collective-permute-start | bytes 1572872 | tf_op jit(solution)/shard_map/ppermute | solution.py:20
  102.9 12.7 %collective-permute-start.9 = (bf16[4,256,256]{2,1,0:T(8,128)(2,1)}, bf16[4,256,256]{2,1,0:T(8,128)(2,1)}, u32[]{:S(2)}, u32[]{:S(2)}) collective-permute-start(bf16[4,256,256]{2,1,0:T(8,128)(2,1)} %collective-permute-done.8.refs_1_), channel_id=1, source_target_pairs={{0,1},{1,2},{2,3},{3,4},{4,5},{5,6},{6,7},{7,0},{8,15},{9,8},{10,9... | collective-permute-start | bytes 1572872 | tf_op jit(solution)/shard_map/ppermute | solution.py:20
  108.7 14.7 %collective-permute-start.1 = (bf16[4,256,256]{2,1,0:T(8,128)(2,1)}, bf16[4,256,256]{2,1,0:T(8,128)(2,1)S(1)}, u32[]{:S(2)}, u32[]{:S(2)}) collective-permute-start(bf16[4,256,256]{2,1,0:T(8,128)(2,1)} %collective-permute-done.refs_1_), channel_id=1, source_target_pairs={{0,1},{1,2},{2,3},{3,4},{4,5},{5,6},{6,7},{7,0},{8,15},{9,8},{10,9... | collective-permute-start | bytes 1572872 | tf_op jit(solution)/shard_map/ppermute | solution.py:20
  121.4 26.6 %collective-permute-start.10 = (f32[4,384,256]{2,1,0:T(8,128)S(1)}, f32[4,384,256]{2,1,0:T(8,128)S(1)}, u32[]{:S(2)}, u32[]{:S(2)}) collective-permute-start(f32[4,384,256]{2,1,0:T(8,128)S(1)} %shard_map.65), channel_id=1, source_target_pairs={{0,8},{8,0},{1,9},{9,1},{2,10},{10,2},{3,11},{11,3},{4,12},{12,4},... | collective-permute-start | bytes 4718600 | tf_op jit(solution)/shard_map/ppermute | solution.py:13
  123.3 12.3 %collective-permute-start.2 = (bf16[4,256,256]{2,1,0:T(8,128)(2,1)S(1)}, bf16[4,256,256]{2,1,0:T(8,128)(2,1)S(1)}, u32[]{:S(2)}, u32[]{:S(2)}) collective-permute-start(bf16[4,256,256]{2,1,0:T(8,128)(2,1)S(1)} %collective-permute-done.1.refs_2_), channel_id=1, source_target_pairs={{0,1},{1,2},{2,3},{3,4},{4,5},{5,6},{6,7},{7,0},{8,15},{9,8},{10,9... | collective-permute-start | bytes 1572872 | tf_op jit(solution)/shard_map/ppermute | solution.py:20
  135.7 12.3 %collective-permute-start.3 = (bf16[4,256,256]{2,1,0:T(8,128)(2,1)S(1)}, bf16[4,256,256]{2,1,0:T(8,128)(2,1)S(1)}, u32[]{:S(2)}, u32[]{:S(2)}) collective-permute-start(bf16[4,256,256]{2,1,0:T(8,128)(2,1)S(1)} %collective-permute-done.2.refs_3_), channel_id=1, source_target_pairs={{0,1},{1,2},{2,3},{3,4},{4,5},{5,6},{6,7},{7,0},{8,15},{9,8},{10,9... | collective-permute-start | bytes 1572872 | tf_op jit(solution)/shard_map/ppermute | solution.py:20
  151.5 4.4 %collective-permute-start.16 = (bf16[4,192,256]{2,1,0:T(8,128)(2,1)S(1)}, bf16[4,192,256]{2,1,0:T(8,128)(2,1)S(1)}, u32[]{:S(2)}, u32[]{:S(2)}) collective-permute-start(bf16[4,192,256]{2,1,0:T(8,128)(2,1)S(1)} %shard_map.66.refs_0_), channel_id=1, source_target_pairs={{0,8},{8,0},{1,9},{9,1},{2,10},{10,2},{3,11},{11,3},{4,12},{12,4},... | collective-permute-start | bytes 1179656 | tf_op jit(solution)/shard_map/ppermute | solution.py:13
  153.4 34.1 %collective-permute-start.15 = (bf16[2,1536,256]{2,1,0:T(8,128)(2,1)S(1)}, bf16[2,1536,256]{2,1,0:T(8,128)(2,1)S(1)}, u32[]{:S(2)}, u32[]{:S(2)}) collective-permute-start(bf16[2,1536,256]{2,1,0:T(8,128)(2,1)S(1)} %copy-done), channel_id=1, source_target_pairs={{0,8},{8,0},{1,9},{9,1},{2,10},{10,2},{3,11},{11,3},{4,12},{12,4},... | collective-permute-start | bytes 4718600 | tf_op jit(solution)/shard_map/ppermute | solution.py:13
  155.9 10.9 %collective-permute-start.17 = (bf16[4,192,256]{2,1,0:T(8,128)(2,1)S(1)}, bf16[4,192,256]{2,1,0:T(8,128)(2,1)S(1)}, u32[]{:S(2)}, u32[]{:S(2)}) collective-permute-start(bf16[4,192,256]{2,1,0:T(8,128)(2,1)S(1)} %collective-permute-done.16), channel_id=1, source_target_pairs={{0,1},{1,2},{2,3},{3,4},{4,5},{5,6},{6,7},{7,0},{8,15},{9,8},{10,9... | collective-permute-start | bytes 1179656 | tf_op jit(solution)/shard_map/ppermute | solution.py:20
  166.8 10.9 %collective-permute-start.18 = (bf16[4,192,256]{2,1,0:T(8,128)(2,1)S(1)}, bf16[4,192,256]{2,1,0:T(8,128)(2,1)S(1)}, u32[]{:S(2)}, u32[]{:S(2)}) collective-permute-start(bf16[4,192,256]{2,1,0:T(8,128)(2,1)S(1)} %collective-permute-done.17.refs_0_), channel_id=1, source_target_pairs={{0,1},{1,2},{2,3},{3,4},{4,5},{5,6},{6,7},{7,0},{8,15},{9,8},{10,9... | collective-permute-start | bytes 1179656 | tf_op jit(solution)/shard_map/ppermute | solution.py:20
  172.4 10.9 %collective-permute-start.11 = (bf16[4,192,256]{2,1,0:T(8,128)(2,1)S(1)}, bf16[4,192,256]{2,1,0:T(8,128)(2,1)S(1)}, u32[]{:S(2)}, u32[]{:S(2)}) collective-permute-start(bf16[4,192,256]{2,1,0:T(8,128)(2,1)S(1)} %shard_map.66.refs_0_), channel_id=1, source_target_pairs={{0,1},{1,2},{2,3},{3,4},{4,5},{5,6},{6,7},{7,0},{8,15},{9,8},{10,9... | collective-permute-start | bytes 1179656 | tf_op jit(solution)/shard_map/ppermute | solution.py:20
  177.7 10.9 %collective-permute-start.19 = (bf16[4,192,256]{2,1,0:T(8,128)(2,1)S(1)}, bf16[4,192,256]{2,1,0:T(8,128)(2,1)S(1)}, u32[]{:S(2)}, u32[]{:S(2)}) collective-permute-start(bf16[4,192,256]{2,1,0:T(8,128)(2,1)S(1)} %collective-permute-done.18.refs_1_), channel_id=1, source_target_pairs={{0,1},{1,2},{2,3},{3,4},{4,5},{5,6},{6,7},{7,0},{8,15},{9,8},{10,9... | collective-permute-start | bytes 1179656 | tf_op jit(solution)/shard_map/ppermute | solution.py:20
  183.3 9.7 %collective-permute-start.12 = (bf16[4,192,256]{2,1,0:T(8,128)(2,1)S(1)}, bf16[4,192,256]{2,1,0:T(8,128)(2,1)S(1)}, u32[]{:S(2)}, u32[]{:S(2)}) collective-permute-start(bf16[4,192,256]{2,1,0:T(8,128)(2,1)S(1)} %collective-permute-done.11.refs_1_), channel_id=1, source_target_pairs={{0,1},{1,2},{2,3},{3,4},{4,5},{5,6},{6,7},{7,0},{8,15},{9,8},{10,9... | collective-permute-start | bytes 1179656 | tf_op jit(solution)/shard_map/ppermute | solution.py:20
  190.5 24.1 %collective-permute-start.20 = (f32[4,256,256]{2,1,0:T(8,128)S(1)}, f32[4,256,256]{2,1,0:T(8,128)S(1)}, u32[]{:S(2)}, u32[]{:S(2)}) collective-permute-start(f32[4,256,256]{2,1,0:T(8,128)S(1)} %shard_map.68), channel_id=1, source_target_pairs={{0,8},{8,0},{1,9},{9,1},{2,10},{10,2},{3,11},{11,3},{4,12},{12,4},... | collective-permute-start | bytes 3145736 | tf_op jit(solution)/shard_map/ppermute | solution.py:13
  193.0 10.7 %collective-permute-start.13 = (bf16[4,192,256]{2,1,0:T(8,128)(2,1)S(1)}, bf16[4,192,256]{2,1,0:T(8,128)(2,1)S(1)}, u32[]{:S(2)}, u32[]{:S(2)}) collective-permute-start(bf16[4,192,256]{2,1,0:T(8,128)(2,1)S(1)} %collective-permute-done.12.refs_2_), channel_id=1, source_target_pairs={{0,1},{1,2},{2,3},{3,4},{4,5},{5,6},{6,7},{7,0},{8,15},{9,8},{10,9... | collective-permute-start | bytes 1179656 | tf_op jit(solution)/shard_map/ppermute | solution.py:20
  203.7 10.9 %collective-permute-start.14 = (bf16[4,192,256]{2,1,0:T(8,128)(2,1)S(1)}, bf16[4,192,256]{2,1,0:T(8,128)(2,1)S(1)}, u32[]{:S(2)}, u32[]{:S(2)}) collective-permute-start(bf16[4,192,256]{2,1,0:T(8,128)(2,1)S(1)} %collective-permute-done.13.refs_3_), channel_id=1, source_target_pairs={{0,1},{1,2},{2,3},{3,4},{4,5},{5,6},{6,7},{7,0},{8,15},{9,8},{10,9... | collective-permute-start | bytes 1179656 | tf_op jit(solution)/shard_map/ppermute | solution.py:20
  217.2 31.2 %all-to-all-start = ((bf16[16,4,16,256]{3,2,1,0:T(8,128)(2,1)}), bf16[16,4,16,256]{3,2,1,0:T(8,128)(2,1)S(1)}, u32[]{:S(2)}, u32[]{:S(2)}) async-start(bf16[16,4,16,256]{3,2,1,0:T(8,128)(2,1)} %shard_map.69), calls=%async_computation | async-start | bytes 1048576 | tf_op jit(solution)/shard_map/all_to_all | solution.py:202
  (5 other events, 28.5 us)
where the time goes:
time: 250 us; the launch traced here: 249 us
  starting transfers between devices  87.5 us (35%)
  blocking collectives  71.7 us (29%)
  waiting for transfers between devices  63.5 us (25%)
  Pallas kernels  20 us (8%)
  local copies, waits for them, and re-layouts  2.68 us (1%)
    all_gather x1, blocking collectives, layer(): lax.all_gather(jnp.concatenate([tokens, ids_rows], axis=0), 'z', axis=0)  71.7 us
    ppermute x14, starting transfers between devices, onward(): return lax.ppermute(block, ('core', 'dp'), up + down)  68.9 us
    ppermute x14, waiting for transfers between devices, onward(): return lax.ppermute(block, ('core', 'dp'), up + down)  36.8 us
    all_to_all x1, waiting for transfers between devices, layer(): lax.all_to_all(result, 'z', split_axis=0, concat_axis=0, tiled=True)  26.8 us
    pallas_call x6, Pallas kernels, weighted_sum(): pl.pallas_call(body, grid_spec=pltpu.PrefetchScalarGridSpec(num_scalar_pr...  20 us
    ppermute x7, starting transfers between devices, swap(): return lax.ppermute(block, 'core', [(0, 1), (1, 0)])  14.6 us
  transfers between devices with their start and end apart: 22, of which 12 were waited for; matrix products, arithmetic and copies ran while one was open for 0% of the time, Pallas kernels for 6%

commit v1 on v0

v1 whole, which is shorter than its diff:
```python
import jax
import jax.numpy as jnp
from jax import lax
from jax.experimental import pallas as pl
from jax.experimental.pallas import tpu as pltpu
from jax.sharding import Mesh, PartitionSpec as P


CORES = 2


def swap(block):
    return lax.ppermute(block, "core", [(0, 1), (1, 0)])


def onward(block):
    count = lax.axis_size("dp")
    up = [(i, (i + 1) % count) for i in range(count)]
    down = [(count + i, count + (i - 1) % count) for i in range(count)]
    return lax.ppermute(block, ("core", "dp"), up + down)


def positions(member):
    count = member.shape[-1]
    row = lax.broadcasted_iota(jnp.int32, (count, count), 0)
    col = lax.broadcasted_iota(jnp.int32, (count, count), 1)
    before = (row < col).astype(jnp.bfloat16)
    return jnp.einsum(
        "...i,ij->...j", member.astype(jnp.bfloat16), before, preferred_element_type=jnp.float32
    ).astype(jnp.int32)


def weighted_sum(parts, steps, weights, table, kind, ours_first, extra=(), finish=None, out=None):
    chip_experts = parts[0].shape[0]
    exp_dev = weights[0][0].shape[0]
    n_parts, n_kinds = len(parts), len(weights)
    into = kind == "in"
    if into:
        hid, width = weights[0][0].shape[1], parts[0].shape[2]
        rows = parts[0].shape[1]
        sum_shape = (n_kinds * hid, rows)
        dims = (((1,), (1,)), ((), ()))
    else:
        hid, width = parts[0].shape[1], weights[0][0].shape[2]
        rows = parts[0].shape[2]
        sum_shape = (rows, width)
        dims = (((0,), (0,)), ((), ()))
    out_shape = out or jax.ShapeDtypeStruct((chip_experts, *sum_shape), jnp.float32)

    def body(table_ref, *refs):
        part_refs, rest = refs[:n_parts], refs[n_parts:]
        weight_refs, rest = rest[: 2 * n_kinds], rest[2 * n_kinds :]
        extra_refs, out_ref = rest[:-1], rest[-1]
        for e in range(chip_experts):
            side = (e // exp_dev) ^ (0 if ours_first else 1)
            sums = []
            for k in range(n_kinds):
                ref = weight_refs[2 * k + side]
                if into:
                    total = [x[e, k * hid : (k + 1) * hid] for x in extra_refs]
                else:
                    total = [x[e] for x in extra_refs]
                for part_ref, step in zip(part_refs, steps):
                    if into:
                        at = pl.ds(pl.multiple_of(table_ref[step] * width, width), width)
                        pair = (ref[e % exp_dev, :, at], part_ref[e])
                    else:
                        at = pl.ds(pl.multiple_of(table_ref[step] * hid, hid), hid)
                        pair = (part_ref[e], ref[e % exp_dev, at, :])
                    total.append(lax.dot_general(*pair, dims, preferred_element_type=jnp.float32))
                sums.append(sum(total[1:], total[0]))
            if finish is not None:
                finish(out_ref, e, *sums)
            elif into:
                for k, total in enumerate(sums):
                    out_ref[e, k * hid : (k + 1) * hid] = total
            else:
                out_ref[e] = sums[0]

    whole = pl.BlockSpec(memory_space=pltpu.VMEM)
    operands = [*parts, *(w for pair in weights for w in pair), *extra]
    flops = 2 * chip_experts * n_parts * n_kinds * rows * hid * width
    moved = 2 * sum(x.size for x in operands)
    return pl.pallas_call(
        body,
        in_specs=[pl.BlockSpec(memory_space=pltpu.SMEM)] + [whole] * len(operands),
        out_specs=whole,
        out_shape=out_shape,
        compiler_params=pltpu.CompilerParams(vmem_limit_bytes=24 * 2**20),
        cost_estimate=pl.CostEstimate(flops=flops, bytes_accessed=moved, transcendentals=0),
    )(table, *operands)


def gather_sum(own, weights, table, kind, finish, out):
    half = lax.axis_size("dp") // 2
    mine = [own]
    for _ in range(1, half + 1):
        mine.append(onward(mine[-1]))
    other = [swap(own)]
    for _ in range(1, half):
        other.append(onward(other[-1]))
    early = weighted_sum(mine[:half], range(half), weights, table, kind, True)
    aside = weighted_sum(other[1:], range(1, half), weights, table, kind, False)
    back = swap(aside)
    return weighted_sum(mine[half:], [half], weights, table, kind, True, (early, back), finish, out)


def layer(tokens, expert_ids, gate_levels, gate_weight, up_weight, down_weight):
    tok_dev, width = tokens.shape
    picks = expert_ids.shape[1]
    exp_dev = gate_weight.shape[0]
    hid = gate_weight.shape[2]
    n_z = lax.axis_size("z")
    chip_experts = exp_dev * CORES
    experts = chip_experts * n_z
    capacity = min(tok_dev, max(2, 2 * tok_dev * picks // experts))
    core = lax.axis_index("core")
    z = lax.axis_index("z")

    ids_rows = jnp.zeros((2 * picks, width), jnp.bfloat16)
    ids_rows = ids_rows.at[:picks, :tok_dev].set(expert_ids.T.astype(jnp.bfloat16))
    n_dp = lax.axis_size("dp")
    step = jnp.arange(n_dp, dtype=jnp.int32)
    table = (lax.axis_index("dp") + jnp.where(core == 0, -step, step)) % n_dp

    payload = jnp.concatenate([tokens, ids_rows], axis=0)
    payload, table = lax.optimization_barrier((payload, table))
    gathered = lax.all_gather(payload, "z", axis=0)
    all_tokens = gathered[:, :tok_dev]
    all_ids = gathered[:, tok_dev : tok_dev + picks, :tok_dev].astype(jnp.int32)

    local = jnp.arange(chip_experts, dtype=jnp.int32)
    names = z * chip_experts + (local + core * exp_dev) % chip_experts
    member = jnp.any(all_ids[:, None, :, :] == names[None, :, None, None], axis=2)
    spot = jnp.where(member, positions(member), -1)
    chosen = spot[:, :, None, :] == jnp.arange(capacity, dtype=jnp.int32)[None, None, :, None]
    rows = jnp.einsum(
        "sepj,sjd->espd",
        chosen.astype(jnp.bfloat16),
        all_tokens,
        preferred_element_type=jnp.float32,
    ).astype(jnp.bfloat16)
    count = n_z * capacity
    rows = rows.reshape(chip_experts, count, width)

    pairs = []
    for weights in (jnp.swapaxes(gate_weight, 1, 2), jnp.swapaxes(up_weight, 1, 2), down_weight):
        pairs.append((weights, swap(weights)))

    def gated(out_ref, e, gate_sum, up_sum):
        out_ref[e] = (gate_sum / (1.0 + jnp.exp(-gate_sum)) * up_sum).astype(jnp.bfloat16)

    hidden = gather_sum(
        rows,
        pairs[:2],
        table,
        "in",
        gated,
        jax.ShapeDtypeStruct((chip_experts, hid, count), jnp.bfloat16),
    )

    out_features = down_weight.shape[2]

    def returning(out_ref, e, total):
        out_ref[:, e] = total.astype(jnp.bfloat16).reshape(n_z, capacity, out_features)

    result = gather_sum(
        hidden,
        pairs[2:],
        table,
        "out",
        returning,
        jax.ShapeDtypeStruct((n_z, chip_experts, capacity, out_features), jnp.bfloat16),
    )
    returned = lax.all_to_all(result, "z", split_axis=0, concat_axis=0, tiled=True)
    slot_count = experts * capacity
    returned = returned.reshape(slot_count, out_features)

    own_ids = expert_ids.T
    every = jnp.arange(experts, dtype=jnp.int32)
    in_chip = every % chip_experts
    names = every - in_chip + (in_chip + core * exp_dev) % chip_experts
    named = own_ids[None, :, :] == names[:, None, None]
    own_spot = positions(jnp.any(named, axis=1))
    shares = gate_levels.astype(jnp.float32) / 256.0
    factor = jnp.sum(jnp.where(named, shares.T[None, :, :], 0.0), axis=1)
    weighting = jnp.where(
        own_spot[:, None, :] == jnp.arange(capacity, dtype=jnp.int32)[None, :, None],
        factor[:, None, :],
        0.0,
    ).astype(jnp.bfloat16)
    weighting = weighting.reshape(slot_count, tok_dev)
    combined = jnp.einsum("sj,sd->jd", weighting, returned, preferred_element_type=jnp.float32)
    return combined.astype(jnp.bfloat16)


def solution(mesh):
    groups, expert, dp = (mesh.shape[name] for name in ("groups", "expert", "dp"))
    split = Mesh(
        mesh.devices.reshape(groups, expert // CORES, CORES, dp), ("groups", "z", "core", "dp")
    )
    rows, held = ("groups", "z", "core"), ("z", "core")
    in_specs = (
        P(rows, "dp"),
        P(rows, None),
        P(rows, None),
        P(held, None, "dp"),
        P(held, None, "dp"),
        P(held, None, "dp"),
    )
    return jax.shard_map(
        layer, mesh=split, in_specs=in_specs, out_specs=P(rows, "dp"), check_vma=False
    )
```

time: 250 us -> 244 us (0.976)
  Pallas kernels: 20 us -> 9.02 us
  waiting for transfers between devices: 63.5 us -> 69.3 us
    pallas_call x6, Pallas kernels: 20 us -> 9.02 us  [weighted_sum(): pl.pallas_call(body, in_specs=[pl.BlockSpec(memory_space=pltpu.SMEM)] + [...]
    ppermute x14, waiting for transfers between devices: 36.8 us -> 43.9 us  [onward(): return lax.ppermute(block, ('core', 'dp'), up + down)]
  transfers between devices with their start and end apart: 22 -> 22, of which waited for: 12 -> 13; matrix products, arithmetic and copies ran while one was open for 0% -> 0% of each run, Pallas kernels for 6% -> 3%
where the time goes in v1:
time: 244 us; the launch traced here: 243 us
  starting transfers between devices  87.5 us (36%)
  blocking collectives  71.7 us (29%)
  waiting for transfers between devices  69.3 us (28%)
  Pallas kernels  9.02 us (4%)
  matrix products  2.46 us (1%)
    all_gather x1, blocking collectives, layer(): gathered = lax.all_gather(payload, 'z', axis=0)  71.7 us
    ppermute x14, starting transfers between devices, onward(): return lax.ppermute(block, ('core', 'dp'), up + down)  68.8 us
    ppermute x14, waiting for transfers between devices, onward(): return lax.ppermute(block, ('core', 'dp'), up + down)  43.9 us
    all_to_all x1, waiting for transfers between devices, layer(): lax.all_to_all(result, 'z', split_axis=0, concat_axis=0, tiled=True)  25.4 us
    ppermute x7, starting transfers between devices, swap(): return lax.ppermute(block, 'core', [(0, 1), (1, 0)])  14.6 us
    pallas_call x6, Pallas kernels, weighted_sum(): pl.pallas_call(body, in_specs=[pl.BlockSpec(memory_space=pltpu.SMEM)] + [...  9.02 us
  transfers between devices with their start and end apart: 22, of which 13 were waited for; matrix products, arithmetic and copies ran while one was open for 0% of the time, Pallas kernels for 3%

profile of v1, /device:TPU:70, one launch (start us, length us, event | category | flops | bytes accessed | tf_op | source)
XLA Modules:
  0.0 243.4 jit_solution(1273396788346947524)
XLA Ops:
  1.6 71.7 %all-gather = bf16[1280,256]{1,0:T(8,128)(2,1)S(1)} all-gather(bf16[80,256]{1,0:T(8,128)(2,1)S(1)} %fusion.4), channel_id=2, replica_groups=mesh['groups'=2,'z'=16,'core'=2,'dp'=8] {'z'}, dimensions={0}, use_global_device_ids=true | all-gather | bytes 696320 | tf_op jit(solution)/shard_map/all_gather | solution.py:128
  77.8 2.4 %collective-permute-start.4 = (bf16[2,192,2048]{2,1,0:T(8,128)(2,1)S(1)}, bf16[2,192,2048]{2,1,0:T(8,128)(2,1)S(1)}, u32[]{:S(2)}, u32[]{:S(2)}) collective-permute-start(bf16[2,192,2048]{2,1,0:T(8,128)(2,1)S(1)} %bitcast.23), channel_id=1, source_target_pairs={{0,8},{8,0},{1,9},{9,1},{2,10},{10,2},{3,11},{11,3},{4,12},{12,4},... | collective-permute-start | bytes 4718600 | tf_op jit(solution)/shard_map/ppermute | solution.py:13
  80.3 4.8 %collective-permute-start.7 = (bf16[4,256,256]{2,1,0:T(8,128)(2,1)S(1)}, bf16[4,256,256]{2,1,0:T(8,128)(2,1)S(1)}, u32[]{:S(2)}, u32[]{:S(2)}) collective-permute-start(bf16[4,256,256]{2,1,0:T(8,128)(2,1)S(1)} %collective-permute-done.6), channel_id=1, source_target_pairs={{0,1},{1,2},{2,3},{3,4},{4,5},{5,6},{6,7},{7,0},{8,15},{9,8},{10,9... | collective-permute-start | bytes 1572872 | tf_op jit(solution)/shard_map/ppermute | solution.py:20
  87.1 4.7 %collective-permute-done.7.refs_0_ = bf16[4,256,256]{2,1,0:T(8,128)(2,1)S(1)} collective-permute-done((bf16[4,256,256]{2,1,0:T(8,128)(2,1)S(1)}, bf16[4,256,256]{2,1,0:T(8,128)(2,1)S(1)}, u32[]{:S(2)}, u32[]{:S(2)}) %collective-permute-start.7) | collective-permute-done | bytes 524320 | tf_op jit(solution)/shard_map/ppermute | solution.py:20
  91.8 5.6 %collective-permute-start.8 = (bf16[4,256,256]{2,1,0:T(8,128)(2,1)S(1)}, bf16[4,256,256]{2,1,0:T(8,128)(2,1)S(1)}, u32[]{:S(2)}, u32[]{:S(2)}) collective-permute-start(bf16[4,256,256]{2,1,0:T(8,128)(2,1)S(1)} %collective-permute-done.7.refs_0_), channel_id=1, source_target_pairs={{0,1},{1,2},{2,3},{3,4},{4,5},{5,6},{6,7},{7,0},{8,15},{9,8},{10,9... | collective-permute-start | bytes 1572872 | tf_op jit(solution)/shard_map/ppermute | solution.py:20
  99.3 4.7 %collective-permute-done.8.refs_1_ = bf16[4,256,256]{2,1,0:T(8,128)(2,1)S(1)} collective-permute-done((bf16[4,256,256]{2,1,0:T(8,128)(2,1)S(1)}, bf16[4,256,256]{2,1,0:T(8,128)(2,1)S(1)}, u32[]{:S(2)}, u32[]{:S(2)}) %collective-permute-start.8) | collective-permute-done | bytes 524320 | tf_op jit(solution)/shard_map/ppermute | solution.py:20
  104.1 5.6 %collective-permute-start.9 = (bf16[4,256,256]{2,1,0:T(8,128)(2,1)S(1)}, bf16[4,256,256]{2,1,0:T(8,128)(2,1)S(1)}, u32[]{:S(2)}, u32[]{:S(2)}) collective-permute-start(bf16[4,256,256]{2,1,0:T(8,128)(2,1)S(1)} %collective-permute-done.8.refs_1_), channel_id=1, source_target_pairs={{0,1},{1,2},{2,3},{3,4},{4,5},{5,6},{6,7},{7,0},{8,15},{9,8},{10,9... | collective-permute-start | bytes 1572872 | tf_op jit(solution)/shard_map/ppermute | solution.py:20
  109.7 5.6 %collective-permute-start.1 = (bf16[4,256,256]{2,1,0:T(8,128)(2,1)S(1)}, bf16[4,256,256]{2,1,0:T(8,128)(2,1)S(1)}, u32[]{:S(2)}, u32[]{:S(2)}) collective-permute-start(bf16[4,256,256]{2,1,0:T(8,128)(2,1)S(1)} %collective-permute-done.refs_1_), channel_id=1, source_target_pairs={{0,1},{1,2},{2,3},{3,4},{4,5},{5,6},{6,7},{7,0},{8,15},{9,8},{10,9... | collective-permute-start | bytes 1572872 | tf_op jit(solution)/shard_map/ppermute | solution.py:20
  122.0 5.6 %collective-permute-start.2 = (bf16[4,256,256]{2,1,0:T(8,128)(2,1)S(1)}, bf16[4,256,256]{2,1,0:T(8,128)(2,1)S(1)}, u32[]{:S(2)}, u32[]{:S(2)}) collective-permute-start(bf16[4,256,256]{2,1,0:T(8,128)(2,1)S(1)} %collective-permute-done.1.refs_2_), channel_id=1, source_target_pairs={{0,1},{1,2},{2,3},{3,4},{4,5},{5,6},{6,7},{7,0},{8,15},{9,8},{10,9... | collective-permute-start | bytes 1572872 | tf_op jit(solution)/shard_map/ppermute | solution.py:20
  127.6 6.7 %collective-permute-done.2.refs_3_ = bf16[4,256,256]{2,1,0:T(8,128)(2,1)S(1)} collective-permute-done((bf16[4,256,256]{2,1,0:T(8,128)(2,1)S(1)}, bf16[4,256,256]{2,1,0:T(8,128)(2,1)S(1)}, u32[]{:S(2)}, u32[]{:S(2)}) %collective-permute-start.2) | collective-permute-done | bytes 524320 | tf_op jit(solution)/shard_map/ppermute | solution.py:20
  134.3 5.6 %collective-permute-start.3 = (bf16[4,256,256]{2,1,0:T(8,128)(2,1)S(1)}, bf16[4,256,256]{2,1,0:T(8,128)(2,1)S(1)}, u32[]{:S(2)}, u32[]{:S(2)}) collective-permute-start(bf16[4,256,256]{2,1,0:T(8,128)(2,1)S(1)} %collective-permute-done.2.refs_3_), channel_id=1, source_target_pairs={{0,1},{1,2},{2,3},{3,4},{4,5},{5,6},{6,7},{7,0},{8,15},{9,8},{10,9... | collective-permute-start | bytes 1572872 | tf_op jit(solution)/shard_map/ppermute | solution.py:20
  142.0 4.6 %collective-permute-done.3.refs_0_ = bf16[4,256,256]{2,1,0:T(8,128)(2,1)S(1)} collective-permute-done((bf16[4,256,256]{2,1,0:T(8,128)(2,1)S(1)}, bf16[4,256,256]{2,1,0:T(8,128)(2,1)S(1)}, u32[]{:S(2)}, u32[]{:S(2)}) %collective-permute-start.3) | collective-permute-done | bytes 524320 | tf_op jit(solution)/shard_map/ppermute | solution.py:20
  152.2 5.6 %collective-permute-start.17 = (bf16[4,192,256]{2,1,0:T(8,128)(2,1)S(1)}, bf16[4,192,256]{2,1,0:T(8,128)(2,1)S(1)}, u32[]{:S(2)}, u32[]{:S(2)}) collective-permute-start(bf16[4,192,256]{2,1,0:T(8,128)(2,1)S(1)} %collective-permute-done.16), channel_id=1, source_target_pairs={{0,1},{1,2},{2,3},{3,4},{4,5},{5,6},{6,7},{7,0},{8,15},{9,8},{10,9... | collective-permute-start | bytes 1179656 | tf_op jit(solution)/shard_map/ppermute | solution.py:20
  157.8 5.3 %collective-permute-done.17.refs_0_ = bf16[4,192,256]{2,1,0:T(8,128)(2,1)S(1)} collective-permute-done((bf16[4,192,256]{2,1,0:T(8,128)(2,1)S(1)}, bf16[4,192,256]{2,1,0:T(8,128)(2,1)S(1)}, u32[]{:S(2)}, u32[]{:S(2)}) %collective-permute-start.17) | collective-permute-done | bytes 393248 | tf_op jit(solution)/shard_map/ppermute | solution.py:20
  163.1 5.6 %collective-permute-start.18 = (bf16[4,192,256]{2,1,0:T(8,128)(2,1)S(1)}, bf16[4,192,256]{2,1,0:T(8,128)(2,1)S(1)}, u32[]{:S(2)}, u32[]{:S(2)}) collective-permute-start(bf16[4,192,256]{2,1,0:T(8,128)(2,1)S(1)} %collective-permute-done.17.refs_0_), channel_id=1, source_target_pairs={{0,1},{1,2},{2,3},{3,4},{4,5},{5,6},{6,7},{7,0},{8,15},{9,8},{10,9... | collective-permute-start | bytes 1179656 | tf_op jit(solution)/shard_map/ppermute | solution.py:20
  170.6 3.3 %collective-permute-done.18.refs_1_ = bf16[4,192,256]{2,1,0:T(8,128)(2,1)S(1)} collective-permute-done((bf16[4,192,256]{2,1,0:T(8,128)(2,1)S(1)}, bf16[4,192,256]{2,1,0:T(8,128)(2,1)S(1)}, u32[]{:S(2)}, u32[]{:S(2)}) %collective-permute-start.18) | collective-permute-done | bytes 393248 | tf_op jit(solution)/shard_map/ppermute | solution.py:20
  174.0 5.6 %collective-permute-start.19 = (bf16[4,192,256]{2,1,0:T(8,128)(2,1)S(1)}, bf16[4,192,256]{2,1,0:T(8,128)(2,1)S(1)}, u32[]{:S(2)}, u32[]{:S(2)}) collective-permute-start(bf16[4,192,256]{2,1,0:T(8,128)(2,1)S(1)} %collective-permute-done.18.refs_1_), channel_id=1, source_target_pairs={{0,1},{1,2},{2,3},{3,4},{4,5},{5,6},{6,7},{7,0},{8,15},{9,8},{10,9... | collective-permute-start | bytes 1179656 | tf_op jit(solution)/shard_map/ppermute | solution.py:20
  179.6 4.2 %collective-permute-start.12 = (bf16[4,192,256]{2,1,0:T(8,128)(2,1)S(1)}, bf16[4,192,256]{2,1,0:T(8,128)(2,1)S(1)}, u32[]{:S(2)}, u32[]{:S(2)}) collective-permute-start(bf16[4,192,256]{2,1,0:T(8,128)(2,1)S(1)} %collective-permute-done.11.refs_1_), channel_id=1, source_target_pairs={{0,1},{1,2},{2,3},{3,4},{4,5},{5,6},{6,7},{7,0},{8,15},{9,8},{10,9... | collective-permute-start | bytes 1179656 | tf_op jit(solution)/shard_map/ppermute | solution.py:20
  189.3 5.4 %collective-permute-start.13 = (bf16[4,192,256]{2,1,0:T(8,128)(2,1)S(1)}, bf16[4,192,256]{2,1,0:T(8,128)(2,1)S(1)}, u32[]{:S(2)}, u32[]{:S(2)}) collective-permute-start(bf16[4,192,256]{2,1,0:T(8,128)(2,1)S(1)} %collective-permute-done.12.refs_2_), channel_id=1, source_target_pairs={{0,1},{1,2},{2,3},{3,4},{4,5},{5,6},{6,7},{7,0},{8,15},{9,8},{10,9... | collective-permute-start | bytes 1179656 | tf_op jit(solution)/shard_map/ppermute | solution.py:20
  194.7 5.3 %collective-permute-done.13.refs_3_ = bf16[4,192,256]{2,1,0:T(8,128)(2,1)S(1)} collective-permute-done((bf16[4,192,256]{2,1,0:T(8,128)(2,1)S(1)}, bf16[4,192,256]{2,1,0:T(8,128)(2,1)S(1)}, u32[]{:S(2)}, u32[]{:S(2)}) %collective-permute-start.13) | collective-permute-done | bytes 393248 | tf_op jit(solution)/shard_map/ppermute | solution.py:20
  200.0 5.6 %collective-permute-start.14 = (bf16[4,192,256]{2,1,0:T(8,128)(2,1)S(1)}, bf16[4,192,256]{2,1,0:T(8,128)(2,1)S(1)}, u32[]{:S(2)}, u32[]{:S(2)}) collective-permute-start(bf16[4,192,256]{2,1,0:T(8,128)(2,1)S(1)} %collective-permute-done.13.refs_3_), channel_id=1, source_target_pairs={{0,1},{1,2},{2,3},{3,4},{4,5},{5,6},{6,7},{7,0},{8,15},{9,8},{10,9... | collective-permute-start | bytes 1179656 | tf_op jit(solution)/shard_map/ppermute | solution.py:20
  206.9 3.9 %collective-permute-done.14.refs_0_ = bf16[4,192,256]{2,1,0:T(8,128)(2,1)S(1)} collective-permute-done((bf16[4,192,256]{2,1,0:T(8,128)(2,1)S(1)}, bf16[4,192,256]{2,1,0:T(8,128)(2,1)S(1)}, u32[]{:S(2)}, u32[]{:S(2)}) %collective-permute-start.14) | collective-permute-done | bytes 393248 | tf_op jit(solution)/shard_map/ppermute | solution.py:20
  212.6 4.0 %all-to-all-start = ((bf16[16,4,16,256]{3,2,1,0:T(8,128)(2,1)}), bf16[16,4,16,256]{3,2,1,0:T(8,128)(2,1)S(1)}, u32[]{:S(2)}, u32[]{:S(2)}) async-start(bf16[16,4,16,256]{3,2,1,0:T(8,128)(2,1)} %shard_map.69), calls=%async_computation | async-start | bytes 1048576 | tf_op jit(solution)/shard_map/all_to_all | solution.py:175
  217.2 25.4 %all-to-all-done = bf16[16,4,16,256]{3,2,1,0:T(8,128)(2,1)S(1)} async-done(((bf16[16,4,16,256]{3,2,1,0:T(8,128)(2,1)}), bf16[16,4,16,256]{3,2,1,0:T(8,128)(2,1)S(1)}, u32[]{:S(2)}, u32[]{:S(2)}) %all-to-all-start) | async-done | bytes 524320 | tf_op jit(solution)/shard_map/all_to_all | solution.py:175
  (56 shorter events, 36.1 us)
Async XLA Ops:
  0.7 84.4 %copy-start.1 = (bf16[2,2048,192]{1,2,0:T(8,128)(2,1)S(1)}, bf16[2,2048,192]{1,2,0:T(8,128)(2,1)}, u32[]{:S(2)}) copy-start(bf16[2,2048,192]{1,2,0:T(8,128)(2,1)} %param.12) | copy-start | bytes 4718596
  1.6 76.2 %copy-start = (bf16[2,2048,192]{1,2,0:T(8,128)(2,1)S(1)}, bf16[2,2048,192]{1,2,0:T(8,128)(2,1)}, u32[]{:S(2)}) copy-start(bf16[2,2048,192]{1,2,0:T(8,128)(2,1)} %param.11) | copy-start | bytes 4718596
  75.9 4.4 %collective-permute-start.6 = (bf16[4,256,256]{2,1,0:T(8,128)(2,1)S(1)}, bf16[4,256,256]{2,1,0:T(8,128)(2,1)S(1)}, u32[]{:S(2)}, u32[]{:S(2)}) collective-permute-start(bf16[4,256,256]{2,1,0:T(8,128)(2,1)S(1)} %bitcast.31), channel_id=1, source_target_pairs={{0,8},{8,0},{1,9},{9,1},{2,10},{10,2},{3,11},{11,3},{4,12},{12,4},... | collective-permute-start | bytes 1572872 | tf_op jit(solution)/shard_map/ppermute | solution.py:13
  77.8 37.5 %collective-permute-start.4 = (bf16[2,192,2048]{2,1,0:T(8,128)(2,1)S(1)}, bf16[2,192,2048]{2,1,0:T(8,128)(2,1)S(1)}, u32[]{:S(2)}, u32[]{:S(2)}) collective-permute-start(bf16[2,192,2048]{2,1,0:T(8,128)(2,1)S(1)} %bitcast.23), channel_id=1, source_target_pairs={{0,8},{8,0},{1,9},{9,1},{2,10},{10,2},{3,11},{11,3},{4,12},{12,4},... | collective-permute-start | bytes 4718600 | tf_op jit(solution)/shard_map/ppermute | solution.py:13
  80.3 11.5 %collective-permute-start.7 = (bf16[4,256,256]{2,1,0:T(8,128)(2,1)S(1)}, bf16[4,256,256]{2,1,0:T(8,128)(2,1)S(1)}, u32[]{:S(2)}, u32[]{:S(2)}) collective-permute-start(bf16[4,256,256]{2,1,0:T(8,128)(2,1)S(1)} %collective-permute-done.6), channel_id=1, source_target_pairs={{0,1},{1,2},{2,3},{3,4},{4,5},{5,6},{6,7},{7,0},{8,15},{9,8},{10,9... | collective-permute-start | bytes 1572872 | tf_op jit(solution)/shard_map/ppermute | solution.py:20
  85.1 30.2 %collective-permute-start.5 = (bf16[2,192,2048]{2,1,0:T(8,128)(2,1)S(1)}, bf16[2,192,2048]{2,1,0:T(8,128)(2,1)S(1)}, u32[]{:S(2)}, u32[]{:S(2)}) collective-permute-start(bf16[2,192,2048]{2,1,0:T(8,128)(2,1)S(1)} %bitcast.27), channel_id=1, source_target_pairs={{0,8},{8,0},{1,9},{9,1},{2,10},{10,2},{3,11},{11,3},{4,12},{12,4},... | collective-permute-start | bytes 4718600 | tf_op jit(solution)/shard_map/ppermute | solution.py:13
  91.8 12.3 %collective-permute-start.8 = (bf16[4,256,256]{2,1,0:T(8,128)(2,1)S(1)}, bf16[4,256,256]{2,1,0:T(8,128)(2,1)S(1)}, u32[]{:S(2)}, u32[]{:S(2)}) collective-permute-start(bf16[4,256,256]{2,1,0:T(8,128)(2,1)S(1)} %collective-permute-done.7.refs_0_), channel_id=1, source_target_pairs={{0,1},{1,2},{2,3},{3,4},{4,5},{5,6},{6,7},{7,0},{8,15},{9,8},{10,9... | collective-permute-start | bytes 1572872 | tf_op jit(solution)/shard_map/ppermute | solution.py:20
  97.4 12.3 %collective-permute-start = (bf16[4,256,256]{2,1,0:T(8,128)(2,1)S(1)}, bf16[4,256,256]{2,1,0:T(8,128)(2,1)S(1)}, u32[]{:S(2)}, u32[]{:S(2)}) collective-permute-start(bf16[4,256,256]{2,1,0:T(8,128)(2,1)S(1)} %bitcast.32), channel_id=1, source_target_pairs={{0,1},{1,2},{2,3},{3,4},{4,5},{5,6},{6,7},{7,0},{8,15},{9,8},{10,9... | collective-permute-start | bytes 1572872 | tf_op jit(solution)/shard_map/ppermute | solution.py:20
  104.1 12.3 %collective-permute-start.9 = (bf16[4,256,256]{2,1,0:T(8,128)(2,1)S(1)}, bf16[4,256,256]{2,1,0:T(8,128)(2,1)S(1)}, u32[]{:S(2)}, u32[]{:S(2)}) collective-permute-start(bf16[4,256,256]{2,1,0:T(8,128)(2,1)S(1)} %collective-permute-done.8.refs_1_), channel_id=1, source_target_pairs={{0,1},{1,2},{2,3},{3,4},{4,5},{5,6},{6,7},{7,0},{8,15},{9,8},{10,9... | collective-permute-start | bytes 1572872 | tf_op jit(solution)/shard_map/ppermute | solution.py:20
  109.7 12.3 %collective-permute-start.1 = (bf16[4,256,256]{2,1,0:T(8,128)(2,1)S(1)}, bf16[4,256,256]{2,1,0:T(8,128)(2,1)S(1)}, u32[]{:S(2)}, u32[]{:S(2)}) collective-permute-start(bf16[4,256,256]{2,1,0:T(8,128)(2,1)S(1)} %collective-permute-done.refs_1_), channel_id=1, source_target_pairs={{0,1},{1,2},{2,3},{3,4},{4,5},{5,6},{6,7},{7,0},{8,15},{9,8},{10,9... | collective-permute-start | bytes 1572872 | tf_op jit(solution)/shard_map/ppermute | solution.py:20
  118.1 28.5 %collective-permute-start.10 = (f32[4,384,256]{2,1,0:T(8,128)S(1)}, f32[4,384,256]{2,1,0:T(8,128)S(1)}, u32[]{:S(2)}, u32[]{:S(2)}) collective-permute-start(f32[4,384,256]{2,1,0:T(8,128)S(1)} %shard_map.65), channel_id=1, source_target_pairs={{0,8},{8,0},{1,9},{9,1},{2,10},{10,2},{3,11},{11,3},{4,12},{12,4},... | collective-permute-start | bytes 4718600 | tf_op jit(solution)/shard_map/ppermute | solution.py:13
  122.0 12.3 %collective-permute-start.2 = (bf16[4,256,256]{2,1,0:T(8,128)(2,1)S(1)}, bf16[4,256,256]{2,1,0:T(8,128)(2,1)S(1)}, u32[]{:S(2)}, u32[]{:S(2)}) collective-permute-start(bf16[4,256,256]{2,1,0:T(8,128)(2,1)S(1)} %collective-permute-done.1.refs_2_), channel_id=1, source_target_pairs={{0,1},{1,2},{2,3},{3,4},{4,5},{5,6},{6,7},{7,0},{8,15},{9,8},{10,9... | collective-permute-start | bytes 1572872 | tf_op jit(solution)/shard_map/ppermute | solution.py:20
  134.3 12.3 %collective-permute-start.3 = (bf16[4,256,256]{2,1,0:T(8,128)(2,1)S(1)}, bf16[4,256,256]{2,1,0:T(8,128)(2,1)S(1)}, u32[]{:S(2)}, u32[]{:S(2)}) collective-permute-start(bf16[4,256,256]{2,1,0:T(8,128)(2,1)S(1)} %collective-permute-done.2.refs_3_), channel_id=1, source_target_pairs={{0,1},{1,2},{2,3},{3,4},{4,5},{5,6},{6,7},{7,0},{8,15},{9,8},{10,9... | collective-permute-start | bytes 1572872 | tf_op jit(solution)/shard_map/ppermute | solution.py:20
  147.7 4.4 %collective-permute-start.16 = (bf16[4,192,256]{2,1,0:T(8,128)(2,1)S(1)}, bf16[4,192,256]{2,1,0:T(8,128)(2,1)S(1)}, u32[]{:S(2)}, u32[]{:S(2)}) collective-permute-start(bf16[4,192,256]{2,1,0:T(8,128)(2,1)S(1)} %shard_map.66.refs_0_), channel_id=1, source_target_pairs={{0,8},{8,0},{1,9},{9,1},{2,10},{10,2},{3,11},{11,3},{4,12},{12,4},... | collective-permute-start | bytes 1179656 | tf_op jit(solution)/shard_map/ppermute | solution.py:13
  149.7 34.1 %collective-permute-start.15 = (bf16[2,1536,256]{2,1,0:T(8,128)(2,1)S(1)}, bf16[2,1536,256]{2,1,0:T(8,128)(2,1)S(1)}, u32[]{:S(2)}, u32[]{:S(2)}) collective-permute-start(bf16[2,1536,256]{2,1,0:T(8,128)(2,1)S(1)} %copy-done.2), channel_id=1, source_target_pairs={{0,8},{8,0},{1,9},{9,1},{2,10},{10,2},{3,11},{11,3},{4,12},{12,4},... | collective-permute-start | bytes 4718600 | tf_op jit(solution)/shard_map/ppermute | solution.py:13
  152.2 10.9 %collective-permute-start.17 = (bf16[4,192,256]{2,1,0:T(8,128)(2,1)S(1)}, bf16[4,192,256]{2,1,0:T(8,128)(2,1)S(1)}, u32[]{:S(2)}, u32[]{:S(2)}) collective-permute-start(bf16[4,192,256]{2,1,0:T(8,128)(2,1)S(1)} %collective-permute-done.16), channel_id=1, source_target_pairs={{0,1},{1,2},{2,3},{3,4},{4,5},{5,6},{6,7},{7,0},{8,15},{9,8},{10,9... | collective-permute-start | bytes 1179656 | tf_op jit(solution)/shard_map/ppermute | solution.py:20
  163.1 10.9 %collective-permute-start.18 = (bf16[4,192,256]{2,1,0:T(8,128)(2,1)S(1)}, bf16[4,192,256]{2,1,0:T(8,128)(2,1)S(1)}, u32[]{:S(2)}, u32[]{:S(2)}) collective-permute-start(bf16[4,192,256]{2,1,0:T(8,128)(2,1)S(1)} %collective-permute-done.17.refs_0_), channel_id=1, source_target_pairs={{0,1},{1,2},{2,3},{3,4},{4,5},{5,6},{6,7},{7,0},{8,15},{9,8},{10,9... | collective-permute-start | bytes 1179656 | tf_op jit(solution)/shard_map/ppermute | solution.py:20
  168.7 10.9 %collective-permute-start.11 = (bf16[4,192,256]{2,1,0:T(8,128)(2,1)S(1)}, bf16[4,192,256]{2,1,0:T(8,128)(2,1)S(1)}, u32[]{:S(2)}, u32[]{:S(2)}) collective-permute-start(bf16[4,192,256]{2,1,0:T(8,128)(2,1)S(1)} %shard_map.66.refs_0_), channel_id=1, source_target_pairs={{0,1},{1,2},{2,3},{3,4},{4,5},{5,6},{6,7},{7,0},{8,15},{9,8},{10,9... | collective-permute-start | bytes 1179656 | tf_op jit(solution)/shard_map/ppermute | solution.py:20
  174.0 10.9 %collective-permute-start.19 = (bf16[4,192,256]{2,1,0:T(8,128)(2,1)S(1)}, bf16[4,192,256]{2,1,0:T(8,128)(2,1)S(1)}, u32[]{:S(2)}, u32[]{:S(2)}) collective-permute-start(bf16[4,192,256]{2,1,0:T(8,128)(2,1)S(1)} %collective-permute-done.18.refs_1_), channel_id=1, source_target_pairs={{0,1},{1,2},{2,3},{3,4},{4,5},{5,6},{6,7},{7,0},{8,15},{9,8},{10,9... | collective-permute-start | bytes 1179656 | tf_op jit(solution)/shard_map/ppermute | solution.py:20
  179.6 9.7 %collective-permute-start.12 = (bf16[4,192,256]{2,1,0:T(8,128)(2,1)S(1)}, bf16[4,192,256]{2,1,0:T(8,128)(2,1)S(1)}, u32[]{:S(2)}, u32[]{:S(2)}) collective-permute-start(bf16[4,192,256]{2,1,0:T(8,128)(2,1)S(1)} %collective-permute-done.11.refs_1_), channel_id=1, source_target_pairs={{0,1},{1,2},{2,3},{3,4},{4,5},{5,6},{6,7},{7,0},{8,15},{9,8},{10,9... | collective-permute-start | bytes 1179656 | tf_op jit(solution)/shard_map/ppermute | solution.py:20
  186.0 24.8 %collective-permute-start.20 = (f32[4,256,256]{2,1,0:T(8,128)S(1)}, f32[4,256,256]{2,1,0:T(8,128)S(1)}, u32[]{:S(2)}, u32[]{:S(2)}) collective-permute-start(f32[4,256,256]{2,1,0:T(8,128)S(1)} %shard_map.68), channel_id=1, source_target_pairs={{0,8},{8,0},{1,9},{9,1},{2,10},{10,2},{3,11},{11,3},{4,12},{12,4},... | collective-permute-start | bytes 3145736 | tf_op jit(solution)/shard_map/ppermute | solution.py:13
  189.3 10.7 %collective-permute-start.13 = (bf16[4,192,256]{2,1,0:T(8,128)(2,1)S(1)}, bf16[4,192,256]{2,1,0:T(8,128)(2,1)S(1)}, u32[]{:S(2)}, u32[]{:S(2)}) collective-permute-start(bf16[4,192,256]{2,1,0:T(8,128)(2,1)S(1)} %collective-permute-done.12.refs_2_), channel_id=1, source_target_pairs={{0,1},{1,2},{2,3},{3,4},{4,5},{5,6},{6,7},{7,0},{8,15},{9,8},{10,9... | collective-permute-start | bytes 1179656 | tf_op jit(solution)/shard_map/ppermute | solution.py:20
  200.0 10.9 %collective-permute-start.14 = (bf16[4,192,256]{2,1,0:T(8,128)(2,1)S(1)}, bf16[4,192,256]{2,1,0:T(8,128)(2,1)S(1)}, u32[]{:S(2)}, u32[]{:S(2)}) collective-permute-start(bf16[4,192,256]{2,1,0:T(8,128)(2,1)S(1)} %collective-permute-done.13.refs_3_), channel_id=1, source_target_pairs={{0,1},{1,2},{2,3},{3,4},{4,5},{5,6},{6,7},{7,0},{8,15},{9,8},{10,9... | collective-permute-start | bytes 1179656 | tf_op jit(solution)/shard_map/ppermute | solution.py:20
  212.6 30.0 %all-to-all-start = ((bf16[16,4,16,256]{3,2,1,0:T(8,128)(2,1)}), bf16[16,4,16,256]{3,2,1,0:T(8,128)(2,1)S(1)}, u32[]{:S(2)}, u32[]{:S(2)}) async-start(bf16[16,4,16,256]{3,2,1,0:T(8,128)(2,1)} %shard_map.69), calls=%async_computation | async-start | bytes 1048576 | tf_op jit(solution)/shard_map/all_to_all | solution.py:175
  (4 other events, 28.1 us)

commit v2 on v1

--- a/solution.py
+++ b/solution.py
@@ -28,6 +28,61 @@
     return jnp.einsum(
         "...i,ij->...j", member.astype(jnp.bfloat16), before, preferred_element_type=jnp.float32
     ).astype(jnp.int32)
+
+
+def chosen_rows(gathered, first, turn, tok_dev, picks, chip_experts, capacity):
+    sources, _, width = gathered.shape
+    slots = chip_experts * capacity
+
+    def body(table_ref, gathered_ref, out_ref):
+        row = lax.broadcasted_iota(jnp.int32, (tok_dev, tok_dev), 0)
+        col = lax.broadcasted_iota(jnp.int32, (tok_dev, tok_dev), 1)
+        before = (row < col).astype(jnp.bfloat16)
+        lines = []
+        for s in range(sources):
+            ids = gathered_ref[s, tok_dev : tok_dev + picks, :tok_dev].astype(jnp.float32)
+            for e in range(chip_experts):
+                name = table_ref[0] + lax.rem(table_ref[1] + e, chip_experts)
+                same = jnp.where(ids == name.astype(jnp.float32), 1.0, 0.0)
+                lines.append(jnp.max(same, axis=0, keepdims=True))
+        member = jnp.concatenate(lines, axis=0)
+        spot = lax.dot_general(
+            member.astype(jnp.bfloat16),
+            before,
+            (((1,), (0,)), ((), ())),
+            preferred_element_type=jnp.float32,
+        )
+        spot = jnp.where(member > 0.5, spot, -1.0)
+        slot = lax.broadcasted_iota(jnp.int32, (capacity, tok_dev), 0).astype(jnp.float32)
+        for s in range(sources):
+            picked = [
+                jnp.where(spot[at : at + 1] == slot, 1.0, 0.0)
+                for at in range(s * chip_experts, (s + 1) * chip_experts)
+            ]
+            found = lax.dot_general(
+                jnp.concatenate(picked, axis=0).astype(jnp.bfloat16),
+                gathered_ref[s, :tok_dev],
+                (((1,), (0,)), ((), ())),
+                preferred_element_type=jnp.float32,
+            ).astype(jnp.bfloat16)
+            for e in range(chip_experts):
+                out_ref[e, s * capacity : (s + 1) * capacity] = found[
+                    e * capacity : (e + 1) * capacity
+                ]
+
+    table = jnp.stack([first, turn]).astype(jnp.int32)
+    return pl.pallas_call(
+        body,
+        in_specs=[pl.BlockSpec(memory_space=pltpu.SMEM), pl.BlockSpec(memory_space=pltpu.VMEM)],
+        out_specs=pl.BlockSpec(memory_space=pltpu.VMEM),
+        out_shape=jax.ShapeDtypeStruct((chip_experts, sources * capacity, width), jnp.bfloat16),
+        compiler_params=pltpu.CompilerParams(vmem_limit_bytes=16 * 2**20),
+        cost_estimate=pl.CostEstimate(
+            flops=2 * sources * slots * tok_dev * width,
+            bytes_accessed=2 * gathered.size,
+            transcendentals=0,
+        ),
+    )(table, gathered)
 
 
 def weighted_sum(parts, steps, weights, table, kind, ours_first, extra=(), finish=None, out=None):
@@ -126,22 +181,8 @@
     payload = jnp.concatenate([tokens, ids_rows], axis=0)
     payload, table = lax.optimization_barrier((payload, table))
     gathered = lax.all_gather(payload, "z", axis=0)
-    all_tokens = gathered[:, :tok_dev]
-    all_ids = gathered[:, tok_dev : tok_dev + picks, :tok_dev].astype(jnp.int32)
-
-    local = jnp.arange(chip_experts, dtype=jnp.int32)
-    names = z * chip_experts + (local + core * exp_dev) % chip_experts
-    member = jnp.any(all_ids[:, None, :, :] == names[None, :, None, None], axis=2)
-    spot = jnp.where(member, positions(member), -1)
-    chosen = spot[:, :, None, :] == jnp.arange(capacity, dtype=jnp.int32)[None, None, :, None]
-    rows = jnp.einsum(
-        "sepj,sjd->espd",
-        chosen.astype(jnp.bfloat16),
-        all_tokens,
-        preferred_element_type=jnp.float32,
-    ).astype(jnp.bfloat16)
     count = n_z * capacity
-    rows = rows.reshape(chip_experts, count, width)
+    rows = chosen_rows(gathered, z * chip_experts, core * exp_dev, tok_dev, picks, chip_experts, capacity)
 
     pairs = []
     for weights in (jnp.swapaxes(gate_weight, 1, 2), jnp.swapaxes(up_weight, 1, 2), down_weight):

time: 244 us -> 243 us (level)
  the two profiles are of different devices: /device:TPU:70 before, /device:TPU:86 now
where the time goes in v2:
time: 243 us; the launch traced here: 242 us
  starting transfers between devices  87.5 us (36%)
  blocking collectives  71.5 us (29%)
  waiting for transfers between devices  67.8 us (28%)
  Pallas kernels  10 us (4%)
    all_gather x1, blocking collectives, layer(): gathered = lax.all_gather(payload, 'z', axis=0)  71.5 us
    ppermute x14, starting transfers between devices, onward(): return lax.ppermute(block, ('core', 'dp'), up + down)  68.8 us
    ppermute x14, waiting for transfers between devices, onward(): return lax.ppermute(block, ('core', 'dp'), up + down)  42.4 us
    all_to_all x1, waiting for transfers between devices, layer(): lax.all_to_all(result, 'z', split_axis=0, concat_axis=0, tiled=True)  25.4 us
    ppermute x7, starting transfers between devices, swap(): return lax.ppermute(block, 'core', [(0, 1), (1, 0)])  14.6 us
    pallas_call x6, Pallas kernels, weighted_sum(): pl.pallas_call(body, in_specs=[pl.BlockSpec(memory_space=pltpu.SMEM)] + [...  9.05 us
  transfers between devices with their start and end apart: 22, of which 13 were waited for; matrix products, arithmetic and copies ran while one was open for 0% of the time, Pallas kernels for 3%

profile of v2, /device:TPU:86, one launch (start us, length us, event | category | flops | bytes accessed | tf_op | source)
XLA Modules:
  0.0 241.8 jit_solution(3288505406327021345)
XLA Ops:
  1.6 71.5 %all-gather = bf16[1280,256]{1,0:T(8,128)(2,1)S(1)} all-gather(bf16[80,256]{1,0:T(8,128)(2,1)S(1)} %fusion.2), channel_id=2, replica_groups=mesh['groups'=2,'z'=16,'core'=2,'dp'=8] {'z'}, dimensions={0}, use_global_device_ids=true | all-gather | bytes 696320 | tf_op jit(solution)/shard_map/all_gather | solution.py:183
  76.2 2.4 %collective-permute-start.4 = (bf16[2,192,2048]{2,1,0:T(8,128)(2,1)S(1)}, bf16[2,192,2048]{2,1,0:T(8,128)(2,1)S(1)}, u32[]{:S(2)}, u32[]{:S(2)}) collective-permute-start(bf16[2,192,2048]{2,1,0:T(8,128)(2,1)S(1)} %bitcast.14), channel_id=1, source_target_pairs={{0,8},{8,0},{1,9},{9,1},{2,10},{10,2},{3,11},{11,3},{4,12},{12,4},... | collective-permute-start | bytes 4718600 | tf_op jit(solution)/shard_map/ppermute | solution.py:13
  78.6 4.8 %collective-permute-start.7 = (bf16[4,256,256]{2,1,0:T(8,128)(2,1)S(1)}, bf16[4,256,256]{2,1,0:T(8,128)(2,1)S(1)}, u32[]{:S(2)}, u32[]{:S(2)}) collective-permute-start(bf16[4,256,256]{2,1,0:T(8,128)(2,1)S(1)} %collective-permute-done.6), channel_id=1, source_target_pairs={{0,1},{1,2},{2,3},{3,4},{4,5},{5,6},{6,7},{7,0},{8,15},{9,8},{10,9... | collective-permute-start | bytes 1572872 | tf_op jit(solution)/shard_map/ppermute | solution.py:20
  85.4 4.7 %collective-permute-done.7.refs_0_ = bf16[4,256,256]{2,1,0:T(8,128)(2,1)S(1)} collective-permute-done((bf16[4,256,256]{2,1,0:T(8,128)(2,1)S(1)}, bf16[4,256,256]{2,1,0:T(8,128)(2,1)S(1)}, u32[]{:S(2)}, u32[]{:S(2)}) %collective-permute-start.7) | collective-permute-done | bytes 524320 | tf_op jit(solution)/shard_map/ppermute | solution.py:20
  90.1 5.6 %collective-permute-start.8 = (bf16[4,256,256]{2,1,0:T(8,128)(2,1)S(1)}, bf16[4,256,256]{2,1,0:T(8,128)(2,1)S(1)}, u32[]{:S(2)}, u32[]{:S(2)}) collective-permute-start(bf16[4,256,256]{2,1,0:T(8,128)(2,1)S(1)} %collective-permute-done.7.refs_0_), channel_id=1, source_target_pairs={{0,1},{1,2},{2,3},{3,4},{4,5},{5,6},{6,7},{7,0},{8,15},{9,8},{10,9... | collective-permute-start | bytes 1572872 | tf_op jit(solution)/shard_map/ppermute | solution.py:20
  97.7 4.7 %collective-permute-done.8.refs_1_ = bf16[4,256,256]{2,1,0:T(8,128)(2,1)S(1)} collective-permute-done((bf16[4,256,256]{2,1,0:T(8,128)(2,1)S(1)}, bf16[4,256,256]{2,1,0:T(8,128)(2,1)S(1)}, u32[]{:S(2)}, u32[]{:S(2)}) %collective-permute-start.8) | collective-permute-done | bytes 524320 | tf_op jit(solution)/shard_map/ppermute | solution.py:20
  102.4 5.6 %collective-permute-start.9 = (bf16[4,256,256]{2,1,0:T(8,128)(2,1)S(1)}, bf16[4,256,256]{2,1,0:T(8,128)(2,1)S(1)}, u32[]{:S(2)}, u32[]{:S(2)}) collective-permute-start(bf16[4,256,256]{2,1,0:T(8,128)(2,1)S(1)} %collective-permute-done.8.refs_1_), channel_id=1, source_target_pairs={{0,1},{1,2},{2,3},{3,4},{4,5},{5,6},{6,7},{7,0},{8,15},{9,8},{10,9... | collective-permute-start | bytes 1572872 | tf_op jit(solution)/shard_map/ppermute | solution.py:20
  108.0 5.6 %collective-permute-start.1 = (bf16[4,256,256]{2,1,0:T(8,128)(2,1)S(1)}, bf16[4,256,256]{2,1,0:T(8,128)(2,1)S(1)}, u32[]{:S(2)}, u32[]{:S(2)}) collective-permute-start(bf16[4,256,256]{2,1,0:T(8,128)(2,1)S(1)} %collective-permute-done.refs_1_), channel_id=1, source_target_pairs={{0,1},{1,2},{2,3},{3,4},{4,5},{5,6},{6,7},{7,0},{8,15},{9,8},{10,9... | collective-permute-start | bytes 1572872 | tf_op jit(solution)/shard_map/ppermute | solution.py:20
  120.3 5.6 %collective-permute-start.2 = (bf16[4,256,256]{2,1,0:T(8,128)(2,1)S(1)}, bf16[4,256,256]{2,1,0:T(8,128)(2,1)S(1)}, u32[]{:S(2)}, u32[]{:S(2)}) collective-permute-start(bf16[4,256,256]{2,1,0:T(8,128)(2,1)S(1)} %collective-permute-done.1.refs_2_), channel_id=1, source_target_pairs={{0,1},{1,2},{2,3},{3,4},{4,5},{5,6},{6,7},{7,0},{8,15},{9,8},{10,9... | collective-permute-start | bytes 1572872 | tf_op jit(solution)/shard_map/ppermute | solution.py:20
  125.9 6.7 %collective-permute-done.2.refs_3_ = bf16[4,256,256]{2,1,0:T(8,128)(2,1)S(1)} collective-permute-done((bf16[4,256,256]{2,1,0:T(8,128)(2,1)S(1)}, bf16[4,256,256]{2,1,0:T(8,128)(2,1)S(1)}, u32[]{:S(2)}, u32[]{:S(2)}) %collective-permute-start.2) | collective-permute-done | bytes 524320 | tf_op jit(solution)/shard_map/ppermute | solution.py:20
  132.6 5.6 %collective-permute-start.3 = (bf16[4,256,256]{2,1,0:T(8,128)(2,1)S(1)}, bf16[4,256,256]{2,1,0:T(8,128)(2,1)S(1)}, u32[]{:S(2)}, u32[]{:S(2)}) collective-permute-start(bf16[4,256,256]{2,1,0:T(8,128)(2,1)S(1)} %collective-permute-done.2.refs_3_), channel_id=1, source_target_pairs={{0,1},{1,2},{2,3},{3,4},{4,5},{5,6},{6,7},{7,0},{8,15},{9,8},{10,9... | collective-permute-start | bytes 1572872 | tf_op jit(solution)/shard_map/ppermute | solution.py:20
  140.3 4.6 %collective-permute-done.3.refs_0_ = bf16[4,256,256]{2,1,0:T(8,128)(2,1)S(1)} collective-permute-done((bf16[4,256,256]{2,1,0:T(8,128)(2,1)S(1)}, bf16[4,256,256]{2,1,0:T(8,128)(2,1)S(1)}, u32[]{:S(2)}, u32[]{:S(2)}) %collective-permute-start.3) | collective-permute-done | bytes 524320 | tf_op jit(solution)/shard_map/ppermute | solution.py:20
  150.5 5.6 %collective-permute-start.17 = (bf16[4,192,256]{2,1,0:T(8,128)(2,1)S(1)}, bf16[4,192,256]{2,1,0:T(8,128)(2,1)S(1)}, u32[]{:S(2)}, u32[]{:S(2)}) collective-permute-start(bf16[4,192,256]{2,1,0:T(8,128)(2,1)S(1)} %collective-permute-done.16), channel_id=1, source_target_pairs={{0,1},{1,2},{2,3},{3,4},{4,5},{5,6},{6,7},{7,0},{8,15},{9,8},{10,9... | collective-permute-start | bytes 1179656 | tf_op jit(solution)/shard_map/ppermute | solution.py:20
  156.1 5.3 %collective-permute-done.17.refs_0_ = bf16[4,192,256]{2,1,0:T(8,128)(2,1)S(1)} collective-permute-done((bf16[4,192,256]{2,1,0:T(8,128)(2,1)S(1)}, bf16[4,192,256]{2,1,0:T(8,128)(2,1)S(1)}, u32[]{:S(2)}, u32[]{:S(2)}) %collective-permute-start.17) | collective-permute-done | bytes 393248 | tf_op jit(solution)/shard_map/ppermute | solution.py:20
  161.4 5.6 %collective-permute-start.18 = (bf16[4,192,256]{2,1,0:T(8,128)(2,1)S(1)}, bf16[4,192,256]{2,1,0:T(8,128)(2,1)S(1)}, u32[]{:S(2)}, u32[]{:S(2)}) collective-permute-start(bf16[4,192,256]{2,1,0:T(8,128)(2,1)S(1)} %collective-permute-done.17.refs_0_), channel_id=1, source_target_pairs={{0,1},{1,2},{2,3},{3,4},{4,5},{5,6},{6,7},{7,0},{8,15},{9,8},{10,9... | collective-permute-start | bytes 1179656 | tf_op jit(solution)/shard_map/ppermute | solution.py:20
  169.0 3.3 %collective-permute-done.18.refs_1_ = bf16[4,192,256]{2,1,0:T(8,128)(2,1)S(1)} collective-permute-done((bf16[4,192,256]{2,1,0:T(8,128)(2,1)S(1)}, bf16[4,192,256]{2,1,0:T(8,128)(2,1)S(1)}, u32[]{:S(2)}, u32[]{:S(2)}) %collective-permute-start.18) | collective-permute-done | bytes 393248 | tf_op jit(solution)/shard_map/ppermute | solution.py:20
  172.3 5.6 %collective-permute-start.19 = (bf16[4,192,256]{2,1,0:T(8,128)(2,1)S(1)}, bf16[4,192,256]{2,1,0:T(8,128)(2,1)S(1)}, u32[]{:S(2)}, u32[]{:S(2)}) collective-permute-start(bf16[4,192,256]{2,1,0:T(8,128)(2,1)S(1)} %collective-permute-done.18.refs_1_), channel_id=1, source_target_pairs={{0,1},{1,2},{2,3},{3,4},{4,5},{5,6},{6,7},{7,0},{8,15},{9,8},{10,9... | collective-permute-start | bytes 1179656 | tf_op jit(solution)/shard_map/ppermute | solution.py:20
  177.9 4.2 %collective-permute-start.12 = (bf16[4,192,256]{2,1,0:T(8,128)(2,1)S(1)}, bf16[4,192,256]{2,1,0:T(8,128)(2,1)S(1)}, u32[]{:S(2)}, u32[]{:S(2)}) collective-permute-start(bf16[4,192,256]{2,1,0:T(8,128)(2,1)S(1)} %collective-permute-done.11.refs_1_), channel_id=1, source_target_pairs={{0,1},{1,2},{2,3},{3,4},{4,5},{5,6},{6,7},{7,0},{8,15},{9,8},{10,9... | collective-permute-start | bytes 1179656 | tf_op jit(solution)/shard_map/ppermute | solution.py:20
  187.6 5.4 %collective-permute-start.13 = (bf16[4,192,256]{2,1,0:T(8,128)(2,1)S(1)}, bf16[4,192,256]{2,1,0:T(8,128)(2,1)S(1)}, u32[]{:S(2)}, u32[]{:S(2)}) collective-permute-start(bf16[4,192,256]{2,1,0:T(8,128)(2,1)S(1)} %collective-permute-done.12.refs_2_), channel_id=1, source_target_pairs={{0,1},{1,2},{2,3},{3,4},{4,5},{5,6},{6,7},{7,0},{8,15},{9,8},{10,9... | collective-permute-start | bytes 1179656 | tf_op jit(solution)/shard_map/ppermute | solution.py:20
  193.0 5.3 %collective-permute-done.13.refs_3_ = bf16[4,192,256]{2,1,0:T(8,128)(2,1)S(1)} collective-permute-done((bf16[4,192,256]{2,1,0:T(8,128)(2,1)S(1)}, bf16[4,192,256]{2,1,0:T(8,128)(2,1)S(1)}, u32[]{:S(2)}, u32[]{:S(2)}) %collective-permute-start.13) | collective-permute-done | bytes 393248 | tf_op jit(solution)/shard_map/ppermute | solution.py:20
  198.3 5.6 %collective-permute-start.14 = (bf16[4,192,256]{2,1,0:T(8,128)(2,1)S(1)}, bf16[4,192,256]{2,1,0:T(8,128)(2,1)S(1)}, u32[]{:S(2)}, u32[]{:S(2)}) collective-permute-start(bf16[4,192,256]{2,1,0:T(8,128)(2,1)S(1)} %collective-permute-done.13.refs_3_), channel_id=1, source_target_pairs={{0,1},{1,2},{2,3},{3,4},{4,5},{5,6},{6,7},{7,0},{8,15},{9,8},{10,9... | collective-permute-start | bytes 1179656 | tf_op jit(solution)/shard_map/ppermute | solution.py:20
  205.3 3.9 %collective-permute-done.14.refs_0_ = bf16[4,192,256]{2,1,0:T(8,128)(2,1)S(1)} collective-permute-done((bf16[4,192,256]{2,1,0:T(8,128)(2,1)S(1)}, bf16[4,192,256]{2,1,0:T(8,128)(2,1)S(1)}, u32[]{:S(2)}, u32[]{:S(2)}) %collective-permute-start.14) | collective-permute-done | bytes 393248 | tf_op jit(solution)/shard_map/ppermute | solution.py:20
  210.9 4.0 %all-to-all-start = ((bf16[16,4,16,256]{3,2,1,0:T(8,128)(2,1)}), bf16[16,4,16,256]{3,2,1,0:T(8,128)(2,1)S(1)}, u32[]{:S(2)}, u32[]{:S(2)}) async-start(bf16[16,4,16,256]{3,2,1,0:T(8,128)(2,1)} %shard_map.70), calls=%async_computation | async-start | bytes 1048576 | tf_op jit(solution)/shard_map/all_to_all | solution.py:216
  215.6 25.4 %all-to-all-done = bf16[16,4,16,256]{3,2,1,0:T(8,128)(2,1)S(1)} async-done(((bf16[16,4,16,256]{3,2,1,0:T(8,128)(2,1)}), bf16[16,4,16,256]{3,2,1,0:T(8,128)(2,1)S(1)}, u32[]{:S(2)}, u32[]{:S(2)}) %all-to-all-start) | async-done | bytes 524320 | tf_op jit(solution)/shard_map/all_to_all | solution.py:216
  (51 shorter events, 34.6 us)
Async XLA Ops:
  0.0 76.2 %copy-start = (bf16[2,2048,192]{1,2,0:T(8,128)(2,1)S(1)}, bf16[2,2048,192]{1,2,0:T(8,128)(2,1)}, u32[]{:S(2)}) copy-start(bf16[2,2048,192]{1,2,0:T(8,128)(2,1)} %param.11) | copy-start | bytes 4718596
  74.2 4.4 %collective-permute-start.6 = (bf16[4,256,256]{2,1,0:T(8,128)(2,1)S(1)}, bf16[4,256,256]{2,1,0:T(8,128)(2,1)S(1)}, u32[]{:S(2)}, u32[]{:S(2)}) collective-permute-start(bf16[4,256,256]{2,1,0:T(8,128)(2,1)S(1)} %shard_map.64.refs_0_), channel_id=1, source_target_pairs={{0,8},{8,0},{1,9},{9,1},{2,10},{10,2},{3,11},{11,3},{4,12},{12,4},... | collective-permute-start | bytes 1572872 | tf_op jit(solution)/shard_map/ppermute | solution.py:13
  76.2 37.5 %collective-permute-start.4 = (bf16[2,192,2048]{2,1,0:T(8,128)(2,1)S(1)}, bf16[2,192,2048]{2,1,0:T(8,128)(2,1)S(1)}, u32[]{:S(2)}, u32[]{:S(2)}) collective-permute-start(bf16[2,192,2048]{2,1,0:T(8,128)(2,1)S(1)} %bitcast.14), channel_id=1, source_target_pairs={{0,8},{8,0},{1,9},{9,1},{2,10},{10,2},{3,11},{11,3},{4,12},{12,4},... | collective-permute-start | bytes 4718600 | tf_op jit(solution)/shard_map/ppermute | solution.py:13
  78.6 11.5 %collective-permute-start.7 = (bf16[4,256,256]{2,1,0:T(8,128)(2,1)S(1)}, bf16[4,256,256]{2,1,0:T(8,128)(2,1)S(1)}, u32[]{:S(2)}, u32[]{:S(2)}) collective-permute-start(bf16[4,256,256]{2,1,0:T(8,128)(2,1)S(1)} %collective-permute-done.6), channel_id=1, source_target_pairs={{0,1},{1,2},{2,3},{3,4},{4,5},{5,6},{6,7},{7,0},{8,15},{9,8},{10,9... | collective-permute-start | bytes 1572872 | tf_op jit(solution)/shard_map/ppermute | solution.py:20
  83.4 30.2 %collective-permute-start.5 = (bf16[2,192,2048]{2,1,0:T(8,128)(2,1)}, bf16[2,192,2048]{2,1,0:T(8,128)(2,1)S(1)}, u32[]{:S(2)}, u32[]{:S(2)}) collective-permute-start(bf16[2,192,2048]{2,1,0:T(8,128)(2,1)} %bitcast.18), channel_id=1, source_target_pairs={{0,8},{8,0},{1,9},{9,1},{2,10},{10,2},{3,11},{11,3},{4,12},{12,4},... | collective-permute-start | bytes 4718600 | tf_op jit(solution)/shard_map/ppermute | solution.py:13
  90.1 12.3 %collective-permute-start.8 = (bf16[4,256,256]{2,1,0:T(8,128)(2,1)S(1)}, bf16[4,256,256]{2,1,0:T(8,128)(2,1)S(1)}, u32[]{:S(2)}, u32[]{:S(2)}) collective-permute-start(bf16[4,256,256]{2,1,0:T(8,128)(2,1)S(1)} %collective-permute-done.7.refs_0_), channel_id=1, source_target_pairs={{0,1},{1,2},{2,3},{3,4},{4,5},{5,6},{6,7},{7,0},{8,15},{9,8},{10,9... | collective-permute-start | bytes 1572872 | tf_op jit(solution)/shard_map/ppermute | solution.py:20
  95.7 12.3 %collective-permute-start = (bf16[4,256,256]{2,1,0:T(8,128)(2,1)S(1)}, bf16[4,256,256]{2,1,0:T(8,128)(2,1)S(1)}, u32[]{:S(2)}, u32[]{:S(2)}) collective-permute-start(bf16[4,256,256]{2,1,0:T(8,128)(2,1)S(1)} %shard_map.64.refs_0_), channel_id=1, source_target_pairs={{0,1},{1,2},{2,3},{3,4},{4,5},{5,6},{6,7},{7,0},{8,15},{9,8},{10,9... | collective-permute-start | bytes 1572872 | tf_op jit(solution)/shard_map/ppermute | solution.py:20
  102.4 12.3 %collective-permute-start.9 = (bf16[4,256,256]{2,1,0:T(8,128)(2,1)S(1)}, bf16[4,256,256]{2,1,0:T(8,128)(2,1)S(1)}, u32[]{:S(2)}, u32[]{:S(2)}) collective-permute-start(bf16[4,256,256]{2,1,0:T(8,128)(2,1)S(1)} %collective-permute-done.8.refs_1_), channel_id=1, source_target_pairs={{0,1},{1,2},{2,3},{3,4},{4,5},{5,6},{6,7},{7,0},{8,15},{9,8},{10,9... | collective-permute-start | bytes 1572872 | tf_op jit(solution)/shard_map/ppermute | solution.py:20
  108.0 12.3 %collective-permute-start.1 = (bf16[4,256,256]{2,1,0:T(8,128)(2,1)S(1)}, bf16[4,256,256]{2,1,0:T(8,128)(2,1)S(1)}, u32[]{:S(2)}, u32[]{:S(2)}) collective-permute-start(bf16[4,256,256]{2,1,0:T(8,128)(2,1)S(1)} %collective-permute-done.refs_1_), channel_id=1, source_target_pairs={{0,1},{1,2},{2,3},{3,4},{4,5},{5,6},{6,7},{7,0},{8,15},{9,8},{10,9... | collective-permute-start | bytes 1572872 | tf_op jit(solution)/shard_map/ppermute | solution.py:20
  116.1 22.1 %copy-start.2 = (bf16[2,2048,192]{1,2,0:T(8,128)(2,1)S(1)}, bf16[2,2048,192]{1,2,0:T(8,128)(2,1)}, u32[]{:S(2)}) copy-start(bf16[2,2048,192]{1,2,0:T(8,128)(2,1)} %param.12) | copy-start | bytes 4718596
  117.8 27.1 %collective-permute-start.10 = (f32[4,384,256]{2,1,0:T(8,128)S(1)}, f32[4,384,256]{2,1,0:T(8,128)S(1)}, u32[]{:S(2)}, u32[]{:S(2)}) collective-permute-start(f32[4,384,256]{2,1,0:T(8,128)S(1)} %shard_map.66), channel_id=1, source_target_pairs={{0,8},{8,0},{1,9},{9,1},{2,10},{10,2},{3,11},{11,3},{4,12},{12,4},... | collective-permute-start | bytes 4718600 | tf_op jit(solution)/shard_map/ppermute | solution.py:13
  120.3 12.3 %collective-permute-start.2 = (bf16[4,256,256]{2,1,0:T(8,128)(2,1)S(1)}, bf16[4,256,256]{2,1,0:T(8,128)(2,1)S(1)}, u32[]{:S(2)}, u32[]{:S(2)}) collective-permute-start(bf16[4,256,256]{2,1,0:T(8,128)(2,1)S(1)} %collective-permute-done.1.refs_2_), channel_id=1, source_target_pairs={{0,1},{1,2},{2,3},{3,4},{4,5},{5,6},{6,7},{7,0},{8,15},{9,8},{10,9... | collective-permute-start | bytes 1572872 | tf_op jit(solution)/shard_map/ppermute | solution.py:20
  132.6 12.3 %collective-permute-start.3 = (bf16[4,256,256]{2,1,0:T(8,128)(2,1)S(1)}, bf16[4,256,256]{2,1,0:T(8,128)(2,1)S(1)}, u32[]{:S(2)}, u32[]{:S(2)}) collective-permute-start(bf16[4,256,256]{2,1,0:T(8,128)(2,1)S(1)} %collective-permute-done.2.refs_3_), channel_id=1, source_target_pairs={{0,1},{1,2},{2,3},{3,4},{4,5},{5,6},{6,7},{7,0},{8,15},{9,8},{10,9... | collective-permute-start | bytes 1572872 | tf_op jit(solution)/shard_map/ppermute | solution.py:20
  146.1 4.4 %collective-permute-start.16 = (bf16[4,192,256]{2,1,0:T(8,128)(2,1)S(1)}, bf16[4,192,256]{2,1,0:T(8,128)(2,1)S(1)}, u32[]{:S(2)}, u32[]{:S(2)}) collective-permute-start(bf16[4,192,256]{2,1,0:T(8,128)(2,1)S(1)} %shard_map.67.refs_0_), channel_id=1, source_target_pairs={{0,8},{8,0},{1,9},{9,1},{2,10},{10,2},{3,11},{11,3},{4,12},{12,4},... | collective-permute-start | bytes 1179656 | tf_op jit(solution)/shard_map/ppermute | solution.py:13
  148.0 34.1 %collective-permute-start.15 = (bf16[2,1536,256]{2,1,0:T(8,128)(2,1)S(1)}, bf16[2,1536,256]{2,1,0:T(8,128)(2,1)S(1)}, u32[]{:S(2)}, u32[]{:S(2)}) collective-permute-start(bf16[2,1536,256]{2,1,0:T(8,128)(2,1)S(1)} %copy-done.3), channel_id=1, source_target_pairs={{0,8},{8,0},{1,9},{9,1},{2,10},{10,2},{3,11},{11,3},{4,12},{12,4},... | collective-permute-start | bytes 4718600 | tf_op jit(solution)/shard_map/ppermute | solution.py:13
  150.5 10.9 %collective-permute-start.17 = (bf16[4,192,256]{2,1,0:T(8,128)(2,1)S(1)}, bf16[4,192,256]{2,1,0:T(8,128)(2,1)S(1)}, u32[]{:S(2)}, u32[]{:S(2)}) collective-permute-start(bf16[4,192,256]{2,1,0:T(8,128)(2,1)S(1)} %collective-permute-done.16), channel_id=1, source_target_pairs={{0,1},{1,2},{2,3},{3,4},{4,5},{5,6},{6,7},{7,0},{8,15},{9,8},{10,9... | collective-permute-start | bytes 1179656 | tf_op jit(solution)/shard_map/ppermute | solution.py:20
  161.4 10.9 %collective-permute-start.18 = (bf16[4,192,256]{2,1,0:T(8,128)(2,1)S(1)}, bf16[4,192,256]{2,1,0:T(8,128)(2,1)S(1)}, u32[]{:S(2)}, u32[]{:S(2)}) collective-permute-start(bf16[4,192,256]{2,1,0:T(8,128)(2,1)S(1)} %collective-permute-done.17.refs_0_), channel_id=1, source_target_pairs={{0,1},{1,2},{2,3},{3,4},{4,5},{5,6},{6,7},{7,0},{8,15},{9,8},{10,9... | collective-permute-start | bytes 1179656 | tf_op jit(solution)/shard_map/ppermute | solution.py:20
  167.0 10.9 %collective-permute-start.11 = (bf16[4,192,256]{2,1,0:T(8,128)(2,1)S(1)}, bf16[4,192,256]{2,1,0:T(8,128)(2,1)S(1)}, u32[]{:S(2)}, u32[]{:S(2)}) collective-permute-start(bf16[4,192,256]{2,1,0:T(8,128)(2,1)S(1)} %shard_map.67.refs_0_), channel_id=1, source_target_pairs={{0,1},{1,2},{2,3},{3,4},{4,5},{5,6},{6,7},{7,0},{8,15},{9,8},{10,9... | collective-permute-start | bytes 1179656 | tf_op jit(solution)/shard_map/ppermute | solution.py:20
  172.3 10.9 %collective-permute-start.19 = (bf16[4,192,256]{2,1,0:T(8,128)(2,1)S(1)}, bf16[4,192,256]{2,1,0:T(8,128)(2,1)S(1)}, u32[]{:S(2)}, u32[]{:S(2)}) collective-permute-start(bf16[4,192,256]{2,1,0:T(8,128)(2,1)S(1)} %collective-permute-done.18.refs_1_), channel_id=1, source_target_pairs={{0,1},{1,2},{2,3},{3,4},{4,5},{5,6},{6,7},{7,0},{8,15},{9,8},{10,9... | collective-permute-start | bytes 1179656 | tf_op jit(solution)/shard_map/ppermute | solution.py:20
  177.9 9.7 %collective-permute-start.12 = (bf16[4,192,256]{2,1,0:T(8,128)(2,1)S(1)}, bf16[4,192,256]{2,1,0:T(8,128)(2,1)S(1)}, u32[]{:S(2)}, u32[]{:S(2)}) collective-permute-start(bf16[4,192,256]{2,1,0:T(8,128)(2,1)S(1)} %collective-permute-done.11.refs_1_), channel_id=1, source_target_pairs={{0,1},{1,2},{2,3},{3,4},{4,5},{5,6},{6,7},{7,0},{8,15},{9,8},{10,9... | collective-permute-start | bytes 1179656 | tf_op jit(solution)/shard_map/ppermute | solution.py:20
  184.4 24.8 %collective-permute-start.20 = (f32[4,256,256]{2,1,0:T(8,128)S(1)}, f32[4,256,256]{2,1,0:T(8,128)S(1)}, u32[]{:S(2)}, u32[]{:S(2)}) collective-permute-start(f32[4,256,256]{2,1,0:T(8,128)S(1)} %shard_map.69), channel_id=1, source_target_pairs={{0,8},{8,0},{1,9},{9,1},{2,10},{10,2},{3,11},{11,3},{4,12},{12,4},... | collective-permute-start | bytes 3145736 | tf_op jit(solution)/shard_map/ppermute | solution.py:13
  187.6 10.7 %collective-permute-start.13 = (bf16[4,192,256]{2,1,0:T(8,128)(2,1)S(1)}, bf16[4,192,256]{2,1,0:T(8,128)(2,1)S(1)}, u32[]{:S(2)}, u32[]{:S(2)}) collective-permute-start(bf16[4,192,256]{2,1,0:T(8,128)(2,1)S(1)} %collective-permute-done.12.refs_2_), channel_id=1, source_target_pairs={{0,1},{1,2},{2,3},{3,4},{4,5},{5,6},{6,7},{7,0},{8,15},{9,8},{10,9... | collective-permute-start | bytes 1179656 | tf_op jit(solution)/shard_map/ppermute | solution.py:20
  198.3 10.9 %collective-permute-start.14 = (bf16[4,192,256]{2,1,0:T(8,128)(2,1)S(1)}, bf16[4,192,256]{2,1,0:T(8,128)(2,1)S(1)}, u32[]{:S(2)}, u32[]{:S(2)}) collective-permute-start(bf16[4,192,256]{2,1,0:T(8,128)(2,1)S(1)} %collective-permute-done.13.refs_3_), channel_id=1, source_target_pairs={{0,1},{1,2},{2,3},{3,4},{4,5},{5,6},{6,7},{7,0},{8,15},{9,8},{10,9... | collective-permute-start | bytes 1179656 | tf_op jit(solution)/shard_map/ppermute | solution.py:20
  210.9 30.0 %all-to-all-start = ((bf16[16,4,16,256]{3,2,1,0:T(8,128)(2,1)}), bf16[16,4,16,256]{3,2,1,0:T(8,128)(2,1)S(1)}, u32[]{:S(2)}, u32[]{:S(2)}) async-start(bf16[16,4,16,256]{3,2,1,0:T(8,128)(2,1)} %shard_map.70), calls=%async_computation | async-start | bytes 1048576 | tf_op jit(solution)/shard_map/all_to_all | solution.py:216
  (4 other events, 28.7 us)

commit v3 on v2

--- a/solution.py
+++ b/solution.py
@@ -11,6 +11,11 @@
 
 def swap(block):
     return lax.ppermute(block, "core", [(0, 1), (1, 0)])
+
+
+def shift(block, step):
+    count = lax.axis_size("dp")
+    return lax.ppermute(block, "dp", [(i, (i + step) % count) for i in range(count)])
 
 
 def onward(block):
@@ -30,9 +35,29 @@
     ).astype(jnp.int32)
 
 
-def chosen_rows(gathered, first, turn, tok_dev, picks, chip_experts, capacity):
+def with_ids(tokens, ids):
+    tok_dev, width = tokens.shape
+    picks = ids.shape[0]
+
+    def body(tokens_ref, ids_ref, out_ref):
+        out_ref[:tok_dev] = tokens_ref[...]
+        found = ids_ref[...].astype(jnp.float32)
+        tall = jnp.concatenate([found, jnp.zeros((picks, tok_dev), jnp.float32)], axis=0)
+        wide = jnp.concatenate([tall, jnp.zeros((2 * picks, width - tok_dev), jnp.float32)], axis=1)
+        out_ref[tok_dev:] = wide.astype(jnp.bfloat16)
+
+    return pl.pallas_call(
+        body,
+        out_shape=jax.ShapeDtypeStruct((tok_dev + 2 * picks, width), jnp.bfloat16),
+        compiler_params=pltpu.CompilerParams(vmem_limit_bytes=4 * 2**20),
+        cost_estimate=pl.CostEstimate(flops=2 * tokens.size, bytes_accessed=4 * tokens.size, transcendentals=0),
+    )(tokens, ids)
+
+
+def chosen_rows(gathered, table, tok_dev, picks, chip_experts, capacity):
     sources, _, width = gathered.shape
     slots = chip_experts * capacity
+    end = table.shape[0]
 
     def body(table_ref, gathered_ref, out_ref):
         row = lax.broadcasted_iota(jnp.int32, (tok_dev, tok_dev), 0)
@@ -42,7 +67,7 @@
         for s in range(sources):
             ids = gathered_ref[s, tok_dev : tok_dev + picks, :tok_dev].astype(jnp.float32)
             for e in range(chip_experts):
-                name = table_ref[0] + lax.rem(table_ref[1] + e, chip_experts)
+                name = table_ref[end - 2] + lax.rem(table_ref[end - 1] + e, chip_experts)
                 same = jnp.where(ids == name.astype(jnp.float32), 1.0, 0.0)
                 lines.append(jnp.max(same, axis=0, keepdims=True))
         member = jnp.concatenate(lines, axis=0)
@@ -70,7 +95,6 @@
                     e * capacity : (e + 1) * capacity
                 ]
 
-    table = jnp.stack([first, turn]).astype(jnp.int32)
     return pl.pallas_call(
         body,
         in_specs=[pl.BlockSpec(memory_space=pltpu.SMEM), pl.BlockSpec(memory_space=pltpu.VMEM)],
@@ -85,11 +109,22 @@
     )(table, gathered)
 
 
-def weighted_sum(parts, steps, weights, table, kind, ours_first, extra=(), finish=None, out=None):
-    chip_experts = parts[0].shape[0]
+def weighted_sum(parts, steps, weights, table, kind, order, extra=(), finish=None, out=None):
     exp_dev = weights[0][0].shape[0]
-    n_parts, n_kinds = len(parts), len(weights)
+    chip_experts = exp_dev * CORES
+    n_kinds = len(weights)
     into = kind == "in"
+    groups, place, flat = [], [], []
+    for part in parts:
+        blocks = part if isinstance(part, tuple) else (part,)
+        holder, first = [], 0
+        for block in blocks:
+            holder += [len(flat)] * block.shape[0]
+            place.append({first + n: n for n in range(block.shape[0])})
+            flat.append(block)
+            first += block.shape[0]
+        groups.append(holder)
+    parts, n_parts = flat, len(flat)
     if into:
         hid, width = weights[0][0].shape[1], parts[0].shape[2]
         rows = parts[0].shape[1]
@@ -107,30 +142,29 @@
         weight_refs, rest = rest[: 2 * n_kinds], rest[2 * n_kinds :]
         extra_refs, out_ref = rest[:-1], rest[-1]
         for e in range(chip_experts):
-            side = (e // exp_dev) ^ (0 if ours_first else 1)
+            side = order[e // exp_dev]
             sums = []
             for k in range(n_kinds):
                 ref = weight_refs[2 * k + side]
-                if into:
-                    total = [x[e, k * hid : (k + 1) * hid] for x in extra_refs]
-                else:
-                    total = [x[e] for x in extra_refs]
-                for part_ref, step in zip(part_refs, steps):
+                spot = (slice(k * hid, (k + 1) * hid),) if into else ()
+                total = [x[(e, *spot)].astype(jnp.float32) for x in extra_refs]
+                for part_refs_of, step in zip(groups, steps):
+                    part = part_refs[part_refs_of[e]][place[part_refs_of[e]][e]]
                     if into:
                         at = pl.ds(pl.multiple_of(table_ref[step] * width, width), width)
-                        pair = (ref[e % exp_dev, :, at], part_ref[e])
+                        pair = (ref[e % exp_dev, :, at], part)
                     else:
                         at = pl.ds(pl.multiple_of(table_ref[step] * hid, hid), hid)
-                        pair = (part_ref[e], ref[e % exp_dev, at, :])
+                        pair = (part, ref[e % exp_dev, at, :])
                     total.append(lax.dot_general(*pair, dims, preferred_element_type=jnp.float32))
                 sums.append(sum(total[1:], total[0]))
             if finish is not None:
                 finish(out_ref, e, *sums)
             elif into:
                 for k, total in enumerate(sums):
-                    out_ref[e, k * hid : (k + 1) * hid] = total
+                    out_ref[e, k * hid : (k + 1) * hid] = total.astype(out_ref.dtype)
             else:
-                out_ref[e] = sums[0]
+                out_ref[e] = sums[0].astype(out_ref.dtype)
 
     whole = pl.BlockSpec(memory_space=pltpu.VMEM)
     operands = [*parts, *(w for pair in weights for w in pair), *extra]
@@ -146,7 +180,7 @@
     )(table, *operands)
 
 
-def gather_sum(own, weights, table, kind, finish, out):
+def tokens_sum(own, weights, owners, finish, out):
     half = lax.axis_size("dp") // 2
     mine = [own]
     for _ in range(1, half + 1):
@@ -154,14 +188,47 @@
     other = [swap(own)]
     for _ in range(1, half):
         other.append(onward(other[-1]))
-    early = weighted_sum(mine[:half], range(half), weights, table, kind, True)
-    aside = weighted_sum(other[1:], range(1, half), weights, table, kind, False)
+    early = weighted_sum(mine[: half - 1], range(half - 1), weights, owners, "in", (0, 1))
+    ahead = weighted_sum(
+        other[1 : half - 1], range(1, half - 1), weights, owners, "in", (1, 0)
+    )
+    sums = jax.ShapeDtypeStruct(ahead.shape, jnp.bfloat16)
+    aside = weighted_sum(
+        other[half - 1 :], [half - 1], weights, owners, "in", (1, 0), (ahead,), None, sums
+    )
     back = swap(aside)
-    return weighted_sum(mine[half:], [half], weights, table, kind, True, (early, back), finish, out)
+    return weighted_sum(
+        mine[half - 1 :],
+        [half - 1, half],
+        weights,
+        owners,
+        "in",
+        (0, 1),
+        (early, back),
+        finish,
+        out,
+    )
+
+
+def hidden_sum(own, weights, owners, finish, out):
+    count = lax.axis_size("dp")
+    half = count // 2
+    up, down = [own], [own]
+    for _ in range(1, half):
+        up.append(shift(up[-1], 1))
+        down.append(shift(down[-1], -1))
+    middle = own.shape[0] // 2
+    last_up = shift(up[-1][:middle], 1)
+    last_down = shift(down[-1][middle:], -1)
+    steps = [*range(count, count + half), *(2 * count - step for step in range(1, half))]
+    early = weighted_sum([*up, *down[1:]], steps, weights, owners, "out", (0, 1))
+    return weighted_sum(
+        [(last_up, last_down)], [count + half], weights, owners, "out", (0, 1), (early,), finish, out
+    )
 
 
 def layer(tokens, expert_ids, gate_levels, gate_weight, up_weight, down_weight):
-    tok_dev, width = tokens.shape
+    tok_dev, _ = tokens.shape
     picks = expert_ids.shape[1]
     exp_dev = gate_weight.shape[0]
     hid = gate_weight.shape[2]
@@ -172,17 +239,19 @@
     core = lax.axis_index("core")
     z = lax.axis_index("z")
 
-    ids_rows = jnp.zeros((2 * picks, width), jnp.bfloat16)
-    ids_rows = ids_rows.at[:picks, :tok_dev].set(expert_ids.T.astype(jnp.bfloat16))
     n_dp = lax.axis_size("dp")
-    step = jnp.arange(n_dp, dtype=jnp.int32)
-    table = (lax.axis_index("dp") + jnp.where(core == 0, -step, step)) % n_dp
-
-    payload = jnp.concatenate([tokens, ids_rows], axis=0)
+    at = jnp.arange(2 * n_dp + 2, dtype=jnp.int32)
+    me = lax.axis_index("dp")
+    turn = jnp.where((core == 1) & (at < n_dp), 1, -1)
+    table = (me + turn * (at % n_dp)) % n_dp
+    table = jnp.where(at == 2 * n_dp, z * chip_experts, table)
+    table = jnp.where(at == 2 * n_dp + 1, core * exp_dev, table)
+
+    payload = with_ids(tokens, expert_ids.T)
     payload, table = lax.optimization_barrier((payload, table))
     gathered = lax.all_gather(payload, "z", axis=0)
     count = n_z * capacity
-    rows = chosen_rows(gathered, z * chip_experts, core * exp_dev, tok_dev, picks, chip_experts, capacity)
+    rows = chosen_rows(gathered, table, tok_dev, picks, chip_experts, capacity)
 
     pairs = []
     for weights in (jnp.swapaxes(gate_weight, 1, 2), jnp.swapaxes(up_weight, 1, 2), down_weight):
@@ -191,11 +260,10 @@
     def gated(out_ref, e, gate_sum, up_sum):
         out_ref[e] = (gate_sum / (1.0 + jnp.exp(-gate_sum)) * up_sum).astype(jnp.bfloat16)
 
-    hidden = gather_sum(
+    hidden = tokens_sum(
         rows,
         pairs[:2],
         table,
-        "in",
         gated,
         jax.ShapeDtypeStruct((chip_experts, hid, count), jnp.bfloat16),
     )
@@ -205,11 +273,10 @@
     def returning(out_ref, e, total):
         out_ref[:, e] = total.astype(jnp.bfloat16).reshape(n_z, capacity, out_features)
 
-    result = gather_sum(
+    result = hidden_sum(
         hidden,
         pairs[2:],
         table,
-        "out",
         returning,
         jax.ShapeDtypeStruct((n_z, chip_experts, capacity, out_features), jnp.bfloat16),
     )

time: 243 us -> 213 us (0.88)
  waiting for transfers between devices: 67.8 us -> 46.2 us
  starting transfers between devices: 87.5 us -> 79.4 us
    ppermute x14 -> x7, waiting for transfers between devices: 42.4 us -> 8.88 us  [onward(): return lax.ppermute(block, ('core', 'dp'), up + down)]
    ppermute x14 -> x7, starting transfers between devices: 68.8 us -> 35.5 us  [onward(): return lax.ppermute(block, ('core', 'dp'), up + down)]
    ppermute x0 -> x8, starting transfers between devices: none -> 29.7 us  [shift(): lax.ppermute(block, 'dp', [(i, (i + step) % count) for i in range(count)])]
    ppermute x0 -> x8, waiting for transfers between devices: none -> 18.2 us  [shift(): lax.ppermute(block, 'dp', [(i, (i + step) % count) for i in range(count)])]
    all_to_all x1, waiting for transfers between devices: 25.4 us -> 19 us  [layer(): lax.all_to_all(result, 'z', split_axis=0, concat_axis=0, tiled=True)]
    ppermute x7 -> x5, starting transfers between devices: 14.6 us -> 10.2 us  [swap(): return lax.ppermute(block, 'core', [(0, 1), (1, 0)])]
  transfers between devices with their start and end apart: 22 -> 21, of which waited for: 13 -> 11; matrix products, arithmetic and copies ran while one was open for 0% -> 0% of each run, Pallas kernels for 3% -> 3%
where the time goes in v3:
time: 213 us; the launch traced here: 212 us
  starting transfers between devices  79.4 us (37%)
  blocking collectives  71.6 us (34%)
  waiting for transfers between devices  46.2 us (22%)
  Pallas kernels  10 us (5%)
  local copies, waits for them, and re-layouts  3.02 us (1%)
    all_gather x1, blocking collectives, layer(): gathered = lax.all_gather(payload, 'z', axis=0)  71.6 us
    ppermute x7, starting transfers between devices, onward(): return lax.ppermute(block, ('core', 'dp'), up + down)  35.5 us
    ppermute x8, starting transfers between devices, shift(): lax.ppermute(block, 'dp', [(i, (i + step) % count) for i in range(count)])  29.7 us
    all_to_all x1, waiting for transfers between devices, layer(): lax.all_to_all(result, 'z', split_axis=0, concat_axis=0, tiled=True)  19 us
    ppermute x8, waiting for transfers between devices, shift(): lax.ppermute(block, 'dp', [(i, (i + step) % count) for i in range(count)])  18.2 us
    ppermute x5, starting transfers between devices, swap(): return lax.ppermute(block, 'core', [(0, 1), (1, 0)])  10.2 us
    pallas_call x6, Pallas kernels, weighted_sum(): pl.pallas_call(body, in_specs=[pl.BlockSpec(memory_space=pltpu.SMEM)] + [...  9.03 us
    ppermute x7, waiting for transfers between devices, onward(): return lax.ppermute(block, ('core', 'dp'), up + down)  8.88 us
  transfers between devices with their start and end apart: 21, of which 11 were waited for; matrix products, arithmetic and copies ran while one was open for 0% of the time, Pallas kernels for 3%

profile of v3, /device:TPU:86, one launch (start us, length us, event | category | flops | bytes accessed | tf_op | source)
XLA Modules:
  0.0 212.1 jit_solution(11052027128310099715)
XLA Ops:
  1.6 71.6 %all-gather = bf16[1280,256]{1,0:T(8,128)(2,1)S(1)} all-gather(bf16[80,256]{1,0:T(8,128)(2,1)S(1)} %shard_map.64), channel_id=2, replica_groups=mesh['groups'=2,'z'=16,'core'=2,'dp'=8] {'z'}, dimensions={0}, use_global_device_ids=true | all-gather | bytes 696320 | tf_op jit(solution)/shard_map/all_gather | solution.py:252
  76.1 2.4 %collective-permute-start.4 = (bf16[2,192,2048]{2,1,0:T(8,128)(2,1)S(1)}, bf16[2,192,2048]{2,1,0:T(8,128)(2,1)S(1)}, u32[]{:S(2)}, u32[]{:S(2)}) collective-permute-start(bf16[2,192,2048]{2,1,0:T(8,128)(2,1)S(1)} %bitcast.11), channel_id=1, source_target_pairs={{0,8},{8,0},{1,9},{9,1},{2,10},{10,2},{3,11},{11,3},{4,12},{12,4},... | collective-permute-start | bytes 4718600 | tf_op jit(solution)/shard_map/ppermute | solution.py:13
  78.6 2.0 collective-permute-start.5
  80.5 4.8 %collective-permute-start.7 = (bf16[4,256,256]{2,1,0:T(8,128)(2,1)S(1)}, bf16[4,256,256]{2,1,0:T(8,128)(2,1)S(1)}, u32[]{:S(2)}, u32[]{:S(2)}) collective-permute-start(bf16[4,256,256]{2,1,0:T(8,128)(2,1)S(1)} %collective-permute-done.6), channel_id=1, source_target_pairs={{0,1},{1,2},{2,3},{3,4},{4,5},{5,6},{6,7},{7,0},{8,15},{9,8},{10,9... | collective-permute-start | bytes 1572872 | tf_op jit(solution)/shard_map/ppermute | solution.py:25
  85.3 2.7 %collective-permute-start = (bf16[4,256,256]{2,1,0:T(8,128)(2,1)S(1)}, bf16[4,256,256]{2,1,0:T(8,128)(2,1)S(1)}, u32[]{:S(2)}, u32[]{:S(2)}) collective-permute-start(bf16[4,256,256]{2,1,0:T(8,128)(2,1)S(1)} %shard_map.65.refs_0_), channel_id=1, source_target_pairs={{0,1},{1,2},{2,3},{3,4},{4,5},{5,6},{6,7},{7,0},{8,15},{9,8},{10,9... | collective-permute-start | bytes 1572872 | tf_op jit(solution)/shard_map/ppermute | solution.py:25
  88.0 4.0 %collective-permute-done.7.refs_0_ = bf16[4,256,256]{2,1,0:T(8,128)(2,1)S(1)} collective-permute-done((bf16[4,256,256]{2,1,0:T(8,128)(2,1)S(1)}, bf16[4,256,256]{2,1,0:T(8,128)(2,1)S(1)}, u32[]{:S(2)}, u32[]{:S(2)}) %collective-permute-start.7) | collective-permute-done | bytes 524320 | tf_op jit(solution)/shard_map/ppermute | solution.py:25
  92.0 5.6 %collective-permute-start.8 = (bf16[4,256,256]{2,1,0:T(8,128)(2,1)S(1)}, bf16[4,256,256]{2,1,0:T(8,128)(2,1)S(1)}, u32[]{:S(2)}, u32[]{:S(2)}) collective-permute-start(bf16[4,256,256]{2,1,0:T(8,128)(2,1)S(1)} %collective-permute-done.7.refs_0_), channel_id=1, source_target_pairs={{0,1},{1,2},{2,3},{3,4},{4,5},{5,6},{6,7},{7,0},{8,15},{9,8},{10,9... | collective-permute-start | bytes 1572872 | tf_op jit(solution)/shard_map/ppermute | solution.py:25
  97.6 5.6 %collective-permute-start.1 = (bf16[4,256,256]{2,1,0:T(8,128)(2,1)S(1)}, bf16[4,256,256]{2,1,0:T(8,128)(2,1)S(1)}, u32[]{:S(2)}, u32[]{:S(2)}) collective-permute-start(bf16[4,256,256]{2,1,0:T(8,128)(2,1)S(1)} %collective-permute-done.refs_1_), channel_id=1, source_target_pairs={{0,1},{1,2},{2,3},{3,4},{4,5},{5,6},{6,7},{7,0},{8,15},{9,8},{10,9... | collective-permute-start | bytes 1572872 | tf_op jit(solution)/shard_map/ppermute | solution.py:25
  104.3 5.6 %collective-permute-start.9 = (bf16[4,256,256]{2,1,0:T(8,128)(2,1)S(1)}, bf16[4,256,256]{2,1,0:T(8,128)(2,1)S(1)}, u32[]{:S(2)}, u32[]{:S(2)}) collective-permute-start(bf16[4,256,256]{2,1,0:T(8,128)(2,1)S(1)} %collective-permute-done.8.refs_1_), channel_id=1, source_target_pairs={{0,1},{1,2},{2,3},{3,4},{4,5},{5,6},{6,7},{7,0},{8,15},{9,8},{10,9... | collective-permute-start | bytes 1572872 | tf_op jit(solution)/shard_map/ppermute | solution.py:25
  109.9 5.6 %collective-permute-start.2 = (bf16[4,256,256]{2,1,0:T(8,128)(2,1)S(1)}, bf16[4,256,256]{2,1,0:T(8,128)(2,1)S(1)}, u32[]{:S(2)}, u32[]{:S(2)}) collective-permute-start(bf16[4,256,256]{2,1,0:T(8,128)(2,1)S(1)} %collective-permute-done.1.refs_2_), channel_id=1, source_target_pairs={{0,1},{1,2},{2,3},{3,4},{4,5},{5,6},{6,7},{7,0},{8,15},{9,8},{10,9... | collective-permute-start | bytes 1572872 | tf_op jit(solution)/shard_map/ppermute | solution.py:25
  119.4 2.0 collective-permute-start.10
  122.2 5.6 %collective-permute-start.3 = (bf16[4,256,256]{2,1,0:T(8,128)(2,1)S(1)}, bf16[4,256,256]{2,1,0:T(8,128)(2,1)S(1)}, u32[]{:S(2)}, u32[]{:S(2)}) collective-permute-start(bf16[4,256,256]{2,1,0:T(8,128)(2,1)S(1)} %collective-permute-done.2.refs_0_), channel_id=1, source_target_pairs={{0,1},{1,2},{2,3},{3,4},{4,5},{5,6},{6,7},{7,0},{8,15},{9,8},{10,9... | collective-permute-start | bytes 1572872 | tf_op jit(solution)/shard_map/ppermute | solution.py:25
  131.5 3.0 %collective-permute-done.3.refs_1_ = bf16[4,256,256]{2,1,0:T(8,128)(2,1)S(1)} collective-permute-done((bf16[4,256,256]{2,1,0:T(8,128)(2,1)S(1)}, bf16[4,256,256]{2,1,0:T(8,128)(2,1)S(1)}, u32[]{:S(2)}, u32[]{:S(2)}) %collective-permute-start.3) | collective-permute-done | bytes 524320 | tf_op jit(solution)/shard_map/ppermute | solution.py:25
  136.0 5.6 %collective-permute-start.11 = (bf16[4,192,256]{2,1,0:T(8,128)(2,1)S(1)}, bf16[4,192,256]{2,1,0:T(8,128)(2,1)S(1)}, u32[]{:S(2)}, u32[]{:S(2)}) collective-permute-start(bf16[4,192,256]{2,1,0:T(8,128)(2,1)S(1)} %shard_map.69.refs_0_), channel_id=1, source_target_pairs={{0,1},{1,2},{2,3},{3,4},{4,5},{5,6},{6,7},{7,0},{8,9},{9,10},{10,1... | collective-permute-start | bytes 1179656 | tf_op jit(solution)/shard_map/ppermute | solution.py:18
  141.7 2.0 collective-permute-start.15
  143.6 3.9 %collective-permute-done.11.refs_1_ = bf16[4,192,256]{2,1,0:T(8,128)(2,1)S(1)} collective-permute-done((bf16[4,192,256]{2,1,0:T(8,128)(2,1)S(1)}, bf16[4,192,256]{2,1,0:T(8,128)(2,1)S(1)}, u32[]{:S(2)}, u32[]{:S(2)}) %collective-permute-start.11) | collective-permute-done | bytes 393248 | tf_op jit(solution)/shard_map/ppermute | solution.py:18
  147.5 5.0 %collective-permute-start.12 = (bf16[4,192,256]{2,1,0:T(8,128)(2,1)S(1)}, bf16[4,192,256]{2,1,0:T(8,128)(2,1)S(1)}, u32[]{:S(2)}, u32[]{:S(2)}) collective-permute-start(bf16[4,192,256]{2,1,0:T(8,128)(2,1)S(1)} %collective-permute-done.11.refs_1_), channel_id=1, source_target_pairs={{0,1},{1,2},{2,3},{3,4},{4,5},{5,6},{6,7},{7,0},{8,9},{9,10},{10,1... | collective-permute-start | bytes 1179656 | tf_op jit(solution)/shard_map/ppermute | solution.py:18
  154.5 3.8 %collective-permute-done.12.refs_2_ = bf16[4,192,256]{2,1,0:T(8,128)(2,1)S(1)} collective-permute-done((bf16[4,192,256]{2,1,0:T(8,128)(2,1)S(1)}, bf16[4,192,256]{2,1,0:T(8,128)(2,1)S(1)}, u32[]{:S(2)}, u32[]{:S(2)}) %collective-permute-start.12) | collective-permute-done | bytes 393248 | tf_op jit(solution)/shard_map/ppermute | solution.py:18
  158.3 5.6 %collective-permute-start.13 = (bf16[4,192,256]{2,1,0:T(8,128)(2,1)S(1)}, bf16[4,192,256]{2,1,0:T(8,128)(2,1)S(1)}, u32[]{:S(2)}, u32[]{:S(2)}) collective-permute-start(bf16[4,192,256]{2,1,0:T(8,128)(2,1)S(1)} %collective-permute-done.12.refs_2_), channel_id=1, source_target_pairs={{0,1},{1,2},{2,3},{3,4},{4,5},{5,6},{6,7},{7,0},{8,9},{9,10},{10,1... | collective-permute-start | bytes 1179656 | tf_op jit(solution)/shard_map/ppermute | solution.py:18
  166.2 4.6 %collective-permute-done.13.refs_3_ = bf16[4,192,256]{2,1,0:T(8,128)(2,1)S(1)} collective-permute-done((bf16[4,192,256]{2,1,0:T(8,128)(2,1)S(1)}, bf16[4,192,256]{2,1,0:T(8,128)(2,1)S(1)}, u32[]{:S(2)}, u32[]{:S(2)}) %collective-permute-start.13) | collective-permute-done | bytes 393248 | tf_op jit(solution)/shard_map/ppermute | solution.py:18
  170.8 5.6 %collective-permute-start.14 = (bf16[2,192,256]{2,1,0:T(8,128)(2,1)S(1)}, bf16[2,192,256]{2,1,0:T(8,128)(2,1)S(1)}, u32[]{:S(2)}, u32[]{:S(2)}) collective-permute-start(bf16[2,192,256]{2,1,0:T(8,128)(2,1)S(1)} %slice.8), channel_id=1, source_target_pairs={{0,1},{1,2},{2,3},{3,4},{4,5},{5,6},{6,7},{7,0},{8,9},{9,10},{10,1... | collective-permute-start | bytes 589832 | tf_op jit(solution)/shard_map/ppermute | solution.py:18
  180.8 5.1 %collective-permute-done.18.refs_1_ = bf16[2,192,256]{2,1,0:T(8,128)(2,1)S(1)} collective-permute-done((bf16[2,192,256]{2,1,0:T(8,128)(2,1)S(1)}, bf16[2,192,256]{2,1,0:T(8,128)(2,1)S(1)}, u32[]{:S(2)}, u32[]{:S(2)}) %collective-permute-start.18) | collective-permute-done | bytes 196640 | tf_op jit(solution)/shard_map/ppermute | solution.py:18
  187.5 4.0 %all-to-all-start = ((bf16[16,4,16,256]{3,2,1,0:T(8,128)(2,1)}), bf16[16,4,16,256]{3,2,1,0:T(8,128)(2,1)S(1)}, u32[]{:S(2)}, u32[]{:S(2)}) async-start(bf16[16,4,16,256]{3,2,1,0:T(8,128)(2,1)} %shard_map.71), calls=%async_computation | async-start | bytes 1048576 | tf_op jit(solution)/shard_map/all_to_all | solution.py:283
  192.2 19.0 %all-to-all-done = bf16[16,4,16,256]{3,2,1,0:T(8,128)(2,1)S(1)} async-done(((bf16[16,4,16,256]{3,2,1,0:T(8,128)(2,1)}), bf16[16,4,16,256]{3,2,1,0:T(8,128)(2,1)S(1)}, u32[]{:S(2)}, u32[]{:S(2)}) %all-to-all-start) | async-done | bytes 524320 | tf_op jit(solution)/shard_map/all_to_all | solution.py:283
  (53 shorter events, 27.0 us)
Async XLA Ops:
  0.0 76.1 %copy-start = (bf16[2,2048,192]{1,2,0:T(8,128)(2,1)S(1)}, bf16[2,2048,192]{1,2,0:T(8,128)(2,1)}, u32[]{:S(2)}) copy-start(bf16[2,2048,192]{1,2,0:T(8,128)(2,1)} %param.9) | copy-start | bytes 4718596
  74.2 6.4 %collective-permute-start.6 = (bf16[4,256,256]{2,1,0:T(8,128)(2,1)S(1)}, bf16[4,256,256]{2,1,0:T(8,128)(2,1)S(1)}, u32[]{:S(2)}, u32[]{:S(2)}) collective-permute-start(bf16[4,256,256]{2,1,0:T(8,128)(2,1)S(1)} %shard_map.65.refs_0_), channel_id=1, source_target_pairs={{0,8},{8,0},{1,9},{9,1},{2,10},{10,2},{3,11},{11,3},{4,12},{12,4},... | collective-permute-start | bytes 1572872 | tf_op jit(solution)/shard_map/ppermute | solution.py:13
  76.1 39.4 %collective-permute-start.4 = (bf16[2,192,2048]{2,1,0:T(8,128)(2,1)S(1)}, bf16[2,192,2048]{2,1,0:T(8,128)(2,1)S(1)}, u32[]{:S(2)}, u32[]{:S(2)}) collective-permute-start(bf16[2,192,2048]{2,1,0:T(8,128)(2,1)S(1)} %bitcast.11), channel_id=1, source_target_pairs={{0,8},{8,0},{1,9},{9,1},{2,10},{10,2},{3,11},{11,3},{4,12},{12,4},... | collective-permute-start | bytes 4718600 | tf_op jit(solution)/shard_map/ppermute | solution.py:13
  78.6 37.0 %collective-permute-start.5 = (bf16[2,192,2048]{2,1,0:T(8,128)(2,1)}, bf16[2,192,2048]{2,1,0:T(8,128)(2,1)S(1)}, u32[]{:S(2)}, u32[]{:S(2)}) collective-permute-start(bf16[2,192,2048]{2,1,0:T(8,128)(2,1)} %bitcast.16), channel_id=1, source_target_pairs={{0,8},{8,0},{1,9},{9,1},{2,10},{10,2},{3,11},{11,3},{4,12},{12,4},... | collective-permute-start | bytes 4718600 | tf_op jit(solution)/shard_map/ppermute | solution.py:13
  80.5 11.5 %collective-permute-start.7 = (bf16[4,256,256]{2,1,0:T(8,128)(2,1)S(1)}, bf16[4,256,256]{2,1,0:T(8,128)(2,1)S(1)}, u32[]{:S(2)}, u32[]{:S(2)}) collective-permute-start(bf16[4,256,256]{2,1,0:T(8,128)(2,1)S(1)} %collective-permute-done.6), channel_id=1, source_target_pairs={{0,1},{1,2},{2,3},{3,4},{4,5},{5,6},{6,7},{7,0},{8,15},{9,8},{10,9... | collective-permute-start | bytes 1572872 | tf_op jit(solution)/shard_map/ppermute | solution.py:25
  85.3 12.3 %collective-permute-start = (bf16[4,256,256]{2,1,0:T(8,128)(2,1)S(1)}, bf16[4,256,256]{2,1,0:T(8,128)(2,1)S(1)}, u32[]{:S(2)}, u32[]{:S(2)}) collective-permute-start(bf16[4,256,256]{2,1,0:T(8,128)(2,1)S(1)} %shard_map.65.refs_0_), channel_id=1, source_target_pairs={{0,1},{1,2},{2,3},{3,4},{4,5},{5,6},{6,7},{7,0},{8,15},{9,8},{10,9... | collective-permute-start | bytes 1572872 | tf_op jit(solution)/shard_map/ppermute | solution.py:25
  92.0 12.3 %collective-permute-start.8 = (bf16[4,256,256]{2,1,0:T(8,128)(2,1)S(1)}, bf16[4,256,256]{2,1,0:T(8,128)(2,1)S(1)}, u32[]{:S(2)}, u32[]{:S(2)}) collective-permute-start(bf16[4,256,256]{2,1,0:T(8,128)(2,1)S(1)} %collective-permute-done.7.refs_0_), channel_id=1, source_target_pairs={{0,1},{1,2},{2,3},{3,4},{4,5},{5,6},{6,7},{7,0},{8,15},{9,8},{10,9... | collective-permute-start | bytes 1572872 | tf_op jit(solution)/shard_map/ppermute | solution.py:25
  97.6 12.3 %collective-permute-start.1 = (bf16[4,256,256]{2,1,0:T(8,128)(2,1)S(1)}, bf16[4,256,256]{2,1,0:T(8,128)(2,1)S(1)}, u32[]{:S(2)}, u32[]{:S(2)}) collective-permute-start(bf16[4,256,256]{2,1,0:T(8,128)(2,1)S(1)} %collective-permute-done.refs_1_), channel_id=1, source_target_pairs={{0,1},{1,2},{2,3},{3,4},{4,5},{5,6},{6,7},{7,0},{8,15},{9,8},{10,9... | collective-permute-start | bytes 1572872 | tf_op jit(solution)/shard_map/ppermute | solution.py:25
  104.3 14.1 %collective-permute-start.9 = (bf16[4,256,256]{2,1,0:T(8,128)(2,1)S(1)}, bf16[4,256,256]{2,1,0:T(8,128)(2,1)S(1)}, u32[]{:S(2)}, u32[]{:S(2)}) collective-permute-start(bf16[4,256,256]{2,1,0:T(8,128)(2,1)S(1)} %collective-permute-done.8.refs_1_), channel_id=1, source_target_pairs={{0,1},{1,2},{2,3},{3,4},{4,5},{5,6},{6,7},{7,0},{8,15},{9,8},{10,9... | collective-permute-start | bytes 1572872 | tf_op jit(solution)/shard_map/ppermute | solution.py:25
  109.9 12.3 %collective-permute-start.2 = (bf16[4,256,256]{2,1,0:T(8,128)(2,1)S(1)}, bf16[4,256,256]{2,1,0:T(8,128)(2,1)S(1)}, u32[]{:S(2)}, u32[]{:S(2)}) collective-permute-start(bf16[4,256,256]{2,1,0:T(8,128)(2,1)S(1)} %collective-permute-done.1.refs_2_), channel_id=1, source_target_pairs={{0,1},{1,2},{2,3},{3,4},{4,5},{5,6},{6,7},{7,0},{8,15},{9,8},{10,9... | collective-permute-start | bytes 1572872 | tf_op jit(solution)/shard_map/ppermute | solution.py:25
  118.4 11.5 %copy-start.2 = (bf16[2,2048,192]{1,2,0:T(8,128)(2,1)S(1)}, bf16[2,2048,192]{1,2,0:T(8,128)(2,1)}, u32[]{:S(2)}) copy-start(bf16[2,2048,192]{1,2,0:T(8,128)(2,1)} %param.10) | copy-start | bytes 4718596
  119.4 15.1 %collective-permute-start.10 = (bf16[4,384,256]{2,1,0:T(8,128)(2,1)S(1)}, bf16[4,384,256]{2,1,0:T(8,128)(2,1)S(1)}, u32[]{:S(2)}, u32[]{:S(2)}) collective-permute-start(bf16[4,384,256]{2,1,0:T(8,128)(2,1)S(1)} %shard_map.68), channel_id=1, source_target_pairs={{0,8},{8,0},{1,9},{9,1},{2,10},{10,2},{3,11},{11,3},{4,12},{12,4},... | collective-permute-start | bytes 2359304 | tf_op jit(solution)/shard_map/ppermute | solution.py:13
  122.2 12.3 %collective-permute-start.3 = (bf16[4,256,256]{2,1,0:T(8,128)(2,1)S(1)}, bf16[4,256,256]{2,1,0:T(8,128)(2,1)S(1)}, u32[]{:S(2)}, u32[]{:S(2)}) collective-permute-start(bf16[4,256,256]{2,1,0:T(8,128)(2,1)S(1)} %collective-permute-done.2.refs_0_), channel_id=1, source_target_pairs={{0,1},{1,2},{2,3},{3,4},{4,5},{5,6},{6,7},{7,0},{8,15},{9,8},{10,9... | collective-permute-start | bytes 1572872 | tf_op jit(solution)/shard_map/ppermute | solution.py:25
  127.9 51.1 %collective-permute-start.19 = (bf16[2,1536,256]{2,1,0:T(8,128)(2,1)S(1)}, bf16[2,1536,256]{2,1,0:T(8,128)(2,1)S(1)}, u32[]{:S(2)}, u32[]{:S(2)}) collective-permute-start(bf16[2,1536,256]{2,1,0:T(8,128)(2,1)S(1)} %copy-done.3), channel_id=1, source_target_pairs={{0,8},{8,0},{1,9},{9,1},{2,10},{10,2},{3,11},{11,3},{4,12},{12,4},... | collective-permute-start | bytes 4718600 | tf_op jit(solution)/shard_map/ppermute | solution.py:13
  136.0 11.5 %collective-permute-start.11 = (bf16[4,192,256]{2,1,0:T(8,128)(2,1)S(1)}, bf16[4,192,256]{2,1,0:T(8,128)(2,1)S(1)}, u32[]{:S(2)}, u32[]{:S(2)}) collective-permute-start(bf16[4,192,256]{2,1,0:T(8,128)(2,1)S(1)} %shard_map.69.refs_0_), channel_id=1, source_target_pairs={{0,1},{1,2},{2,3},{3,4},{4,5},{5,6},{6,7},{7,0},{8,9},{9,10},{10,1... | collective-permute-start | bytes 1179656 | tf_op jit(solution)/shard_map/ppermute | solution.py:18
  141.7 10.9 %collective-permute-start.15 = (bf16[4,192,256]{2,1,0:T(8,128)(2,1)S(1)}, bf16[4,192,256]{2,1,0:T(8,128)(2,1)S(1)}, u32[]{:S(2)}, u32[]{:S(2)}) collective-permute-start(bf16[4,192,256]{2,1,0:T(8,128)(2,1)S(1)} %shard_map.69.refs_0_), channel_id=1, source_target_pairs={{0,7},{1,0},{2,1},{3,2},{4,3},{5,4},{6,5},{7,6},{8,15},{9,8},{10,9... | collective-permute-start | bytes 1179656 | tf_op jit(solution)/shard_map/ppermute | solution.py:18
  147.5 10.8 %collective-permute-start.12 = (bf16[4,192,256]{2,1,0:T(8,128)(2,1)S(1)}, bf16[4,192,256]{2,1,0:T(8,128)(2,1)S(1)}, u32[]{:S(2)}, u32[]{:S(2)}) collective-permute-start(bf16[4,192,256]{2,1,0:T(8,128)(2,1)S(1)} %collective-permute-done.11.refs_1_), channel_id=1, source_target_pairs={{0,1},{1,2},{2,3},{3,4},{4,5},{5,6},{6,7},{7,0},{8,9},{9,10},{10,1... | collective-permute-start | bytes 1179656 | tf_op jit(solution)/shard_map/ppermute | solution.py:18
  152.6 11.7 %collective-permute-start.16 = (bf16[4,192,256]{2,1,0:T(8,128)(2,1)S(1)}, bf16[4,192,256]{2,1,0:T(8,128)(2,1)S(1)}, u32[]{:S(2)}, u32[]{:S(2)}) collective-permute-start(bf16[4,192,256]{2,1,0:T(8,128)(2,1)S(1)} %collective-permute-done.15.refs_4_), channel_id=1, source_target_pairs={{0,7},{1,0},{2,1},{3,2},{4,3},{5,4},{6,5},{7,6},{8,15},{9,8},{10,9... | collective-permute-start | bytes 1179656 | tf_op jit(solution)/shard_map/ppermute | solution.py:18
  158.3 12.5 %collective-permute-start.13 = (bf16[4,192,256]{2,1,0:T(8,128)(2,1)S(1)}, bf16[4,192,256]{2,1,0:T(8,128)(2,1)S(1)}, u32[]{:S(2)}, u32[]{:S(2)}) collective-permute-start(bf16[4,192,256]{2,1,0:T(8,128)(2,1)S(1)} %collective-permute-done.12.refs_2_), channel_id=1, source_target_pairs={{0,1},{1,2},{2,3},{3,4},{4,5},{5,6},{6,7},{7,0},{8,9},{9,10},{10,1... | collective-permute-start | bytes 1179656 | tf_op jit(solution)/shard_map/ppermute | solution.py:18
  164.2 12.8 %collective-permute-start.17 = (bf16[4,192,256]{2,1,0:T(8,128)(2,1)S(1)}, bf16[4,192,256]{2,1,0:T(8,128)(2,1)S(1)}, u32[]{:S(2)}, u32[]{:S(2)}) collective-permute-start(bf16[4,192,256]{2,1,0:T(8,128)(2,1)S(1)} %collective-permute-done.16.refs_5_), channel_id=1, source_target_pairs={{0,7},{1,0},{2,1},{3,2},{4,3},{5,4},{6,5},{7,6},{8,15},{9,8},{10,9... | collective-permute-start | bytes 1179656 | tf_op jit(solution)/shard_map/ppermute | solution.py:18
  170.8 9.9 %collective-permute-start.14 = (bf16[2,192,256]{2,1,0:T(8,128)(2,1)S(1)}, bf16[2,192,256]{2,1,0:T(8,128)(2,1)S(1)}, u32[]{:S(2)}, u32[]{:S(2)}) collective-permute-start(bf16[2,192,256]{2,1,0:T(8,128)(2,1)S(1)} %slice.8), channel_id=1, source_target_pairs={{0,1},{1,2},{2,3},{3,4},{4,5},{5,6},{6,7},{7,0},{8,9},{9,10},{10,1... | collective-permute-start | bytes 589832 | tf_op jit(solution)/shard_map/ppermute | solution.py:18
  177.0 8.8 %collective-permute-start.18 = (bf16[2,192,256]{2,1,0:T(8,128)(2,1)S(1)}, bf16[2,192,256]{2,1,0:T(8,128)(2,1)S(1)}, u32[]{:S(2)}, u32[]{:S(2)}) collective-permute-start(bf16[2,192,256]{2,1,0:T(8,128)(2,1)S(1)} %slice.9), channel_id=1, source_target_pairs={{0,7},{1,0},{2,1},{3,2},{4,3},{5,4},{6,5},{7,6},{8,15},{9,8},{10,9... | collective-permute-start | bytes 589832 | tf_op jit(solution)/shard_map/ppermute | solution.py:18
  180.8 11.0 %copy-start.7 = (s32[64,8]{0,1:T(8,128)S(1)}, s32[64,8]{0,1:T(8,128)}, u32[]{:S(2)}) copy-start(s32[64,8]{0,1:T(8,128)} %param.8) | copy-start | bytes 6148
  187.5 23.7 %all-to-all-start = ((bf16[16,4,16,256]{3,2,1,0:T(8,128)(2,1)}), bf16[16,4,16,256]{3,2,1,0:T(8,128)(2,1)S(1)}, u32[]{:S(2)}, u32[]{:S(2)}) async-start(bf16[16,4,16,256]{3,2,1,0:T(8,128)(2,1)} %shard_map.71), calls=%async_computation | async-start | bytes 1048576 | tf_op jit(solution)/shard_map/all_to_all | solution.py:283
  (5 other events, 23.3 us)

commit v4 on v2

--- a/solution.py
+++ b/solution.py
@@ -30,9 +30,29 @@
     ).astype(jnp.int32)
 
 
-def chosen_rows(gathered, first, turn, tok_dev, picks, chip_experts, capacity):
+def with_ids(tokens, ids):
+    tok_dev, width = tokens.shape
+    picks = ids.shape[0]
+
+    def body(tokens_ref, ids_ref, out_ref):
+        out_ref[:tok_dev] = tokens_ref[...]
+        found = ids_ref[...].astype(jnp.float32)
+        tall = jnp.concatenate([found, jnp.zeros((picks, tok_dev), jnp.float32)], axis=0)
+        wide = jnp.concatenate([tall, jnp.zeros((2 * picks, width - tok_dev), jnp.float32)], axis=1)
+        out_ref[tok_dev:] = wide.astype(jnp.bfloat16)
+
+    return pl.pallas_call(
+        body,
+        out_shape=jax.ShapeDtypeStruct((tok_dev + 2 * picks, width), jnp.bfloat16),
+        compiler_params=pltpu.CompilerParams(vmem_limit_bytes=4 * 2**20),
+        cost_estimate=pl.CostEstimate(flops=2 * tokens.size, bytes_accessed=4 * tokens.size, transcendentals=0),
+    )(tokens, ids)
+
+
+def chosen_rows(gathered, table, tok_dev, picks, chip_experts, capacity):
     sources, _, width = gathered.shape
     slots = chip_experts * capacity
+    end = table.shape[0]
 
     def body(table_ref, gathered_ref, out_ref):
         row = lax.broadcasted_iota(jnp.int32, (tok_dev, tok_dev), 0)
@@ -42,7 +62,7 @@
         for s in range(sources):
             ids = gathered_ref[s, tok_dev : tok_dev + picks, :tok_dev].astype(jnp.float32)
             for e in range(chip_experts):
-                name = table_ref[0] + lax.rem(table_ref[1] + e, chip_experts)
+                name = table_ref[end - 2] + lax.rem(table_ref[end - 1] + e, chip_experts)
                 same = jnp.where(ids == name.astype(jnp.float32), 1.0, 0.0)
                 lines.append(jnp.max(same, axis=0, keepdims=True))
         member = jnp.concatenate(lines, axis=0)
@@ -70,7 +90,6 @@
                     e * capacity : (e + 1) * capacity
                 ]
 
-    table = jnp.stack([first, turn]).astype(jnp.int32)
     return pl.pallas_call(
         body,
         in_specs=[pl.BlockSpec(memory_space=pltpu.SMEM), pl.BlockSpec(memory_space=pltpu.VMEM)],
@@ -85,11 +104,12 @@
     )(table, gathered)
 
 
-def weighted_sum(parts, steps, weights, table, kind, ours_first, extra=(), finish=None, out=None):
-    chip_experts = parts[0].shape[0]
+def weighted_sum(parts, steps, weights, table, kind, order, extra=(), finish=None, out=None):
     exp_dev = weights[0][0].shape[0]
-    n_parts, n_kinds = len(parts), len(weights)
+    chip_experts = exp_dev * CORES
+    n_kinds = len(weights)
     into = kind == "in"
+    n_parts = len(parts)
     if into:
         hid, width = weights[0][0].shape[1], parts[0].shape[2]
         rows = parts[0].shape[1]
@@ -107,30 +127,29 @@
         weight_refs, rest = rest[: 2 * n_kinds], rest[2 * n_kinds :]
         extra_refs, out_ref = rest[:-1], rest[-1]
         for e in range(chip_experts):
-            side = (e // exp_dev) ^ (0 if ours_first else 1)
+            side = order[e // exp_dev]
             sums = []
             for k in range(n_kinds):
                 ref = weight_refs[2 * k + side]
-                if into:
-                    total = [x[e, k * hid : (k + 1) * hid] for x in extra_refs]
-                else:
-                    total = [x[e] for x in extra_refs]
+                spot = (slice(k * hid, (k + 1) * hid),) if into else ()
+                total = [x[(e, *spot)].astype(jnp.float32) for x in extra_refs]
                 for part_ref, step in zip(part_refs, steps):
+                    part = part_ref[e]
                     if into:
                         at = pl.ds(pl.multiple_of(table_ref[step] * width, width), width)
-                        pair = (ref[e % exp_dev, :, at], part_ref[e])
+                        pair = (ref[e % exp_dev, :, at], part)
                     else:
                         at = pl.ds(pl.multiple_of(table_ref[step] * hid, hid), hid)
-                        pair = (part_ref[e], ref[e % exp_dev, at, :])
+                        pair = (part, ref[e % exp_dev, at, :])
                     total.append(lax.dot_general(*pair, dims, preferred_element_type=jnp.float32))
                 sums.append(sum(total[1:], total[0]))
             if finish is not None:
                 finish(out_ref, e, *sums)
             elif into:
                 for k, total in enumerate(sums):
-                    out_ref[e, k * hid : (k + 1) * hid] = total
+                    out_ref[e, k * hid : (k + 1) * hid] = total.astype(out_ref.dtype)
             else:
-                out_ref[e] = sums[0]
+                out_ref[e] = sums[0].astype(out_ref.dtype)
 
     whole = pl.BlockSpec(memory_space=pltpu.VMEM)
     operands = [*parts, *(w for pair in weights for w in pair), *extra]
@@ -146,22 +165,26 @@
     )(table, *operands)
 
 
-def gather_sum(own, weights, table, kind, finish, out):
+def gather_sum(own, weights, owners, kind, finish, out):
     half = lax.axis_size("dp") // 2
+    summed = lambda parts, steps, order, *rest: weighted_sum(
+        parts, steps, weights, owners, kind, order, *rest
+    )
     mine = [own]
     for _ in range(1, half + 1):
         mine.append(onward(mine[-1]))
     other = [swap(own)]
     for _ in range(1, half):
         other.append(onward(other[-1]))
-    early = weighted_sum(mine[:half], range(half), weights, table, kind, True)
-    aside = weighted_sum(other[1:], range(1, half), weights, table, kind, False)
+    early = summed(mine[: half - 1], range(half - 1), (0, 1))
+    ahead = summed(other[1 : half - 1], range(1, half - 1), (1, 0))
+    aside = summed(other[half - 1 :], [half - 1], (1, 0), (ahead,))
     back = swap(aside)
-    return weighted_sum(mine[half:], [half], weights, table, kind, True, (early, back), finish, out)
+    return summed(mine[half - 1 :], [half - 1, half], (0, 1), (early, back), finish, out)
 
 
 def layer(tokens, expert_ids, gate_levels, gate_weight, up_weight, down_weight):
-    tok_dev, width = tokens.shape
+    tok_dev, _ = tokens.shape
     picks = expert_ids.shape[1]
     exp_dev = gate_weight.shape[0]
     hid = gate_weight.shape[2]
@@ -172,17 +195,17 @@
     core = lax.axis_index("core")
     z = lax.axis_index("z")
 
-    ids_rows = jnp.zeros((2 * picks, width), jnp.bfloat16)
-    ids_rows = ids_rows.at[:picks, :tok_dev].set(expert_ids.T.astype(jnp.bfloat16))
     n_dp = lax.axis_size("dp")
-    step = jnp.arange(n_dp, dtype=jnp.int32)
-    table = (lax.axis_index("dp") + jnp.where(core == 0, -step, step)) % n_dp
-
-    payload = jnp.concatenate([tokens, ids_rows], axis=0)
+    at = jnp.arange(n_dp + 2, dtype=jnp.int32)
+    table = (lax.axis_index("dp") + jnp.where(core == 1, at, -at)) % n_dp
+    table = jnp.where(at == n_dp, z * chip_experts, table)
+    table = jnp.where(at == n_dp + 1, core * exp_dev, table)
+
+    payload = with_ids(tokens, expert_ids.T)
     payload, table = lax.optimization_barrier((payload, table))
     gathered = lax.all_gather(payload, "z", axis=0)
     count = n_z * capacity
-    rows = chosen_rows(gathered, z * chip_experts, core * exp_dev, tok_dev, picks, chip_experts, capacity)
+    rows = chosen_rows(gathered, table, tok_dev, picks, chip_experts, capacity)
 
     pairs = []
     for weights in (jnp.swapaxes(gate_weight, 1, 2), jnp.swapaxes(up_weight, 1, 2), down_weight):

time: 243 us -> 244 us (level)
    pallas_call x6 -> x8, Pallas kernels: 9.05 us -> 10.5 us  [weighted_sum(): pl.pallas_call(body, in_specs=[pl.BlockSpec(memory_space=pltpu.SMEM)] + [...]
  transfers between devices with their start and end apart: 22 -> 22, of which waited for: 13 -> 12; matrix products, arithmetic and copies ran while one was open for 0% -> 0% of each run, Pallas kernels for 3% -> 4%
where the time goes in v4:
time: 244 us; the launch traced here: 243 us
  starting transfers between devices  87 us (36%)
  blocking collectives  71.6 us (29%)
  waiting for transfers between devices  68.5 us (28%)
  Pallas kernels  11.5 us (5%)
  local copies, waits for them, and re-layouts  3 us (1%)
    all_gather x1, blocking collectives, layer(): gathered = lax.all_gather(payload, 'z', axis=0)  71.6 us
    ppermute x14, starting transfers between devices, onward(): return lax.ppermute(block, ('core', 'dp'), up + down)  68.8 us
    ppermute x14, waiting for transfers between devices, onward(): return lax.ppermute(block, ('core', 'dp'), up + down)  41.4 us
    all_to_all x1, waiting for transfers between devices, layer(): lax.all_to_all(result, 'z', split_axis=0, concat_axis=0, tiled=True)  25.3 us
    ppermute x7, starting transfers between devices, swap(): return lax.ppermute(block, 'core', [(0, 1), (1, 0)])  14.1 us
    pallas_call x8, Pallas kernels, weighted_sum(): pl.pallas_call(body, in_specs=[pl.BlockSpec(memory_space=pltpu.SMEM)] + [...  10.5 us
  transfers between devices with their start and end apart: 22, of which 12 were waited for; matrix products, arithmetic and copies ran while one was open for 0% of the time, Pallas kernels for 4%

profile of v4, /device:TPU:86, one launch (start us, length us, event | category | flops | bytes accessed | tf_op | source)
XLA Modules:
  0.0 243.4 jit_solution(8081581701861597713)
XLA Ops:
  1.6 71.6 %all-gather = bf16[1280,256]{1,0:T(8,128)(2,1)S(1)} all-gather(bf16[80,256]{1,0:T(8,128)(2,1)S(1)} %shard_map.64), channel_id=2, replica_groups=mesh['groups'=2,'z'=16,'core'=2,'dp'=8] {'z'}, dimensions={0}, use_global_device_ids=true | all-gather | bytes 696320 | tf_op jit(solution)/shard_map/all_gather | solution.py:206
  76.1 2.4 %collective-permute-start.4 = (bf16[2,192,2048]{2,1,0:T(8,128)(2,1)S(1)}, bf16[2,192,2048]{2,1,0:T(8,128)(2,1)S(1)}, u32[]{:S(2)}, u32[]{:S(2)}) collective-permute-start(bf16[2,192,2048]{2,1,0:T(8,128)(2,1)S(1)} %bitcast.11), channel_id=1, source_target_pairs={{0,8},{8,0},{1,9},{9,1},{2,10},{10,2},{3,11},{11,3},{4,12},{12,4},... | collective-permute-start | bytes 4718600 | tf_op jit(solution)/shard_map/ppermute | solution.py:13
  80.5 4.8 %collective-permute-start.7 = (bf16[4,256,256]{2,1,0:T(8,128)(2,1)S(1)}, bf16[4,256,256]{2,1,0:T(8,128)(2,1)S(1)}, u32[]{:S(2)}, u32[]{:S(2)}) collective-permute-start(bf16[4,256,256]{2,1,0:T(8,128)(2,1)S(1)} %collective-permute-done.6), channel_id=1, source_target_pairs={{0,1},{1,2},{2,3},{3,4},{4,5},{5,6},{6,7},{7,0},{8,15},{9,8},{10,9... | collective-permute-start | bytes 1572872 | tf_op jit(solution)/shard_map/ppermute | solution.py:20
  85.3 6.7 %collective-permute-done.7.refs_0_ = bf16[4,256,256]{2,1,0:T(8,128)(2,1)S(1)} collective-permute-done((bf16[4,256,256]{2,1,0:T(8,128)(2,1)S(1)}, bf16[4,256,256]{2,1,0:T(8,128)(2,1)S(1)}, u32[]{:S(2)}, u32[]{:S(2)}) %collective-permute-start.7) | collective-permute-done | bytes 524320 | tf_op jit(solution)/shard_map/ppermute | solution.py:20
  92.0 5.6 %collective-permute-start.8 = (bf16[4,256,256]{2,1,0:T(8,128)(2,1)S(1)}, bf16[4,256,256]{2,1,0:T(8,128)(2,1)S(1)}, u32[]{:S(2)}, u32[]{:S(2)}) collective-permute-start(bf16[4,256,256]{2,1,0:T(8,128)(2,1)S(1)} %collective-permute-done.7.refs_0_), channel_id=1, source_target_pairs={{0,1},{1,2},{2,3},{3,4},{4,5},{5,6},{6,7},{7,0},{8,15},{9,8},{10,9... | collective-permute-start | bytes 1572872 | tf_op jit(solution)/shard_map/ppermute | solution.py:20
  99.6 4.7 %collective-permute-done.8.refs_1_ = bf16[4,256,256]{2,1,0:T(8,128)(2,1)S(1)} collective-permute-done((bf16[4,256,256]{2,1,0:T(8,128)(2,1)S(1)}, bf16[4,256,256]{2,1,0:T(8,128)(2,1)S(1)}, u32[]{:S(2)}, u32[]{:S(2)}) %collective-permute-start.8) | collective-permute-done | bytes 524320 | tf_op jit(solution)/shard_map/ppermute | solution.py:20
  104.3 5.6 %collective-permute-start.9 = (bf16[4,256,256]{2,1,0:T(8,128)(2,1)S(1)}, bf16[4,256,256]{2,1,0:T(8,128)(2,1)S(1)}, u32[]{:S(2)}, u32[]{:S(2)}) collective-permute-start(bf16[4,256,256]{2,1,0:T(8,128)(2,1)S(1)} %collective-permute-done.8.refs_1_), channel_id=1, source_target_pairs={{0,1},{1,2},{2,3},{3,4},{4,5},{5,6},{6,7},{7,0},{8,15},{9,8},{10,9... | collective-permute-start | bytes 1572872 | tf_op jit(solution)/shard_map/ppermute | solution.py:20
  109.9 5.6 %collective-permute-start.1 = (bf16[4,256,256]{2,1,0:T(8,128)(2,1)S(1)}, bf16[4,256,256]{2,1,0:T(8,128)(2,1)S(1)}, u32[]{:S(2)}, u32[]{:S(2)}) collective-permute-start(bf16[4,256,256]{2,1,0:T(8,128)(2,1)S(1)} %collective-permute-done.refs_1_), channel_id=1, source_target_pairs={{0,1},{1,2},{2,3},{3,4},{4,5},{5,6},{6,7},{7,0},{8,15},{9,8},{10,9... | collective-permute-start | bytes 1572872 | tf_op jit(solution)/shard_map/ppermute | solution.py:20
  122.2 5.6 %collective-permute-start.2 = (bf16[4,256,256]{2,1,0:T(8,128)(2,1)S(1)}, bf16[4,256,256]{2,1,0:T(8,128)(2,1)S(1)}, u32[]{:S(2)}, u32[]{:S(2)}) collective-permute-start(bf16[4,256,256]{2,1,0:T(8,128)(2,1)S(1)} %collective-permute-done.1.refs_2_), channel_id=1, source_target_pairs={{0,1},{1,2},{2,3},{3,4},{4,5},{5,6},{6,7},{7,0},{8,15},{9,8},{10,9... | collective-permute-start | bytes 1572872 | tf_op jit(solution)/shard_map/ppermute | solution.py:20
  127.9 6.7 %collective-permute-done.2.refs_0_ = bf16[4,256,256]{2,1,0:T(8,128)(2,1)S(1)} collective-permute-done((bf16[4,256,256]{2,1,0:T(8,128)(2,1)S(1)}, bf16[4,256,256]{2,1,0:T(8,128)(2,1)S(1)}, u32[]{:S(2)}, u32[]{:S(2)}) %collective-permute-start.2) | collective-permute-done | bytes 524320 | tf_op jit(solution)/shard_map/ppermute | solution.py:20
  134.5 5.6 %collective-permute-start.3 = (bf16[4,256,256]{2,1,0:T(8,128)(2,1)S(1)}, bf16[4,256,256]{2,1,0:T(8,128)(2,1)S(1)}, u32[]{:S(2)}, u32[]{:S(2)}) collective-permute-start(bf16[4,256,256]{2,1,0:T(8,128)(2,1)S(1)} %collective-permute-done.2.refs_0_), channel_id=1, source_target_pairs={{0,1},{1,2},{2,3},{3,4},{4,5},{5,6},{6,7},{7,0},{8,15},{9,8},{10,9... | collective-permute-start | bytes 1572872 | tf_op jit(solution)/shard_map/ppermute | solution.py:20
  143.9 3.0 %collective-permute-done.3.refs_1_ = bf16[4,256,256]{2,1,0:T(8,128)(2,1)S(1)} collective-permute-done((bf16[4,256,256]{2,1,0:T(8,128)(2,1)S(1)}, bf16[4,256,256]{2,1,0:T(8,128)(2,1)S(1)}, u32[]{:S(2)}, u32[]{:S(2)}) %collective-permute-start.3) | collective-permute-done | bytes 524320 | tf_op jit(solution)/shard_map/ppermute | solution.py:20
  152.0 5.6 %collective-permute-start.17 = (bf16[4,192,256]{2,1,0:T(8,128)(2,1)S(1)}, bf16[4,192,256]{2,1,0:T(8,128)(2,1)S(1)}, u32[]{:S(2)}, u32[]{:S(2)}) collective-permute-start(bf16[4,192,256]{2,1,0:T(8,128)(2,1)S(1)} %collective-permute-done.16), channel_id=1, source_target_pairs={{0,1},{1,2},{2,3},{3,4},{4,5},{5,6},{6,7},{7,0},{8,15},{9,8},{10,9... | collective-permute-start | bytes 1179656 | tf_op jit(solution)/shard_map/ppermute | solution.py:20
  157.6 5.3 %collective-permute-done.17.refs_0_ = bf16[4,192,256]{2,1,0:T(8,128)(2,1)S(1)} collective-permute-done((bf16[4,192,256]{2,1,0:T(8,128)(2,1)S(1)}, bf16[4,192,256]{2,1,0:T(8,128)(2,1)S(1)}, u32[]{:S(2)}, u32[]{:S(2)}) %collective-permute-start.17) | collective-permute-done | bytes 393248 | tf_op jit(solution)/shard_map/ppermute | solution.py:20
  162.9 5.6 %collective-permute-start.18 = (bf16[4,192,256]{2,1,0:T(8,128)(2,1)S(1)}, bf16[4,192,256]{2,1,0:T(8,128)(2,1)S(1)}, u32[]{:S(2)}, u32[]{:S(2)}) collective-permute-start(bf16[4,192,256]{2,1,0:T(8,128)(2,1)S(1)} %collective-permute-done.17.refs_0_), channel_id=1, source_target_pairs={{0,1},{1,2},{2,3},{3,4},{4,5},{5,6},{6,7},{7,0},{8,15},{9,8},{10,9... | collective-permute-start | bytes 1179656 | tf_op jit(solution)/shard_map/ppermute | solution.py:20
  170.5 3.3 %collective-permute-done.18.refs_1_ = bf16[4,192,256]{2,1,0:T(8,128)(2,1)S(1)} collective-permute-done((bf16[4,192,256]{2,1,0:T(8,128)(2,1)S(1)}, bf16[4,192,256]{2,1,0:T(8,128)(2,1)S(1)}, u32[]{:S(2)}, u32[]{:S(2)}) %collective-permute-start.18) | collective-permute-done | bytes 393248 | tf_op jit(solution)/shard_map/ppermute | solution.py:20
  173.8 5.6 %collective-permute-start.19 = (bf16[4,192,256]{2,1,0:T(8,128)(2,1)S(1)}, bf16[4,192,256]{2,1,0:T(8,128)(2,1)S(1)}, u32[]{:S(2)}, u32[]{:S(2)}) collective-permute-start(bf16[4,192,256]{2,1,0:T(8,128)(2,1)S(1)} %collective-permute-done.18.refs_1_), channel_id=1, source_target_pairs={{0,1},{1,2},{2,3},{3,4},{4,5},{5,6},{6,7},{7,0},{8,15},{9,8},{10,9... | collective-permute-start | bytes 1179656 | tf_op jit(solution)/shard_map/ppermute | solution.py:20
  179.4 4.2 %collective-permute-start.12 = (bf16[4,192,256]{2,1,0:T(8,128)(2,1)S(1)}, bf16[4,192,256]{2,1,0:T(8,128)(2,1)S(1)}, u32[]{:S(2)}, u32[]{:S(2)}) collective-permute-start(bf16[4,192,256]{2,1,0:T(8,128)(2,1)S(1)} %collective-permute-done.11.refs_1_), channel_id=1, source_target_pairs={{0,1},{1,2},{2,3},{3,4},{4,5},{5,6},{6,7},{7,0},{8,15},{9,8},{10,9... | collective-permute-start | bytes 1179656 | tf_op jit(solution)/shard_map/ppermute | solution.py:20
  189.1 5.4 %collective-permute-start.13 = (bf16[4,192,256]{2,1,0:T(8,128)(2,1)S(1)}, bf16[4,192,256]{2,1,0:T(8,128)(2,1)S(1)}, u32[]{:S(2)}, u32[]{:S(2)}) collective-permute-start(bf16[4,192,256]{2,1,0:T(8,128)(2,1)S(1)} %collective-permute-done.12.refs_2_), channel_id=1, source_target_pairs={{0,1},{1,2},{2,3},{3,4},{4,5},{5,6},{6,7},{7,0},{8,15},{9,8},{10,9... | collective-permute-start | bytes 1179656 | tf_op jit(solution)/shard_map/ppermute | solution.py:20
  194.5 5.3 %collective-permute-done.13.refs_0_ = bf16[4,192,256]{2,1,0:T(8,128)(2,1)S(1)} collective-permute-done((bf16[4,192,256]{2,1,0:T(8,128)(2,1)S(1)}, bf16[4,192,256]{2,1,0:T(8,128)(2,1)S(1)}, u32[]{:S(2)}, u32[]{:S(2)}) %collective-permute-start.13) | collective-permute-done | bytes 393248 | tf_op jit(solution)/shard_map/ppermute | solution.py:20
  199.8 5.6 %collective-permute-start.14 = (bf16[4,192,256]{2,1,0:T(8,128)(2,1)S(1)}, bf16[4,192,256]{2,1,0:T(8,128)(2,1)S(1)}, u32[]{:S(2)}, u32[]{:S(2)}) collective-permute-start(bf16[4,192,256]{2,1,0:T(8,128)(2,1)S(1)} %collective-permute-done.13.refs_0_), channel_id=1, source_target_pairs={{0,1},{1,2},{2,3},{3,4},{4,5},{5,6},{6,7},{7,0},{8,15},{9,8},{10,9... | collective-permute-start | bytes 1179656 | tf_op jit(solution)/shard_map/ppermute | solution.py:20
  206.6 4.1 %collective-permute-done.14.refs_1_ = bf16[4,192,256]{2,1,0:T(8,128)(2,1)S(1)} collective-permute-done((bf16[4,192,256]{2,1,0:T(8,128)(2,1)S(1)}, bf16[4,192,256]{2,1,0:T(8,128)(2,1)S(1)}, u32[]{:S(2)}, u32[]{:S(2)}) %collective-permute-start.14) | collective-permute-done | bytes 393248 | tf_op jit(solution)/shard_map/ppermute | solution.py:20
  212.5 4.0 %all-to-all-start = ((bf16[16,4,16,256]{3,2,1,0:T(8,128)(2,1)}), bf16[16,4,16,256]{3,2,1,0:T(8,128)(2,1)S(1)}, u32[]{:S(2)}, u32[]{:S(2)}) async-start(bf16[16,4,16,256]{3,2,1,0:T(8,128)(2,1)} %shard_map.73), calls=%async_computation | async-start | bytes 1048576 | tf_op jit(solution)/shard_map/all_to_all | solution.py:239
  217.2 25.3 %all-to-all-done = bf16[16,4,16,256]{3,2,1,0:T(8,128)(2,1)S(1)} async-done(((bf16[16,4,16,256]{3,2,1,0:T(8,128)(2,1)}), bf16[16,4,16,256]{3,2,1,0:T(8,128)(2,1)S(1)}, u32[]{:S(2)}, u32[]{:S(2)}) %all-to-all-start) | async-done | bytes 524320 | tf_op jit(solution)/shard_map/all_to_all | solution.py:239
  (55 shorter events, 35.7 us)
Async XLA Ops:
  0.0 76.1 %copy-start = (bf16[2,2048,192]{1,2,0:T(8,128)(2,1)S(1)}, bf16[2,2048,192]{1,2,0:T(8,128)(2,1)}, u32[]{:S(2)}) copy-start(bf16[2,2048,192]{1,2,0:T(8,128)(2,1)} %param.9) | copy-start | bytes 4718596
  74.2 6.4 %collective-permute-start.6 = (bf16[4,256,256]{2,1,0:T(8,128)(2,1)S(1)}, bf16[4,256,256]{2,1,0:T(8,128)(2,1)S(1)}, u32[]{:S(2)}, u32[]{:S(2)}) collective-permute-start(bf16[4,256,256]{2,1,0:T(8,128)(2,1)S(1)} %shard_map.65.refs_0_), channel_id=1, source_target_pairs={{0,8},{8,0},{1,9},{9,1},{2,10},{10,2},{3,11},{11,3},{4,12},{12,4},... | collective-permute-start | bytes 1572872 | tf_op jit(solution)/shard_map/ppermute | solution.py:13
  76.1 39.4 %collective-permute-start.4 = (bf16[2,192,2048]{2,1,0:T(8,128)(2,1)S(1)}, bf16[2,192,2048]{2,1,0:T(8,128)(2,1)S(1)}, u32[]{:S(2)}, u32[]{:S(2)}) collective-permute-start(bf16[2,192,2048]{2,1,0:T(8,128)(2,1)S(1)} %bitcast.11), channel_id=1, source_target_pairs={{0,8},{8,0},{1,9},{9,1},{2,10},{10,2},{3,11},{11,3},{4,12},{12,4},... | collective-permute-start | bytes 4718600 | tf_op jit(solution)/shard_map/ppermute | solution.py:13
  78.6 37.0 %collective-permute-start.5 = (bf16[2,192,2048]{2,1,0:T(8,128)(2,1)}, bf16[2,192,2048]{2,1,0:T(8,128)(2,1)S(1)}, u32[]{:S(2)}, u32[]{:S(2)}) collective-permute-start(bf16[2,192,2048]{2,1,0:T(8,128)(2,1)} %bitcast.16), channel_id=1, source_target_pairs={{0,8},{8,0},{1,9},{9,1},{2,10},{10,2},{3,11},{11,3},{4,12},{12,4},... | collective-permute-start | bytes 4718600 | tf_op jit(solution)/shard_map/ppermute | solution.py:13
  80.5 11.5 %collective-permute-start.7 = (bf16[4,256,256]{2,1,0:T(8,128)(2,1)S(1)}, bf16[4,256,256]{2,1,0:T(8,128)(2,1)S(1)}, u32[]{:S(2)}, u32[]{:S(2)}) collective-permute-start(bf16[4,256,256]{2,1,0:T(8,128)(2,1)S(1)} %collective-permute-done.6), channel_id=1, source_target_pairs={{0,1},{1,2},{2,3},{3,4},{4,5},{5,6},{6,7},{7,0},{8,15},{9,8},{10,9... | collective-permute-start | bytes 1572872 | tf_op jit(solution)/shard_map/ppermute | solution.py:20
  92.0 12.3 %collective-permute-start.8 = (bf16[4,256,256]{2,1,0:T(8,128)(2,1)S(1)}, bf16[4,256,256]{2,1,0:T(8,128)(2,1)S(1)}, u32[]{:S(2)}, u32[]{:S(2)}) collective-permute-start(bf16[4,256,256]{2,1,0:T(8,128)(2,1)S(1)} %collective-permute-done.7.refs_0_), channel_id=1, source_target_pairs={{0,1},{1,2},{2,3},{3,4},{4,5},{5,6},{6,7},{7,0},{8,15},{9,8},{10,9... | collective-permute-start | bytes 1572872 | tf_op jit(solution)/shard_map/ppermute | solution.py:20
  97.6 12.3 %collective-permute-start = (bf16[4,256,256]{2,1,0:T(8,128)(2,1)S(1)}, bf16[4,256,256]{2,1,0:T(8,128)(2,1)S(1)}, u32[]{:S(2)}, u32[]{:S(2)}) collective-permute-start(bf16[4,256,256]{2,1,0:T(8,128)(2,1)S(1)} %shard_map.65.refs_0_), channel_id=1, source_target_pairs={{0,1},{1,2},{2,3},{3,4},{4,5},{5,6},{6,7},{7,0},{8,15},{9,8},{10,9... | collective-permute-start | bytes 1572872 | tf_op jit(solution)/shard_map/ppermute | solution.py:20
  104.3 14.1 %collective-permute-start.9 = (bf16[4,256,256]{2,1,0:T(8,128)(2,1)S(1)}, bf16[4,256,256]{2,1,0:T(8,128)(2,1)S(1)}, u32[]{:S(2)}, u32[]{:S(2)}) collective-permute-start(bf16[4,256,256]{2,1,0:T(8,128)(2,1)S(1)} %collective-permute-done.8.refs_1_), channel_id=1, source_target_pairs={{0,1},{1,2},{2,3},{3,4},{4,5},{5,6},{6,7},{7,0},{8,15},{9,8},{10,9... | collective-permute-start | bytes 1572872 | tf_op jit(solution)/shard_map/ppermute | solution.py:20
  109.9 12.3 %collective-permute-start.1 = (bf16[4,256,256]{2,1,0:T(8,128)(2,1)S(1)}, bf16[4,256,256]{2,1,0:T(8,128)(2,1)S(1)}, u32[]{:S(2)}, u32[]{:S(2)}) collective-permute-start(bf16[4,256,256]{2,1,0:T(8,128)(2,1)S(1)} %collective-permute-done.refs_1_), channel_id=1, source_target_pairs={{0,1},{1,2},{2,3},{3,4},{4,5},{5,6},{6,7},{7,0},{8,15},{9,8},{10,9... | collective-permute-start | bytes 1572872 | tf_op jit(solution)/shard_map/ppermute | solution.py:20
  118.4 23.8 %copy-start.2 = (bf16[2,2048,192]{1,2,0:T(8,128)(2,1)S(1)}, bf16[2,2048,192]{1,2,0:T(8,128)(2,1)}, u32[]{:S(2)}) copy-start(bf16[2,2048,192]{1,2,0:T(8,128)(2,1)} %param.10) | copy-start | bytes 4718596
  119.4 27.4 %collective-permute-start.10 = (f32[4,384,256]{2,1,0:T(8,128)S(1)}, f32[4,384,256]{2,1,0:T(8,128)S(1)}, u32[]{:S(2)}, u32[]{:S(2)}) collective-permute-start(f32[4,384,256]{2,1,0:T(8,128)S(1)} %shard_map.68), channel_id=1, source_target_pairs={{0,8},{8,0},{1,9},{9,1},{2,10},{10,2},{3,11},{11,3},{4,12},{12,4},... | collective-permute-start | bytes 4718600 | tf_op jit(solution)/shard_map/ppermute | solution.py:13
  122.2 12.3 %collective-permute-start.2 = (bf16[4,256,256]{2,1,0:T(8,128)(2,1)S(1)}, bf16[4,256,256]{2,1,0:T(8,128)(2,1)S(1)}, u32[]{:S(2)}, u32[]{:S(2)}) collective-permute-start(bf16[4,256,256]{2,1,0:T(8,128)(2,1)S(1)} %collective-permute-done.1.refs_2_), channel_id=1, source_target_pairs={{0,1},{1,2},{2,3},{3,4},{4,5},{5,6},{6,7},{7,0},{8,15},{9,8},{10,9... | collective-permute-start | bytes 1572872 | tf_op jit(solution)/shard_map/ppermute | solution.py:20
  134.5 12.3 %collective-permute-start.3 = (bf16[4,256,256]{2,1,0:T(8,128)(2,1)S(1)}, bf16[4,256,256]{2,1,0:T(8,128)(2,1)S(1)}, u32[]{:S(2)}, u32[]{:S(2)}) collective-permute-start(bf16[4,256,256]{2,1,0:T(8,128)(2,1)S(1)} %collective-permute-done.2.refs_0_), channel_id=1, source_target_pairs={{0,1},{1,2},{2,3},{3,4},{4,5},{5,6},{6,7},{7,0},{8,15},{9,8},{10,9... | collective-permute-start | bytes 1572872 | tf_op jit(solution)/shard_map/ppermute | solution.py:20
  140.2 43.4 %collective-permute-start.15 = (bf16[2,1536,256]{2,1,0:T(8,128)(2,1)S(1)}, bf16[2,1536,256]{2,1,0:T(8,128)(2,1)S(1)}, u32[]{:S(2)}, u32[]{:S(2)}) collective-permute-start(bf16[2,1536,256]{2,1,0:T(8,128)(2,1)S(1)} %copy-done.3), channel_id=1, source_target_pairs={{0,8},{8,0},{1,9},{9,1},{2,10},{10,2},{3,11},{11,3},{4,12},{12,4},... | collective-permute-start | bytes 4718600 | tf_op jit(solution)/shard_map/ppermute | solution.py:13
  148.3 3.6 %collective-permute-start.16 = (bf16[4,192,256]{2,1,0:T(8,128)(2,1)S(1)}, bf16[4,192,256]{2,1,0:T(8,128)(2,1)S(1)}, u32[]{:S(2)}, u32[]{:S(2)}) collective-permute-start(bf16[4,192,256]{2,1,0:T(8,128)(2,1)S(1)} %shard_map.69.refs_0_), channel_id=1, source_target_pairs={{0,8},{8,0},{1,9},{9,1},{2,10},{10,2},{3,11},{11,3},{4,12},{12,4},... | collective-permute-start | bytes 1179656 | tf_op jit(solution)/shard_map/ppermute | solution.py:13
  152.0 10.9 %collective-permute-start.17 = (bf16[4,192,256]{2,1,0:T(8,128)(2,1)S(1)}, bf16[4,192,256]{2,1,0:T(8,128)(2,1)S(1)}, u32[]{:S(2)}, u32[]{:S(2)}) collective-permute-start(bf16[4,192,256]{2,1,0:T(8,128)(2,1)S(1)} %collective-permute-done.16), channel_id=1, source_target_pairs={{0,1},{1,2},{2,3},{3,4},{4,5},{5,6},{6,7},{7,0},{8,15},{9,8},{10,9... | collective-permute-start | bytes 1179656 | tf_op jit(solution)/shard_map/ppermute | solution.py:20
  162.9 10.9 %collective-permute-start.18 = (bf16[4,192,256]{2,1,0:T(8,128)(2,1)S(1)}, bf16[4,192,256]{2,1,0:T(8,128)(2,1)S(1)}, u32[]{:S(2)}, u32[]{:S(2)}) collective-permute-start(bf16[4,192,256]{2,1,0:T(8,128)(2,1)S(1)} %collective-permute-done.17.refs_0_), channel_id=1, source_target_pairs={{0,1},{1,2},{2,3},{3,4},{4,5},{5,6},{6,7},{7,0},{8,15},{9,8},{10,9... | collective-permute-start | bytes 1179656 | tf_op jit(solution)/shard_map/ppermute | solution.py:20
  168.5 10.9 %collective-permute-start.11 = (bf16[4,192,256]{2,1,0:T(8,128)(2,1)S(1)}, bf16[4,192,256]{2,1,0:T(8,128)(2,1)S(1)}, u32[]{:S(2)}, u32[]{:S(2)}) collective-permute-start(bf16[4,192,256]{2,1,0:T(8,128)(2,1)S(1)} %shard_map.69.refs_0_), channel_id=1, source_target_pairs={{0,1},{1,2},{2,3},{3,4},{4,5},{5,6},{6,7},{7,0},{8,15},{9,8},{10,9... | collective-permute-start | bytes 1179656 | tf_op jit(solution)/shard_map/ppermute | solution.py:20
  173.8 10.9 %collective-permute-start.19 = (bf16[4,192,256]{2,1,0:T(8,128)(2,1)S(1)}, bf16[4,192,256]{2,1,0:T(8,128)(2,1)S(1)}, u32[]{:S(2)}, u32[]{:S(2)}) collective-permute-start(bf16[4,192,256]{2,1,0:T(8,128)(2,1)S(1)} %collective-permute-done.18.refs_1_), channel_id=1, source_target_pairs={{0,1},{1,2},{2,3},{3,4},{4,5},{5,6},{6,7},{7,0},{8,15},{9,8},{10,9... | collective-permute-start | bytes 1179656 | tf_op jit(solution)/shard_map/ppermute | solution.py:20
  179.4 9.7 %collective-permute-start.12 = (bf16[4,192,256]{2,1,0:T(8,128)(2,1)S(1)}, bf16[4,192,256]{2,1,0:T(8,128)(2,1)S(1)}, u32[]{:S(2)}, u32[]{:S(2)}) collective-permute-start(bf16[4,192,256]{2,1,0:T(8,128)(2,1)S(1)} %collective-permute-done.11.refs_1_), channel_id=1, source_target_pairs={{0,1},{1,2},{2,3},{3,4},{4,5},{5,6},{6,7},{7,0},{8,15},{9,8},{10,9... | collective-permute-start | bytes 1179656 | tf_op jit(solution)/shard_map/ppermute | solution.py:20
  185.6 25.1 %collective-permute-start.20 = (f32[4,256,256]{2,1,0:T(8,128)S(1)}, f32[4,256,256]{2,1,0:T(8,128)S(1)}, u32[]{:S(2)}, u32[]{:S(2)}) collective-permute-start(f32[4,256,256]{2,1,0:T(8,128)S(1)} %shard_map.72), channel_id=1, source_target_pairs={{0,8},{8,0},{1,9},{9,1},{2,10},{10,2},{3,11},{11,3},{4,12},{12,4},... | collective-permute-start | bytes 3145736 | tf_op jit(solution)/shard_map/ppermute | solution.py:13
  189.1 10.7 %collective-permute-start.13 = (bf16[4,192,256]{2,1,0:T(8,128)(2,1)S(1)}, bf16[4,192,256]{2,1,0:T(8,128)(2,1)S(1)}, u32[]{:S(2)}, u32[]{:S(2)}) collective-permute-start(bf16[4,192,256]{2,1,0:T(8,128)(2,1)S(1)} %collective-permute-done.12.refs_2_), channel_id=1, source_target_pairs={{0,1},{1,2},{2,3},{3,4},{4,5},{5,6},{6,7},{7,0},{8,15},{9,8},{10,9... | collective-permute-start | bytes 1179656 | tf_op jit(solution)/shard_map/ppermute | solution.py:20
  199.8 10.9 %collective-permute-start.14 = (bf16[4,192,256]{2,1,0:T(8,128)(2,1)S(1)}, bf16[4,192,256]{2,1,0:T(8,128)(2,1)S(1)}, u32[]{:S(2)}, u32[]{:S(2)}) collective-permute-start(bf16[4,192,256]{2,1,0:T(8,128)(2,1)S(1)} %collective-permute-done.13.refs_0_), channel_id=1, source_target_pairs={{0,1},{1,2},{2,3},{3,4},{4,5},{5,6},{6,7},{7,0},{8,15},{9,8},{10,9... | collective-permute-start | bytes 1179656 | tf_op jit(solution)/shard_map/ppermute | solution.py:20
  212.5 30.0 %all-to-all-start = ((bf16[16,4,16,256]{3,2,1,0:T(8,128)(2,1)}), bf16[16,4,16,256]{3,2,1,0:T(8,128)(2,1)S(1)}, u32[]{:S(2)}, u32[]{:S(2)}) async-start(bf16[16,4,16,256]{3,2,1,0:T(8,128)(2,1)} %shard_map.73), calls=%async_computation | async-start | bytes 1048576 | tf_op jit(solution)/shard_map/all_to_all | solution.py:239
  (6 other events, 44.9 us)

commit v5 on v4

--- a/solution.py
+++ b/solution.py
@@ -17,6 +17,13 @@
     count = lax.axis_size("dp")
     up = [(i, (i + 1) % count) for i in range(count)]
     down = [(count + i, count + (i - 1) % count) for i in range(count)]
+    return lax.ppermute(block, ("core", "dp"), up + down)
+
+
+def across(block):
+    count = lax.axis_size("dp")
+    up = [(count + i, (i + 1) % count) for i in range(count)]
+    down = [(i, count + (i - 1) % count) for i in range(count)]
     return lax.ppermute(block, ("core", "dp"), up + down)
 
 
@@ -173,12 +180,12 @@
     mine = [own]
     for _ in range(1, half + 1):
         mine.append(onward(mine[-1]))
-    other = [swap(own)]
+    other = []
     for _ in range(1, half):
-        other.append(onward(other[-1]))
+        other.append(onward(other[-1]) if other else across(own))
     early = summed(mine[: half - 1], range(half - 1), (0, 1))
-    ahead = summed(other[1 : half - 1], range(1, half - 1), (1, 0))
-    aside = summed(other[half - 1 :], [half - 1], (1, 0), (ahead,))
+    ahead = summed(other[:-1], range(1, half - 1), (1, 0))
+    aside = summed(other[-1:], [half - 1], (1, 0), (ahead,))
     back = swap(aside)
     return summed(mine[half - 1 :], [half - 1, half], (0, 1), (early, back), finish, out)
 

time: 244 us -> 238 us (0.975)
  the two profiles are of different devices: /device:TPU:86 before, /device:TPU:70 now
where the time goes in v5:
time: 238 us; the launch traced here: 237 us
  starting transfers between devices  77.1 us (32%)
  blocking collectives  71.6 us (30%)
  waiting for transfers between devices  68.8 us (29%)
  Pallas kernels  15.2 us (6%)
  local copies, waits for them, and re-layouts  2.87 us (1%)
    all_gather x1, blocking collectives, layer(): gathered = lax.all_gather(payload, 'z', axis=0)  71.6 us
    ppermute x12, starting transfers between devices, onward(): return lax.ppermute(block, ('core', 'dp'), up + down)  58.8 us
    ppermute x12, waiting for transfers between devices, onward(): return lax.ppermute(block, ('core', 'dp'), up + down)  27.8 us
    all_to_all x1, waiting for transfers between devices, layer(): lax.all_to_all(result, 'z', split_axis=0, concat_axis=0, tiled=True)  25.3 us
    ppermute x2, waiting for transfers between devices, across(): return lax.ppermute(block, ('core', 'dp'), up + down)  15.7 us
    pallas_call x8, Pallas kernels, weighted_sum(): pl.pallas_call(body, in_specs=[pl.BlockSpec(memory_space=pltpu.SMEM)] + [...  14.2 us
    ppermute x5, starting transfers between devices, swap(): return lax.ppermute(block, 'core', [(0, 1), (1, 0)])  10.4 us
  transfers between devices with their start and end apart: 20, of which 10 were waited for; matrix products, arithmetic and copies ran while one was open for 0% of the time, Pallas kernels for 6%

profile of v5, /device:TPU:70, one launch (start us, length us, event | category | flops | bytes accessed | tf_op | source)
XLA Modules:
  0.0 237.5 jit_solution(14347463033324996278)
XLA Ops:
  2.1 2.4 %collective-permute-start.5 = (bf16[2,192,2048]{2,1,0:T(8,128)(2,1)}, bf16[2,192,2048]{2,1,0:T(8,128)(2,1)}, u32[]{:S(2)}, u32[]{:S(2)}) collective-permute-start(bf16[2,192,2048]{2,1,0:T(8,128)(2,1)} %bitcast.16), channel_id=1, source_target_pairs={{0,8},{8,0},{1,9},{9,1},{2,10},{10,2},{3,11},{11,3},{4,12},{12,4},... | collective-permute-start | bytes 4718600 | tf_op jit(solution)/shard_map/ppermute | solution.py:13
  6.0 71.6 %all-gather = bf16[1280,256]{1,0:T(8,128)(2,1)S(1)} all-gather(bf16[80,256]{1,0:T(8,128)(2,1)S(1)} %shard_map.64), channel_id=2, replica_groups=mesh['groups'=2,'z'=16,'core'=2,'dp'=8] {'z'}, dimensions={0}, use_global_device_ids=true | all-gather | bytes 696320 | tf_op jit(solution)/shard_map/all_gather | solution.py:213
  80.5 8.6 %collective-permute-done.6.refs_0_ = bf16[4,256,256]{2,1,0:T(8,128)(2,1)S(1)} collective-permute-done((bf16[4,256,256]{2,1,0:T(8,128)(2,1)S(1)}, bf16[4,256,256]{2,1,0:T(8,128)(2,1)S(1)}, u32[]{:S(2)}, u32[]{:S(2)}) %collective-permute-start.6) | collective-permute-done | bytes 524320 | tf_op jit(solution)/shard_map/ppermute | solution.py:27
  89.1 6.0 %collective-permute-start.7 = (bf16[4,256,256]{2,1,0:T(8,128)(2,1)S(1)}, bf16[4,256,256]{2,1,0:T(8,128)(2,1)S(1)}, u32[]{:S(2)}, u32[]{:S(2)}) collective-permute-start(bf16[4,256,256]{2,1,0:T(8,128)(2,1)S(1)} %collective-permute-done.6.refs_0_), channel_id=1, source_target_pairs={{0,1},{1,2},{2,3},{3,4},{4,5},{5,6},{6,7},{7,0},{8,15},{9,8},{10,9... | collective-permute-start | bytes 1572872 | tf_op jit(solution)/shard_map/ppermute | solution.py:20
  97.0 4.7 %collective-permute-done.7.refs_1_ = bf16[4,256,256]{2,1,0:T(8,128)(2,1)S(1)} collective-permute-done((bf16[4,256,256]{2,1,0:T(8,128)(2,1)S(1)}, bf16[4,256,256]{2,1,0:T(8,128)(2,1)S(1)}, u32[]{:S(2)}, u32[]{:S(2)}) %collective-permute-start.7) | collective-permute-done | bytes 524320 | tf_op jit(solution)/shard_map/ppermute | solution.py:20
  101.8 5.6 %collective-permute-start.8 = (bf16[4,256,256]{2,1,0:T(8,128)(2,1)S(1)}, bf16[4,256,256]{2,1,0:T(8,128)(2,1)S(1)}, u32[]{:S(2)}, u32[]{:S(2)}) collective-permute-start(bf16[4,256,256]{2,1,0:T(8,128)(2,1)S(1)} %collective-permute-done.7.refs_1_), channel_id=1, source_target_pairs={{0,1},{1,2},{2,3},{3,4},{4,5},{5,6},{6,7},{7,0},{8,15},{9,8},{10,9... | collective-permute-start | bytes 1572872 | tf_op jit(solution)/shard_map/ppermute | solution.py:20
  107.4 5.6 %collective-permute-start.1 = (bf16[4,256,256]{2,1,0:T(8,128)(2,1)S(1)}, bf16[4,256,256]{2,1,0:T(8,128)(2,1)S(1)}, u32[]{:S(2)}, u32[]{:S(2)}) collective-permute-start(bf16[4,256,256]{2,1,0:T(8,128)(2,1)S(1)} %collective-permute-done.refs_1_), channel_id=1, source_target_pairs={{0,1},{1,2},{2,3},{3,4},{4,5},{5,6},{6,7},{7,0},{8,15},{9,8},{10,9... | collective-permute-start | bytes 1572872 | tf_op jit(solution)/shard_map/ppermute | solution.py:20
  114.5 2.2 shard_map.67.refs_5_
  120.8 4.5 %collective-permute-start.2 = (bf16[4,256,256]{2,1,0:T(8,128)(2,1)S(1)}, bf16[4,256,256]{2,1,0:T(8,128)(2,1)S(1)}, u32[]{:S(2)}, u32[]{:S(2)}) collective-permute-start(bf16[4,256,256]{2,1,0:T(8,128)(2,1)S(1)} %collective-permute-done.1.refs_2_), channel_id=1, source_target_pairs={{0,1},{1,2},{2,3},{3,4},{4,5},{5,6},{6,7},{7,0},{8,15},{9,8},{10,9... | collective-permute-start | bytes 1572872 | tf_op jit(solution)/shard_map/ppermute | solution.py:20
  125.3 6.7 %collective-permute-done.2.refs_0_ = bf16[4,256,256]{2,1,0:T(8,128)(2,1)S(1)} collective-permute-done((bf16[4,256,256]{2,1,0:T(8,128)(2,1)S(1)}, bf16[4,256,256]{2,1,0:T(8,128)(2,1)S(1)}, u32[]{:S(2)}, u32[]{:S(2)}) %collective-permute-start.2) | collective-permute-done | bytes 524320 | tf_op jit(solution)/shard_map/ppermute | solution.py:20
  132.0 5.6 %collective-permute-start.3 = (bf16[4,256,256]{2,1,0:T(8,128)(2,1)S(1)}, bf16[4,256,256]{2,1,0:T(8,128)(2,1)S(1)}, u32[]{:S(2)}, u32[]{:S(2)}) collective-permute-start(bf16[4,256,256]{2,1,0:T(8,128)(2,1)S(1)} %collective-permute-done.2.refs_0_), channel_id=1, source_target_pairs={{0,1},{1,2},{2,3},{3,4},{4,5},{5,6},{6,7},{7,0},{8,15},{9,8},{10,9... | collective-permute-start | bytes 1572872 | tf_op jit(solution)/shard_map/ppermute | solution.py:20
  139.6 2.6 %shard_map.66.refs_6_ = f32[4,384,256]{2,1,0:T(8,128)S(1)} custom-call(s32[10]{0:T(128)S(1)} %compare_select_fusion.6.table_ref, bf16[4,256,256]{2,1,0:T(8,128)(2,1)S(1)} %shard_map.65.refs_0_, bf16[4,256,256]{2,1,0:T(8,128)(2,1)S(1)} %collective-permute-done.refs_1_, bf16[4,256,256]{2,1,0:T(8,128)(2,1)S(1)} %collective-permute-done.1.refs_2_, ...), custom_call_target="tpu_custom_call" | custom-call | flops 603979776 | bytes 7864320 | tf_op jit(solution)/shard_map/pallas_call | solution.py:165
  144.3 2.4 %shard_map.69.refs_0_ = bf16[4,192,256]{2,1,0:T(8,128)(2,1)S(1)} custom-call(s32[10]{0:T(128)S(1)} %compare_select_fusion.6.table_ref, bf16[4,256,256]{2,1,0:T(8,128)(2,1)S(1)} %collective-permute-done.2.refs_0_, bf16[4,256,256]{2,1,0:T(8,128)(2,1)S(1)} %collective-permute-done.3.refs_1_, bf16[2,192,2048]{2,1,0:T(8,128)(2,1)S(1)} %bitcast.15, ...), custom_call_target="tpu_custom_call" | custom-call | flops 402653184 | bytes 8912896 | tf_op jit(solution)/shard_map/pallas_call | solution.py:165
  148.7 7.2 %collective-permute-done.15.refs_0_ = bf16[4,192,256]{2,1,0:T(8,128)(2,1)S(1)} collective-permute-done((bf16[4,192,256]{2,1,0:T(8,128)(2,1)S(1)}, bf16[4,192,256]{2,1,0:T(8,128)(2,1)S(1)}, u32[]{:S(2)}, u32[]{:S(2)}) %collective-permute-start.15) | collective-permute-done | bytes 393248 | tf_op jit(solution)/shard_map/ppermute | solution.py:27
  155.8 6.8 %collective-permute-start.16 = (bf16[4,192,256]{2,1,0:T(8,128)(2,1)S(1)}, bf16[4,192,256]{2,1,0:T(8,128)(2,1)S(1)}, u32[]{:S(2)}, u32[]{:S(2)}) collective-permute-start(bf16[4,192,256]{2,1,0:T(8,128)(2,1)S(1)} %collective-permute-done.15.refs_0_), channel_id=1, source_target_pairs={{0,1},{1,2},{2,3},{3,4},{4,5},{5,6},{6,7},{7,0},{8,15},{9,8},{10,9... | collective-permute-start | bytes 1179656 | tf_op jit(solution)/shard_map/ppermute | solution.py:20
  164.6 3.3 %collective-permute-done.16.refs_1_ = bf16[4,192,256]{2,1,0:T(8,128)(2,1)S(1)} collective-permute-done((bf16[4,192,256]{2,1,0:T(8,128)(2,1)S(1)}, bf16[4,192,256]{2,1,0:T(8,128)(2,1)S(1)}, u32[]{:S(2)}, u32[]{:S(2)}) %collective-permute-start.16) | collective-permute-done | bytes 393248 | tf_op jit(solution)/shard_map/ppermute | solution.py:20
  167.9 5.6 %collective-permute-start.17 = (bf16[4,192,256]{2,1,0:T(8,128)(2,1)S(1)}, bf16[4,192,256]{2,1,0:T(8,128)(2,1)S(1)}, u32[]{:S(2)}, u32[]{:S(2)}) collective-permute-start(bf16[4,192,256]{2,1,0:T(8,128)(2,1)S(1)} %collective-permute-done.16.refs_1_), channel_id=1, source_target_pairs={{0,1},{1,2},{2,3},{3,4},{4,5},{5,6},{6,7},{7,0},{8,15},{9,8},{10,9... | collective-permute-start | bytes 1179656 | tf_op jit(solution)/shard_map/ppermute | solution.py:20
  173.5 4.2 %collective-permute-start.11 = (bf16[4,192,256]{2,1,0:T(8,128)(2,1)S(1)}, bf16[4,192,256]{2,1,0:T(8,128)(2,1)S(1)}, u32[]{:S(2)}, u32[]{:S(2)}) collective-permute-start(bf16[4,192,256]{2,1,0:T(8,128)(2,1)S(1)} %collective-permute-done.10.refs_1_), channel_id=1, source_target_pairs={{0,1},{1,2},{2,3},{3,4},{4,5},{5,6},{6,7},{7,0},{8,15},{9,8},{10,9... | collective-permute-start | bytes 1179656 | tf_op jit(solution)/shard_map/ppermute | solution.py:20
  183.2 5.4 %collective-permute-start.12 = (bf16[4,192,256]{2,1,0:T(8,128)(2,1)S(1)}, bf16[4,192,256]{2,1,0:T(8,128)(2,1)S(1)}, u32[]{:S(2)}, u32[]{:S(2)}) collective-permute-start(bf16[4,192,256]{2,1,0:T(8,128)(2,1)S(1)} %collective-permute-done.11.refs_2_), channel_id=1, source_target_pairs={{0,1},{1,2},{2,3},{3,4},{4,5},{5,6},{6,7},{7,0},{8,15},{9,8},{10,9... | collective-permute-start | bytes 1179656 | tf_op jit(solution)/shard_map/ppermute | solution.py:20
  188.6 5.3 %collective-permute-done.12.refs_0_ = bf16[4,192,256]{2,1,0:T(8,128)(2,1)S(1)} collective-permute-done((bf16[4,192,256]{2,1,0:T(8,128)(2,1)S(1)}, bf16[4,192,256]{2,1,0:T(8,128)(2,1)S(1)}, u32[]{:S(2)}, u32[]{:S(2)}) %collective-permute-start.12) | collective-permute-done | bytes 393248 | tf_op jit(solution)/shard_map/ppermute | solution.py:20
  193.9 5.6 %collective-permute-start.13 = (bf16[4,192,256]{2,1,0:T(8,128)(2,1)S(1)}, bf16[4,192,256]{2,1,0:T(8,128)(2,1)S(1)}, u32[]{:S(2)}, u32[]{:S(2)}) collective-permute-start(bf16[4,192,256]{2,1,0:T(8,128)(2,1)S(1)} %collective-permute-done.12.refs_0_), channel_id=1, source_target_pairs={{0,1},{1,2},{2,3},{3,4},{4,5},{5,6},{6,7},{7,0},{8,15},{9,8},{10,9... | collective-permute-start | bytes 1179656 | tf_op jit(solution)/shard_map/ppermute | solution.py:20
  200.7 4.1 %collective-permute-done.13.refs_1_ = bf16[4,192,256]{2,1,0:T(8,128)(2,1)S(1)} collective-permute-done((bf16[4,192,256]{2,1,0:T(8,128)(2,1)S(1)}, bf16[4,192,256]{2,1,0:T(8,128)(2,1)S(1)}, u32[]{:S(2)}, u32[]{:S(2)}) %collective-permute-start.13) | collective-permute-done | bytes 393248 | tf_op jit(solution)/shard_map/ppermute | solution.py:20
  206.7 4.0 %all-to-all-start = ((bf16[16,4,16,256]{3,2,1,0:T(8,128)(2,1)}), bf16[16,4,16,256]{3,2,1,0:T(8,128)(2,1)S(1)}, u32[]{:S(2)}, u32[]{:S(2)}) async-start(bf16[16,4,16,256]{3,2,1,0:T(8,128)(2,1)} %shard_map.73), calls=%async_computation | async-start | bytes 1048576 | tf_op jit(solution)/shard_map/all_to_all | solution.py:246
  211.3 25.3 %all-to-all-done = bf16[16,4,16,256]{3,2,1,0:T(8,128)(2,1)S(1)} async-done(((bf16[16,4,16,256]{3,2,1,0:T(8,128)(2,1)}), bf16[16,4,16,256]{3,2,1,0:T(8,128)(2,1)S(1)}, u32[]{:S(2)}, u32[]{:S(2)}) %all-to-all-start) | async-done | bytes 524320 | tf_op jit(solution)/shard_map/all_to_all | solution.py:246
  (51 shorter events, 31.8 us)
Async XLA Ops:
  0.0 113.0 %copy-start = (bf16[2,2048,192]{1,2,0:T(8,128)(2,1)S(1)}, bf16[2,2048,192]{1,2,0:T(8,128)(2,1)}, u32[]{:S(2)}) copy-start(bf16[2,2048,192]{1,2,0:T(8,128)(2,1)} %param.9) | copy-start | bytes 4718596
  0.0 113.0 %collective-permute-start.4 = (bf16[2,192,2048]{2,1,0:T(8,128)(2,1)}, bf16[2,192,2048]{2,1,0:T(8,128)(2,1)S(1)}, u32[]{:S(2)}, u32[]{:S(2)}) collective-permute-start(bf16[2,192,2048]{2,1,0:T(8,128)(2,1)} %bitcast.11), channel_id=1, source_target_pairs={{0,8},{8,0},{1,9},{9,1},{2,10},{10,2},{3,11},{11,3},{4,12},{12,4},... | collective-permute-start | bytes 4718600 | tf_op jit(solution)/shard_map/ppermute | solution.py:13
  2.1 110.9 %collective-permute-start.5 = (bf16[2,192,2048]{2,1,0:T(8,128)(2,1)}, bf16[2,192,2048]{2,1,0:T(8,128)(2,1)}, u32[]{:S(2)}, u32[]{:S(2)}) collective-permute-start(bf16[2,192,2048]{2,1,0:T(8,128)(2,1)} %bitcast.16), channel_id=1, source_target_pairs={{0,8},{8,0},{1,9},{9,1},{2,10},{10,2},{3,11},{11,3},{4,12},{12,4},... | collective-permute-start | bytes 4718600 | tf_op jit(solution)/shard_map/ppermute | solution.py:13
  78.6 10.5 %collective-permute-start.6 = (bf16[4,256,256]{2,1,0:T(8,128)(2,1)S(1)}, bf16[4,256,256]{2,1,0:T(8,128)(2,1)S(1)}, u32[]{:S(2)}, u32[]{:S(2)}) collective-permute-start(bf16[4,256,256]{2,1,0:T(8,128)(2,1)S(1)} %shard_map.65.refs_0_), channel_id=1, source_target_pairs={{8,1},{9,2},{10,3},{11,4},{12,5},{13,6},{14,7},{15,0},{0,15},{1,8}... | collective-permute-start | bytes 1572872 | tf_op jit(solution)/shard_map/ppermute | solution.py:27
  89.1 12.7 %collective-permute-start.7 = (bf16[4,256,256]{2,1,0:T(8,128)(2,1)S(1)}, bf16[4,256,256]{2,1,0:T(8,128)(2,1)S(1)}, u32[]{:S(2)}, u32[]{:S(2)}) collective-permute-start(bf16[4,256,256]{2,1,0:T(8,128)(2,1)S(1)} %collective-permute-done.6.refs_0_), channel_id=1, source_target_pairs={{0,1},{1,2},{2,3},{3,4},{4,5},{5,6},{6,7},{7,0},{8,15},{9,8},{10,9... | collective-permute-start | bytes 1572872 | tf_op jit(solution)/shard_map/ppermute | solution.py:20
  95.1 12.3 %collective-permute-start = (bf16[4,256,256]{2,1,0:T(8,128)(2,1)S(1)}, bf16[4,256,256]{2,1,0:T(8,128)(2,1)S(1)}, u32[]{:S(2)}, u32[]{:S(2)}) collective-permute-start(bf16[4,256,256]{2,1,0:T(8,128)(2,1)S(1)} %shard_map.65.refs_0_), channel_id=1, source_target_pairs={{0,1},{1,2},{2,3},{3,4},{4,5},{5,6},{6,7},{7,0},{8,15},{9,8},{10,9... | collective-permute-start | bytes 1572872 | tf_op jit(solution)/shard_map/ppermute | solution.py:20
  101.8 15.0 %collective-permute-start.8 = (bf16[4,256,256]{2,1,0:T(8,128)(2,1)S(1)}, bf16[4,256,256]{2,1,0:T(8,128)(2,1)S(1)}, u32[]{:S(2)}, u32[]{:S(2)}) collective-permute-start(bf16[4,256,256]{2,1,0:T(8,128)(2,1)S(1)} %collective-permute-done.7.refs_1_), channel_id=1, source_target_pairs={{0,1},{1,2},{2,3},{3,4},{4,5},{5,6},{6,7},{7,0},{8,15},{9,8},{10,9... | collective-permute-start | bytes 1572872 | tf_op jit(solution)/shard_map/ppermute | solution.py:20
  107.4 13.4 %collective-permute-start.1 = (bf16[4,256,256]{2,1,0:T(8,128)(2,1)S(1)}, bf16[4,256,256]{2,1,0:T(8,128)(2,1)S(1)}, u32[]{:S(2)}, u32[]{:S(2)}) collective-permute-start(bf16[4,256,256]{2,1,0:T(8,128)(2,1)S(1)} %collective-permute-done.refs_1_), channel_id=1, source_target_pairs={{0,1},{1,2},{2,3},{3,4},{4,5},{5,6},{6,7},{7,0},{8,15},{9,8},{10,9... | collective-permute-start | bytes 1572872 | tf_op jit(solution)/shard_map/ppermute | solution.py:20
  116.7 20.9 %copy-start.3 = (bf16[2,1536,256]{2,1,0:T(8,128)(2,1)S(1)}, bf16[2,1536,256]{2,1,0:T(8,128)(2,1)}, u32[]{:S(2)}) copy-start(bf16[2,1536,256]{2,1,0:T(8,128)(2,1)} %refs_2_.3) | copy-start | bytes 4718596
  116.7 22.9 %copy-start.2 = (bf16[2,2048,192]{1,2,0:T(8,128)(2,1)S(1)}, bf16[2,2048,192]{1,2,0:T(8,128)(2,1)}, u32[]{:S(2)}) copy-start(bf16[2,2048,192]{1,2,0:T(8,128)(2,1)} %param.10) | copy-start | bytes 4718596
  118.8 25.5 %collective-permute-start.9 = (f32[4,384,256]{2,1,0:T(8,128)S(1)}, f32[4,384,256]{2,1,0:T(8,128)S(1)}, u32[]{:S(2)}, u32[]{:S(2)}) collective-permute-start(f32[4,384,256]{2,1,0:T(8,128)S(1)} %shard_map.68), channel_id=1, source_target_pairs={{0,8},{8,0},{1,9},{9,1},{2,10},{10,2},{3,11},{11,3},{4,12},{12,4},... | collective-permute-start | bytes 4718600 | tf_op jit(solution)/shard_map/ppermute | solution.py:13
  120.8 11.2 %collective-permute-start.2 = (bf16[4,256,256]{2,1,0:T(8,128)(2,1)S(1)}, bf16[4,256,256]{2,1,0:T(8,128)(2,1)S(1)}, u32[]{:S(2)}, u32[]{:S(2)}) collective-permute-start(bf16[4,256,256]{2,1,0:T(8,128)(2,1)S(1)} %collective-permute-done.1.refs_2_), channel_id=1, source_target_pairs={{0,1},{1,2},{2,3},{3,4},{4,5},{5,6},{6,7},{7,0},{8,15},{9,8},{10,9... | collective-permute-start | bytes 1572872 | tf_op jit(solution)/shard_map/ppermute | solution.py:20
  132.0 12.3 %collective-permute-start.3 = (bf16[4,256,256]{2,1,0:T(8,128)(2,1)S(1)}, bf16[4,256,256]{2,1,0:T(8,128)(2,1)S(1)}, u32[]{:S(2)}, u32[]{:S(2)}) collective-permute-start(bf16[4,256,256]{2,1,0:T(8,128)(2,1)S(1)} %collective-permute-done.2.refs_0_), channel_id=1, source_target_pairs={{0,1},{1,2},{2,3},{3,4},{4,5},{5,6},{6,7},{7,0},{8,15},{9,8},{10,9... | collective-permute-start | bytes 1572872 | tf_op jit(solution)/shard_map/ppermute | solution.py:20
  137.6 40.1 %collective-permute-start.14 = (bf16[2,1536,256]{2,1,0:T(8,128)(2,1)S(1)}, bf16[2,1536,256]{2,1,0:T(8,128)(2,1)S(1)}, u32[]{:S(2)}, u32[]{:S(2)}) collective-permute-start(bf16[2,1536,256]{2,1,0:T(8,128)(2,1)S(1)} %copy-done.3), channel_id=1, source_target_pairs={{0,8},{8,0},{1,9},{9,1},{2,10},{10,2},{3,11},{11,3},{4,12},{12,4},... | collective-permute-start | bytes 4718600 | tf_op jit(solution)/shard_map/ppermute | solution.py:13
  146.7 9.1 %collective-permute-start.15 = (bf16[4,192,256]{2,1,0:T(8,128)(2,1)S(1)}, bf16[4,192,256]{2,1,0:T(8,128)(2,1)S(1)}, u32[]{:S(2)}, u32[]{:S(2)}) collective-permute-start(bf16[4,192,256]{2,1,0:T(8,128)(2,1)S(1)} %shard_map.69.refs_0_), channel_id=1, source_target_pairs={{8,1},{9,2},{10,3},{11,4},{12,5},{13,6},{14,7},{15,0},{0,15},{1,8}... | collective-permute-start | bytes 1179656 | tf_op jit(solution)/shard_map/ppermute | solution.py:27
  155.8 12.1 %collective-permute-start.16 = (bf16[4,192,256]{2,1,0:T(8,128)(2,1)S(1)}, bf16[4,192,256]{2,1,0:T(8,128)(2,1)S(1)}, u32[]{:S(2)}, u32[]{:S(2)}) collective-permute-start(bf16[4,192,256]{2,1,0:T(8,128)(2,1)S(1)} %collective-permute-done.15.refs_0_), channel_id=1, source_target_pairs={{0,1},{1,2},{2,3},{3,4},{4,5},{5,6},{6,7},{7,0},{8,15},{9,8},{10,9... | collective-permute-start | bytes 1179656 | tf_op jit(solution)/shard_map/ppermute | solution.py:20
  162.6 10.9 %collective-permute-start.10 = (bf16[4,192,256]{2,1,0:T(8,128)(2,1)S(1)}, bf16[4,192,256]{2,1,0:T(8,128)(2,1)S(1)}, u32[]{:S(2)}, u32[]{:S(2)}) collective-permute-start(bf16[4,192,256]{2,1,0:T(8,128)(2,1)S(1)} %shard_map.69.refs_0_), channel_id=1, source_target_pairs={{0,1},{1,2},{2,3},{3,4},{4,5},{5,6},{6,7},{7,0},{8,15},{9,8},{10,9... | collective-permute-start | bytes 1179656 | tf_op jit(solution)/shard_map/ppermute | solution.py:20
  167.9 10.9 %collective-permute-start.17 = (bf16[4,192,256]{2,1,0:T(8,128)(2,1)S(1)}, bf16[4,192,256]{2,1,0:T(8,128)(2,1)S(1)}, u32[]{:S(2)}, u32[]{:S(2)}) collective-permute-start(bf16[4,192,256]{2,1,0:T(8,128)(2,1)S(1)} %collective-permute-done.16.refs_1_), channel_id=1, source_target_pairs={{0,1},{1,2},{2,3},{3,4},{4,5},{5,6},{6,7},{7,0},{8,15},{9,8},{10,9... | collective-permute-start | bytes 1179656 | tf_op jit(solution)/shard_map/ppermute | solution.py:20
  173.5 9.7 %collective-permute-start.11 = (bf16[4,192,256]{2,1,0:T(8,128)(2,1)S(1)}, bf16[4,192,256]{2,1,0:T(8,128)(2,1)S(1)}, u32[]{:S(2)}, u32[]{:S(2)}) collective-permute-start(bf16[4,192,256]{2,1,0:T(8,128)(2,1)S(1)} %collective-permute-done.10.refs_1_), channel_id=1, source_target_pairs={{0,1},{1,2},{2,3},{3,4},{4,5},{5,6},{6,7},{7,0},{8,15},{9,8},{10,9... | collective-permute-start | bytes 1179656 | tf_op jit(solution)/shard_map/ppermute | solution.py:20
  179.7 25.1 %collective-permute-start.18 = (f32[4,256,256]{2,1,0:T(8,128)S(1)}, f32[4,256,256]{2,1,0:T(8,128)S(1)}, u32[]{:S(2)}, u32[]{:S(2)}) collective-permute-start(f32[4,256,256]{2,1,0:T(8,128)S(1)} %shard_map.72), channel_id=1, source_target_pairs={{0,8},{8,0},{1,9},{9,1},{2,10},{10,2},{3,11},{11,3},{4,12},{12,4},... | collective-permute-start | bytes 3145736 | tf_op jit(solution)/shard_map/ppermute | solution.py:13
  183.2 10.7 %collective-permute-start.12 = (bf16[4,192,256]{2,1,0:T(8,128)(2,1)S(1)}, bf16[4,192,256]{2,1,0:T(8,128)(2,1)S(1)}, u32[]{:S(2)}, u32[]{:S(2)}) collective-permute-start(bf16[4,192,256]{2,1,0:T(8,128)(2,1)S(1)} %collective-permute-done.11.refs_2_), channel_id=1, source_target_pairs={{0,1},{1,2},{2,3},{3,4},{4,5},{5,6},{6,7},{7,0},{8,15},{9,8},{10,9... | collective-permute-start | bytes 1179656 | tf_op jit(solution)/shard_map/ppermute | solution.py:20
  193.9 10.9 %collective-permute-start.13 = (bf16[4,192,256]{2,1,0:T(8,128)(2,1)S(1)}, bf16[4,192,256]{2,1,0:T(8,128)(2,1)S(1)}, u32[]{:S(2)}, u32[]{:S(2)}) collective-permute-start(bf16[4,192,256]{2,1,0:T(8,128)(2,1)S(1)} %collective-permute-done.12.refs_0_), channel_id=1, source_target_pairs={{0,1},{1,2},{2,3},{3,4},{4,5},{5,6},{6,7},{7,0},{8,15},{9,8},{10,9... | collective-permute-start | bytes 1179656 | tf_op jit(solution)/shard_map/ppermute | solution.py:20
  200.7 10.2 %copy-start.7 = (s32[64,8]{0,1:T(8,128)S(1)}, s32[64,8]{0,1:T(8,128)}, u32[]{:S(2)}) copy-start(s32[64,8]{0,1:T(8,128)} %param.8) | copy-start | bytes 6148
  206.7 30.0 %all-to-all-start = ((bf16[16,4,16,256]{3,2,1,0:T(8,128)(2,1)}), bf16[16,4,16,256]{3,2,1,0:T(8,128)(2,1)S(1)}, u32[]{:S(2)}, u32[]{:S(2)}) async-start(bf16[16,4,16,256]{3,2,1,0:T(8,128)(2,1)} %shard_map.73), calls=%async_computation | async-start | bytes 1048576 | tf_op jit(solution)/shard_map/all_to_all | solution.py:246
  (4 other events, 12.8 us)

commit v6 on v5

--- a/solution.py
+++ b/solution.py
@@ -172,7 +172,7 @@
     )(table, *operands)
 
 
-def gather_sum(own, weights, owners, kind, finish, out):
+def gather_sum(own, weights, owners, kind, direct, finish, out):
     half = lax.axis_size("dp") // 2
     summed = lambda parts, steps, order, *rest: weighted_sum(
         parts, steps, weights, owners, kind, order, *rest
@@ -180,9 +180,13 @@
     mine = [own]
     for _ in range(1, half + 1):
         mine.append(onward(mine[-1]))
-    other = []
-    for _ in range(1, half):
-        other.append(onward(other[-1]) if other else across(own))
+    if direct:
+        other = [across(own)]
+    else:
+        paired = swap(own)
+        other = [onward(paired)]
+    for _ in range(2, half):
+        other.append(onward(other[-1]))
     early = summed(mine[: half - 1], range(half - 1), (0, 1))
     ahead = summed(other[:-1], range(1, half - 1), (1, 0))
     aside = summed(other[-1:], [half - 1], (1, 0), (ahead,))
@@ -226,6 +230,7 @@
         pairs[:2],
         table,
         "in",
+        False,
         gated,
         jax.ShapeDtypeStruct((chip_experts, hid, count), jnp.bfloat16),
     )
@@ -240,6 +245,7 @@
         pairs[2:],
         table,
         "out",
+        True,
         returning,
         jax.ShapeDtypeStruct((n_z, chip_experts, capacity, out_features), jnp.bfloat16),
     )

time: 238 us -> 240 us (level)
  the two profiles are of different devices: /device:TPU:70 before, /device:TPU:86 now
where the time goes in v6:
time: 240 us; the launch traced here: 239 us
  starting transfers between devices  82.5 us (34%)
  blocking collectives  71.6 us (30%)
  waiting for transfers between devices  68.7 us (29%)
  Pallas kernels  11.5 us (5%)
  local copies, waits for them, and re-layouts  3 us (1%)
    all_gather x1, blocking collectives, layer(): gathered = lax.all_gather(payload, 'z', axis=0)  71.6 us
    ppermute x13, starting transfers between devices, onward(): return lax.ppermute(block, ('core', 'dp'), up + down)  64.4 us
    ppermute x13, waiting for transfers between devices, onward(): return lax.ppermute(block, ('core', 'dp'), up + down)  36.2 us
    all_to_all x1, waiting for transfers between devices, layer(): lax.all_to_all(result, 'z', split_axis=0, concat_axis=0, tiled=True)  25.3 us
    ppermute x6, starting transfers between devices, swap(): return lax.ppermute(block, 'core', [(0, 1), (1, 0)])  12.2 us
    pallas_call x8, Pallas kernels, weighted_sum(): pl.pallas_call(body, in_specs=[pl.BlockSpec(memory_space=pltpu.SMEM)] + [...  10.5 us
    ppermute x1, waiting for transfers between devices, across(): return lax.ppermute(block, ('core', 'dp'), up + down)  7.17 us
  transfers between devices with their start and end apart: 21, of which 11 were waited for; matrix products, arithmetic and copies ran while one was open for 0% of the time, Pallas kernels for 4%

profile of v6, /device:TPU:86, one launch (start us, length us, event | category | flops | bytes accessed | tf_op | source)
XLA Modules:
  0.0 239.2 jit_solution(10098056011199849849)
XLA Ops:
  1.6 71.6 %all-gather = bf16[1280,256]{1,0:T(8,128)(2,1)S(1)} all-gather(bf16[80,256]{1,0:T(8,128)(2,1)S(1)} %shard_map.64), channel_id=2, replica_groups=mesh['groups'=2,'z'=16,'core'=2,'dp'=8] {'z'}, dimensions={0}, use_global_device_ids=true | all-gather | bytes 696320 | tf_op jit(solution)/shard_map/all_gather | solution.py:217
  76.1 2.4 %collective-permute-start.4 = (bf16[2,192,2048]{2,1,0:T(8,128)(2,1)S(1)}, bf16[2,192,2048]{2,1,0:T(8,128)(2,1)S(1)}, u32[]{:S(2)}, u32[]{:S(2)}) collective-permute-start(bf16[2,192,2048]{2,1,0:T(8,128)(2,1)S(1)} %bitcast.11), channel_id=1, source_target_pairs={{0,8},{8,0},{1,9},{9,1},{2,10},{10,2},{3,11},{11,3},{4,12},{12,4},... | collective-permute-start | bytes 4718600 | tf_op jit(solution)/shard_map/ppermute | solution.py:13
  78.6 2.0 collective-permute-start.5
  80.5 4.8 %collective-permute-start.7 = (bf16[4,256,256]{2,1,0:T(8,128)(2,1)S(1)}, bf16[4,256,256]{2,1,0:T(8,128)(2,1)S(1)}, u32[]{:S(2)}, u32[]{:S(2)}) collective-permute-start(bf16[4,256,256]{2,1,0:T(8,128)(2,1)S(1)} %collective-permute-done.6), channel_id=1, source_target_pairs={{0,1},{1,2},{2,3},{3,4},{4,5},{5,6},{6,7},{7,0},{8,15},{9,8},{10,9... | collective-permute-start | bytes 1572872 | tf_op jit(solution)/shard_map/ppermute | solution.py:20
  85.3 6.7 %collective-permute-done.7.refs_0_ = bf16[4,256,256]{2,1,0:T(8,128)(2,1)S(1)} collective-permute-done((bf16[4,256,256]{2,1,0:T(8,128)(2,1)S(1)}, bf16[4,256,256]{2,1,0:T(8,128)(2,1)S(1)}, u32[]{:S(2)}, u32[]{:S(2)}) %collective-permute-start.7) | collective-permute-done | bytes 524320 | tf_op jit(solution)/shard_map/ppermute | solution.py:20
  92.0 5.6 %collective-permute-start.8 = (bf16[4,256,256]{2,1,0:T(8,128)(2,1)S(1)}, bf16[4,256,256]{2,1,0:T(8,128)(2,1)S(1)}, u32[]{:S(2)}, u32[]{:S(2)}) collective-permute-start(bf16[4,256,256]{2,1,0:T(8,128)(2,1)S(1)} %collective-permute-done.7.refs_0_), channel_id=1, source_target_pairs={{0,1},{1,2},{2,3},{3,4},{4,5},{5,6},{6,7},{7,0},{8,15},{9,8},{10,9... | collective-permute-start | bytes 1572872 | tf_op jit(solution)/shard_map/ppermute | solution.py:20
  99.6 4.7 %collective-permute-done.8.refs_1_ = bf16[4,256,256]{2,1,0:T(8,128)(2,1)S(1)} collective-permute-done((bf16[4,256,256]{2,1,0:T(8,128)(2,1)S(1)}, bf16[4,256,256]{2,1,0:T(8,128)(2,1)S(1)}, u32[]{:S(2)}, u32[]{:S(2)}) %collective-permute-start.8) | collective-permute-done | bytes 524320 | tf_op jit(solution)/shard_map/ppermute | solution.py:20
  104.3 5.6 %collective-permute-start.9 = (bf16[4,256,256]{2,1,0:T(8,128)(2,1)S(1)}, bf16[4,256,256]{2,1,0:T(8,128)(2,1)S(1)}, u32[]{:S(2)}, u32[]{:S(2)}) collective-permute-start(bf16[4,256,256]{2,1,0:T(8,128)(2,1)S(1)} %collective-permute-done.8.refs_1_), channel_id=1, source_target_pairs={{0,1},{1,2},{2,3},{3,4},{4,5},{5,6},{6,7},{7,0},{8,15},{9,8},{10,9... | collective-permute-start | bytes 1572872 | tf_op jit(solution)/shard_map/ppermute | solution.py:20
  109.9 5.6 %collective-permute-start.1 = (bf16[4,256,256]{2,1,0:T(8,128)(2,1)S(1)}, bf16[4,256,256]{2,1,0:T(8,128)(2,1)S(1)}, u32[]{:S(2)}, u32[]{:S(2)}) collective-permute-start(bf16[4,256,256]{2,1,0:T(8,128)(2,1)S(1)} %collective-permute-done.refs_1_), channel_id=1, source_target_pairs={{0,1},{1,2},{2,3},{3,4},{4,5},{5,6},{6,7},{7,0},{8,15},{9,8},{10,9... | collective-permute-start | bytes 1572872 | tf_op jit(solution)/shard_map/ppermute | solution.py:20
  122.2 5.6 %collective-permute-start.2 = (bf16[4,256,256]{2,1,0:T(8,128)(2,1)S(1)}, bf16[4,256,256]{2,1,0:T(8,128)(2,1)S(1)}, u32[]{:S(2)}, u32[]{:S(2)}) collective-permute-start(bf16[4,256,256]{2,1,0:T(8,128)(2,1)S(1)} %collective-permute-done.1.refs_2_), channel_id=1, source_target_pairs={{0,1},{1,2},{2,3},{3,4},{4,5},{5,6},{6,7},{7,0},{8,15},{9,8},{10,9... | collective-permute-start | bytes 1572872 | tf_op jit(solution)/shard_map/ppermute | solution.py:20
  127.9 6.7 %collective-permute-done.2.refs_0_ = bf16[4,256,256]{2,1,0:T(8,128)(2,1)S(1)} collective-permute-done((bf16[4,256,256]{2,1,0:T(8,128)(2,1)S(1)}, bf16[4,256,256]{2,1,0:T(8,128)(2,1)S(1)}, u32[]{:S(2)}, u32[]{:S(2)}) %collective-permute-start.2) | collective-permute-done | bytes 524320 | tf_op jit(solution)/shard_map/ppermute | solution.py:20
  134.5 5.6 %collective-permute-start.3 = (bf16[4,256,256]{2,1,0:T(8,128)(2,1)S(1)}, bf16[4,256,256]{2,1,0:T(8,128)(2,1)S(1)}, u32[]{:S(2)}, u32[]{:S(2)}) collective-permute-start(bf16[4,256,256]{2,1,0:T(8,128)(2,1)S(1)} %collective-permute-done.2.refs_0_), channel_id=1, source_target_pairs={{0,1},{1,2},{2,3},{3,4},{4,5},{5,6},{6,7},{7,0},{8,15},{9,8},{10,9... | collective-permute-start | bytes 1572872 | tf_op jit(solution)/shard_map/ppermute | solution.py:20
  143.9 3.0 %collective-permute-done.3.refs_1_ = bf16[4,256,256]{2,1,0:T(8,128)(2,1)S(1)} collective-permute-done((bf16[4,256,256]{2,1,0:T(8,128)(2,1)S(1)}, bf16[4,256,256]{2,1,0:T(8,128)(2,1)S(1)}, u32[]{:S(2)}, u32[]{:S(2)}) %collective-permute-start.3) | collective-permute-done | bytes 524320 | tf_op jit(solution)/shard_map/ppermute | solution.py:20
  150.3 7.2 %collective-permute-done.16.refs_0_ = bf16[4,192,256]{2,1,0:T(8,128)(2,1)S(1)} collective-permute-done((bf16[4,192,256]{2,1,0:T(8,128)(2,1)S(1)}, bf16[4,192,256]{2,1,0:T(8,128)(2,1)S(1)}, u32[]{:S(2)}, u32[]{:S(2)}) %collective-permute-start.16) | collective-permute-done | bytes 393248 | tf_op jit(solution)/shard_map/ppermute | solution.py:27
  157.5 6.8 %collective-permute-start.17 = (bf16[4,192,256]{2,1,0:T(8,128)(2,1)S(1)}, bf16[4,192,256]{2,1,0:T(8,128)(2,1)S(1)}, u32[]{:S(2)}, u32[]{:S(2)}) collective-permute-start(bf16[4,192,256]{2,1,0:T(8,128)(2,1)S(1)} %collective-permute-done.16.refs_0_), channel_id=1, source_target_pairs={{0,1},{1,2},{2,3},{3,4},{4,5},{5,6},{6,7},{7,0},{8,15},{9,8},{10,9... | collective-permute-start | bytes 1179656 | tf_op jit(solution)/shard_map/ppermute | solution.py:20
  166.2 3.3 %collective-permute-done.17.refs_1_ = bf16[4,192,256]{2,1,0:T(8,128)(2,1)S(1)} collective-permute-done((bf16[4,192,256]{2,1,0:T(8,128)(2,1)S(1)}, bf16[4,192,256]{2,1,0:T(8,128)(2,1)S(1)}, u32[]{:S(2)}, u32[]{:S(2)}) %collective-permute-start.17) | collective-permute-done | bytes 393248 | tf_op jit(solution)/shard_map/ppermute | solution.py:20
  169.6 5.6 %collective-permute-start.18 = (bf16[4,192,256]{2,1,0:T(8,128)(2,1)S(1)}, bf16[4,192,256]{2,1,0:T(8,128)(2,1)S(1)}, u32[]{:S(2)}, u32[]{:S(2)}) collective-permute-start(bf16[4,192,256]{2,1,0:T(8,128)(2,1)S(1)} %collective-permute-done.17.refs_1_), channel_id=1, source_target_pairs={{0,1},{1,2},{2,3},{3,4},{4,5},{5,6},{6,7},{7,0},{8,15},{9,8},{10,9... | collective-permute-start | bytes 1179656 | tf_op jit(solution)/shard_map/ppermute | solution.py:20
  175.2 4.2 %collective-permute-start.12 = (bf16[4,192,256]{2,1,0:T(8,128)(2,1)S(1)}, bf16[4,192,256]{2,1,0:T(8,128)(2,1)S(1)}, u32[]{:S(2)}, u32[]{:S(2)}) collective-permute-start(bf16[4,192,256]{2,1,0:T(8,128)(2,1)S(1)} %collective-permute-done.11.refs_1_), channel_id=1, source_target_pairs={{0,1},{1,2},{2,3},{3,4},{4,5},{5,6},{6,7},{7,0},{8,15},{9,8},{10,9... | collective-permute-start | bytes 1179656 | tf_op jit(solution)/shard_map/ppermute | solution.py:20
  184.9 5.4 %collective-permute-start.13 = (bf16[4,192,256]{2,1,0:T(8,128)(2,1)S(1)}, bf16[4,192,256]{2,1,0:T(8,128)(2,1)S(1)}, u32[]{:S(2)}, u32[]{:S(2)}) collective-permute-start(bf16[4,192,256]{2,1,0:T(8,128)(2,1)S(1)} %collective-permute-done.12.refs_2_), channel_id=1, source_target_pairs={{0,1},{1,2},{2,3},{3,4},{4,5},{5,6},{6,7},{7,0},{8,15},{9,8},{10,9... | collective-permute-start | bytes 1179656 | tf_op jit(solution)/shard_map/ppermute | solution.py:20
  190.3 5.3 %collective-permute-done.13.refs_0_ = bf16[4,192,256]{2,1,0:T(8,128)(2,1)S(1)} collective-permute-done((bf16[4,192,256]{2,1,0:T(8,128)(2,1)S(1)}, bf16[4,192,256]{2,1,0:T(8,128)(2,1)S(1)}, u32[]{:S(2)}, u32[]{:S(2)}) %collective-permute-start.13) | collective-permute-done | bytes 393248 | tf_op jit(solution)/shard_map/ppermute | solution.py:20
  195.6 5.6 %collective-permute-start.14 = (bf16[4,192,256]{2,1,0:T(8,128)(2,1)S(1)}, bf16[4,192,256]{2,1,0:T(8,128)(2,1)S(1)}, u32[]{:S(2)}, u32[]{:S(2)}) collective-permute-start(bf16[4,192,256]{2,1,0:T(8,128)(2,1)S(1)} %collective-permute-done.13.refs_0_), channel_id=1, source_target_pairs={{0,1},{1,2},{2,3},{3,4},{4,5},{5,6},{6,7},{7,0},{8,15},{9,8},{10,9... | collective-permute-start | bytes 1179656 | tf_op jit(solution)/shard_map/ppermute | solution.py:20
  202.4 4.1 %collective-permute-done.14.refs_1_ = bf16[4,192,256]{2,1,0:T(8,128)(2,1)S(1)} collective-permute-done((bf16[4,192,256]{2,1,0:T(8,128)(2,1)S(1)}, bf16[4,192,256]{2,1,0:T(8,128)(2,1)S(1)}, u32[]{:S(2)}, u32[]{:S(2)}) %collective-permute-start.14) | collective-permute-done | bytes 393248 | tf_op jit(solution)/shard_map/ppermute | solution.py:20
  208.3 4.0 %all-to-all-start = ((bf16[16,4,16,256]{3,2,1,0:T(8,128)(2,1)}), bf16[16,4,16,256]{3,2,1,0:T(8,128)(2,1)S(1)}, u32[]{:S(2)}, u32[]{:S(2)}) async-start(bf16[16,4,16,256]{3,2,1,0:T(8,128)(2,1)} %shard_map.73), calls=%async_computation | async-start | bytes 1048576 | tf_op jit(solution)/shard_map/all_to_all | solution.py:252
  213.0 25.3 %all-to-all-done = bf16[16,4,16,256]{3,2,1,0:T(8,128)(2,1)S(1)} async-done(((bf16[16,4,16,256]{3,2,1,0:T(8,128)(2,1)}), bf16[16,4,16,256]{3,2,1,0:T(8,128)(2,1)S(1)}, u32[]{:S(2)}, u32[]{:S(2)}) %all-to-all-start) | async-done | bytes 524320 | tf_op jit(solution)/shard_map/all_to_all | solution.py:252
  (53 shorter events, 32.1 us)
Async XLA Ops:
  0.0 76.1 %copy-start = (bf16[2,2048,192]{1,2,0:T(8,128)(2,1)S(1)}, bf16[2,2048,192]{1,2,0:T(8,128)(2,1)}, u32[]{:S(2)}) copy-start(bf16[2,2048,192]{1,2,0:T(8,128)(2,1)} %param.9) | copy-start | bytes 4718596
  74.2 6.4 %collective-permute-start.6 = (bf16[4,256,256]{2,1,0:T(8,128)(2,1)S(1)}, bf16[4,256,256]{2,1,0:T(8,128)(2,1)S(1)}, u32[]{:S(2)}, u32[]{:S(2)}) collective-permute-start(bf16[4,256,256]{2,1,0:T(8,128)(2,1)S(1)} %shard_map.65.refs_0_), channel_id=1, source_target_pairs={{0,8},{8,0},{1,9},{9,1},{2,10},{10,2},{3,11},{11,3},{4,12},{12,4},... | collective-permute-start | bytes 1572872 | tf_op jit(solution)/shard_map/ppermute | solution.py:13
  76.1 39.4 %collective-permute-start.4 = (bf16[2,192,2048]{2,1,0:T(8,128)(2,1)S(1)}, bf16[2,192,2048]{2,1,0:T(8,128)(2,1)S(1)}, u32[]{:S(2)}, u32[]{:S(2)}) collective-permute-start(bf16[2,192,2048]{2,1,0:T(8,128)(2,1)S(1)} %bitcast.11), channel_id=1, source_target_pairs={{0,8},{8,0},{1,9},{9,1},{2,10},{10,2},{3,11},{11,3},{4,12},{12,4},... | collective-permute-start | bytes 4718600 | tf_op jit(solution)/shard_map/ppermute | solution.py:13
  78.6 37.0 %collective-permute-start.5 = (bf16[2,192,2048]{2,1,0:T(8,128)(2,1)}, bf16[2,192,2048]{2,1,0:T(8,128)(2,1)S(1)}, u32[]{:S(2)}, u32[]{:S(2)}) collective-permute-start(bf16[2,192,2048]{2,1,0:T(8,128)(2,1)} %bitcast.16), channel_id=1, source_target_pairs={{0,8},{8,0},{1,9},{9,1},{2,10},{10,2},{3,11},{11,3},{4,12},{12,4},... | collective-permute-start | bytes 4718600 | tf_op jit(solution)/shard_map/ppermute | solution.py:13
  80.5 11.5 %collective-permute-start.7 = (bf16[4,256,256]{2,1,0:T(8,128)(2,1)S(1)}, bf16[4,256,256]{2,1,0:T(8,128)(2,1)S(1)}, u32[]{:S(2)}, u32[]{:S(2)}) collective-permute-start(bf16[4,256,256]{2,1,0:T(8,128)(2,1)S(1)} %collective-permute-done.6), channel_id=1, source_target_pairs={{0,1},{1,2},{2,3},{3,4},{4,5},{5,6},{6,7},{7,0},{8,15},{9,8},{10,9... | collective-permute-start | bytes 1572872 | tf_op jit(solution)/shard_map/ppermute | solution.py:20
  92.0 12.3 %collective-permute-start.8 = (bf16[4,256,256]{2,1,0:T(8,128)(2,1)S(1)}, bf16[4,256,256]{2,1,0:T(8,128)(2,1)S(1)}, u32[]{:S(2)}, u32[]{:S(2)}) collective-permute-start(bf16[4,256,256]{2,1,0:T(8,128)(2,1)S(1)} %collective-permute-done.7.refs_0_), channel_id=1, source_target_pairs={{0,1},{1,2},{2,3},{3,4},{4,5},{5,6},{6,7},{7,0},{8,15},{9,8},{10,9... | collective-permute-start | bytes 1572872 | tf_op jit(solution)/shard_map/ppermute | solution.py:20
  97.6 12.3 %collective-permute-start = (bf16[4,256,256]{2,1,0:T(8,128)(2,1)S(1)}, bf16[4,256,256]{2,1,0:T(8,128)(2,1)S(1)}, u32[]{:S(2)}, u32[]{:S(2)}) collective-permute-start(bf16[4,256,256]{2,1,0:T(8,128)(2,1)S(1)} %shard_map.65.refs_0_), channel_id=1, source_target_pairs={{0,1},{1,2},{2,3},{3,4},{4,5},{5,6},{6,7},{7,0},{8,15},{9,8},{10,9... | collective-permute-start | bytes 1572872 | tf_op jit(solution)/shard_map/ppermute | solution.py:20
  104.3 14.1 %collective-permute-start.9 = (bf16[4,256,256]{2,1,0:T(8,128)(2,1)S(1)}, bf16[4,256,256]{2,1,0:T(8,128)(2,1)S(1)}, u32[]{:S(2)}, u32[]{:S(2)}) collective-permute-start(bf16[4,256,256]{2,1,0:T(8,128)(2,1)S(1)} %collective-permute-done.8.refs_1_), channel_id=1, source_target_pairs={{0,1},{1,2},{2,3},{3,4},{4,5},{5,6},{6,7},{7,0},{8,15},{9,8},{10,9... | collective-permute-start | bytes 1572872 | tf_op jit(solution)/shard_map/ppermute | solution.py:20
  109.9 12.3 %collective-permute-start.1 = (bf16[4,256,256]{2,1,0:T(8,128)(2,1)S(1)}, bf16[4,256,256]{2,1,0:T(8,128)(2,1)S(1)}, u32[]{:S(2)}, u32[]{:S(2)}) collective-permute-start(bf16[4,256,256]{2,1,0:T(8,128)(2,1)S(1)} %collective-permute-done.refs_1_), channel_id=1, source_target_pairs={{0,1},{1,2},{2,3},{3,4},{4,5},{5,6},{6,7},{7,0},{8,15},{9,8},{10,9... | collective-permute-start | bytes 1572872 | tf_op jit(solution)/shard_map/ppermute | solution.py:20
  118.4 21.8 %copy-start.3 = (bf16[2,1536,256]{2,1,0:T(8,128)(2,1)S(1)}, bf16[2,1536,256]{2,1,0:T(8,128)(2,1)}, u32[]{:S(2)}) copy-start(bf16[2,1536,256]{2,1,0:T(8,128)(2,1)} %refs_2_.3) | copy-start | bytes 4718596
  118.4 23.8 %copy-start.2 = (bf16[2,2048,192]{1,2,0:T(8,128)(2,1)S(1)}, bf16[2,2048,192]{1,2,0:T(8,128)(2,1)}, u32[]{:S(2)}) copy-start(bf16[2,2048,192]{1,2,0:T(8,128)(2,1)} %param.10) | copy-start | bytes 4718596
  119.4 27.4 %collective-permute-start.10 = (f32[4,384,256]{2,1,0:T(8,128)S(1)}, f32[4,384,256]{2,1,0:T(8,128)S(1)}, u32[]{:S(2)}, u32[]{:S(2)}) collective-permute-start(f32[4,384,256]{2,1,0:T(8,128)S(1)} %shard_map.68), channel_id=1, source_target_pairs={{0,8},{8,0},{1,9},{9,1},{2,10},{10,2},{3,11},{11,3},{4,12},{12,4},... | collective-permute-start | bytes 4718600 | tf_op jit(solution)/shard_map/ppermute | solution.py:13
  122.2 12.3 %collective-permute-start.2 = (bf16[4,256,256]{2,1,0:T(8,128)(2,1)S(1)}, bf16[4,256,256]{2,1,0:T(8,128)(2,1)S(1)}, u32[]{:S(2)}, u32[]{:S(2)}) collective-permute-start(bf16[4,256,256]{2,1,0:T(8,128)(2,1)S(1)} %collective-permute-done.1.refs_2_), channel_id=1, source_target_pairs={{0,1},{1,2},{2,3},{3,4},{4,5},{5,6},{6,7},{7,0},{8,15},{9,8},{10,9... | collective-permute-start | bytes 1572872 | tf_op jit(solution)/shard_map/ppermute | solution.py:20
  134.5 12.3 %collective-permute-start.3 = (bf16[4,256,256]{2,1,0:T(8,128)(2,1)S(1)}, bf16[4,256,256]{2,1,0:T(8,128)(2,1)S(1)}, u32[]{:S(2)}, u32[]{:S(2)}) collective-permute-start(bf16[4,256,256]{2,1,0:T(8,128)(2,1)S(1)} %collective-permute-done.2.refs_0_), channel_id=1, source_target_pairs={{0,1},{1,2},{2,3},{3,4},{4,5},{5,6},{6,7},{7,0},{8,15},{9,8},{10,9... | collective-permute-start | bytes 1572872 | tf_op jit(solution)/shard_map/ppermute | solution.py:20
  140.2 39.2 %collective-permute-start.15 = (bf16[2,1536,256]{2,1,0:T(8,128)(2,1)S(1)}, bf16[2,1536,256]{2,1,0:T(8,128)(2,1)S(1)}, u32[]{:S(2)}, u32[]{:S(2)}) collective-permute-start(bf16[2,1536,256]{2,1,0:T(8,128)(2,1)S(1)} %copy-done.3), channel_id=1, source_target_pairs={{0,8},{8,0},{1,9},{9,1},{2,10},{10,2},{3,11},{11,3},{4,12},{12,4},... | collective-permute-start | bytes 4718600 | tf_op jit(solution)/shard_map/ppermute | solution.py:13
  148.3 9.1 %collective-permute-start.16 = (bf16[4,192,256]{2,1,0:T(8,128)(2,1)S(1)}, bf16[4,192,256]{2,1,0:T(8,128)(2,1)S(1)}, u32[]{:S(2)}, u32[]{:S(2)}) collective-permute-start(bf16[4,192,256]{2,1,0:T(8,128)(2,1)S(1)} %shard_map.69.refs_0_), channel_id=1, source_target_pairs={{8,1},{9,2},{10,3},{11,4},{12,5},{13,6},{14,7},{15,0},{0,15},{1,8}... | collective-permute-start | bytes 1179656 | tf_op jit(solution)/shard_map/ppermute | solution.py:27
  157.5 12.1 %collective-permute-start.17 = (bf16[4,192,256]{2,1,0:T(8,128)(2,1)S(1)}, bf16[4,192,256]{2,1,0:T(8,128)(2,1)S(1)}, u32[]{:S(2)}, u32[]{:S(2)}) collective-permute-start(bf16[4,192,256]{2,1,0:T(8,128)(2,1)S(1)} %collective-permute-done.16.refs_0_), channel_id=1, source_target_pairs={{0,1},{1,2},{2,3},{3,4},{4,5},{5,6},{6,7},{7,0},{8,15},{9,8},{10,9... | collective-permute-start | bytes 1179656 | tf_op jit(solution)/shard_map/ppermute | solution.py:20
  164.3 10.9 %collective-permute-start.11 = (bf16[4,192,256]{2,1,0:T(8,128)(2,1)S(1)}, bf16[4,192,256]{2,1,0:T(8,128)(2,1)S(1)}, u32[]{:S(2)}, u32[]{:S(2)}) collective-permute-start(bf16[4,192,256]{2,1,0:T(8,128)(2,1)S(1)} %shard_map.69.refs_0_), channel_id=1, source_target_pairs={{0,1},{1,2},{2,3},{3,4},{4,5},{5,6},{6,7},{7,0},{8,15},{9,8},{10,9... | collective-permute-start | bytes 1179656 | tf_op jit(solution)/shard_map/ppermute | solution.py:20
  169.6 10.9 %collective-permute-start.18 = (bf16[4,192,256]{2,1,0:T(8,128)(2,1)S(1)}, bf16[4,192,256]{2,1,0:T(8,128)(2,1)S(1)}, u32[]{:S(2)}, u32[]{:S(2)}) collective-permute-start(bf16[4,192,256]{2,1,0:T(8,128)(2,1)S(1)} %collective-permute-done.17.refs_1_), channel_id=1, source_target_pairs={{0,1},{1,2},{2,3},{3,4},{4,5},{5,6},{6,7},{7,0},{8,15},{9,8},{10,9... | collective-permute-start | bytes 1179656 | tf_op jit(solution)/shard_map/ppermute | solution.py:20
  175.2 9.7 %collective-permute-start.12 = (bf16[4,192,256]{2,1,0:T(8,128)(2,1)S(1)}, bf16[4,192,256]{2,1,0:T(8,128)(2,1)S(1)}, u32[]{:S(2)}, u32[]{:S(2)}) collective-permute-start(bf16[4,192,256]{2,1,0:T(8,128)(2,1)S(1)} %collective-permute-done.11.refs_1_), channel_id=1, source_target_pairs={{0,1},{1,2},{2,3},{3,4},{4,5},{5,6},{6,7},{7,0},{8,15},{9,8},{10,9... | collective-permute-start | bytes 1179656 | tf_op jit(solution)/shard_map/ppermute | solution.py:20
  181.4 25.1 %collective-permute-start.19 = (f32[4,256,256]{2,1,0:T(8,128)S(1)}, f32[4,256,256]{2,1,0:T(8,128)S(1)}, u32[]{:S(2)}, u32[]{:S(2)}) collective-permute-start(f32[4,256,256]{2,1,0:T(8,128)S(1)} %shard_map.72), channel_id=1, source_target_pairs={{0,8},{8,0},{1,9},{9,1},{2,10},{10,2},{3,11},{11,3},{4,12},{12,4},... | collective-permute-start | bytes 3145736 | tf_op jit(solution)/shard_map/ppermute | solution.py:13
  184.9 10.7 %collective-permute-start.13 = (bf16[4,192,256]{2,1,0:T(8,128)(2,1)S(1)}, bf16[4,192,256]{2,1,0:T(8,128)(2,1)S(1)}, u32[]{:S(2)}, u32[]{:S(2)}) collective-permute-start(bf16[4,192,256]{2,1,0:T(8,128)(2,1)S(1)} %collective-permute-done.12.refs_2_), channel_id=1, source_target_pairs={{0,1},{1,2},{2,3},{3,4},{4,5},{5,6},{6,7},{7,0},{8,15},{9,8},{10,9... | collective-permute-start | bytes 1179656 | tf_op jit(solution)/shard_map/ppermute | solution.py:20
  195.6 10.9 %collective-permute-start.14 = (bf16[4,192,256]{2,1,0:T(8,128)(2,1)S(1)}, bf16[4,192,256]{2,1,0:T(8,128)(2,1)S(1)}, u32[]{:S(2)}, u32[]{:S(2)}) collective-permute-start(bf16[4,192,256]{2,1,0:T(8,128)(2,1)S(1)} %collective-permute-done.13.refs_0_), channel_id=1, source_target_pairs={{0,1},{1,2},{2,3},{3,4},{4,5},{5,6},{6,7},{7,0},{8,15},{9,8},{10,9... | collective-permute-start | bytes 1179656 | tf_op jit(solution)/shard_map/ppermute | solution.py:20
  208.3 30.0 %all-to-all-start = ((bf16[16,4,16,256]{3,2,1,0:T(8,128)(2,1)}), bf16[16,4,16,256]{3,2,1,0:T(8,128)(2,1)S(1)}, u32[]{:S(2)}, u32[]{:S(2)}) async-start(bf16[16,4,16,256]{3,2,1,0:T(8,128)(2,1)} %shard_map.73), calls=%async_computation | async-start | bytes 1048576 | tf_op jit(solution)/shard_map/all_to_all | solution.py:252
  (5 other events, 23.1 us)

commit v7 on v6

--- a/solution.py
+++ b/solution.py
@@ -7,6 +7,7 @@
 
 
 CORES = 2
+Z = ("far", "near")
 
 
 def swap(block):
@@ -57,7 +58,8 @@
 
 
 def chosen_rows(gathered, table, tok_dev, picks, chip_experts, capacity):
-    sources, _, width = gathered.shape
+    near, far, _, width = gathered.shape
+    sources = near * far
     slots = chip_experts * capacity
     end = table.shape[0]
 
@@ -67,7 +69,7 @@
         before = (row < col).astype(jnp.bfloat16)
         lines = []
         for s in range(sources):
-            ids = gathered_ref[s, tok_dev : tok_dev + picks, :tok_dev].astype(jnp.float32)
+            ids = gathered_ref[s % near, s // near, tok_dev : tok_dev + picks, :tok_dev].astype(jnp.float32)
             for e in range(chip_experts):
                 name = table_ref[end - 2] + lax.rem(table_ref[end - 1] + e, chip_experts)
                 same = jnp.where(ids == name.astype(jnp.float32), 1.0, 0.0)
@@ -88,7 +90,7 @@
             ]
             found = lax.dot_general(
                 jnp.concatenate(picked, axis=0).astype(jnp.bfloat16),
-                gathered_ref[s, :tok_dev],
+                gathered_ref[s % near, s // near, :tok_dev],
                 (((1,), (0,)), ((), ())),
                 preferred_element_type=jnp.float32,
             ).astype(jnp.bfloat16)
@@ -199,12 +201,12 @@
     picks = expert_ids.shape[1]
     exp_dev = gate_weight.shape[0]
     hid = gate_weight.shape[2]
-    n_z = lax.axis_size("z")
+    n_z = lax.axis_size(Z)
     chip_experts = exp_dev * CORES
     experts = chip_experts * n_z
     capacity = min(tok_dev, max(2, 2 * tok_dev * picks // experts))
     core = lax.axis_index("core")
-    z = lax.axis_index("z")
+    z = lax.axis_index(Z)
 
     n_dp = lax.axis_size("dp")
     at = jnp.arange(n_dp + 2, dtype=jnp.int32)
@@ -214,7 +216,8 @@
 
     payload = with_ids(tokens, expert_ids.T)
     payload, table = lax.optimization_barrier((payload, table))
-    gathered = lax.all_gather(payload, "z", axis=0)
+    gathered = lax.all_gather(payload, "far", axis=0)
+    gathered = lax.all_gather(gathered, "near", axis=0)
     count = n_z * capacity
     rows = chosen_rows(gathered, table, tok_dev, picks, chip_experts, capacity)
 
@@ -249,7 +252,7 @@
         returning,
         jax.ShapeDtypeStruct((n_z, chip_experts, capacity, out_features), jnp.bfloat16),
     )
-    returned = lax.all_to_all(result, "z", split_axis=0, concat_axis=0, tiled=True)
+    returned = lax.all_to_all(result, Z, split_axis=0, concat_axis=0, tiled=True)
     slot_count = experts * capacity
     returned = returned.reshape(slot_count, out_features)
 
@@ -273,10 +276,13 @@
 
 def solution(mesh):
     groups, expert, dp = (mesh.shape[name] for name in ("groups", "expert", "dp"))
+    chips = expert // CORES
+    near = 4 if chips % 4 == 0 else 1
     split = Mesh(
-        mesh.devices.reshape(groups, expert // CORES, CORES, dp), ("groups", "z", "core", "dp")
-    )
-    rows, held = ("groups", "z", "core"), ("z", "core")
+        mesh.devices.reshape(groups, chips // near, near, CORES, dp),
+        ("groups", *Z, "core", "dp"),
+    )
+    rows, held = ("groups", *Z, "core"), (*Z, "core")
     in_specs = (
         P(rows, "dp"),
         P(rows, None),

time: 240 us -> 244 us (1.017)
  the two profiles are of different devices: /device:TPU:86 before, /device:TPU:70 now
where the time goes in v7:
time: 244 us; the launch traced here: 243 us
  starting transfers between devices  88.7 us (36%)
  blocking collectives  69.9 us (29%)
  waiting for transfers between devices  68.1 us (28%)
  Pallas kernels  11.5 us (5%)
  local copies, waits for them, and re-layouts  3 us (1%)
    ppermute x13, starting transfers between devices, onward(): return lax.ppermute(block, ('core', 'dp'), up + down)  64.4 us
    all_gather x1, blocking collectives, layer(): gathered = lax.all_gather(payload, 'far', axis=0)  49.1 us
    ppermute x13, waiting for transfers between devices, onward(): return lax.ppermute(block, ('core', 'dp'), up + down)  36.2 us
    all_to_all x1, waiting for transfers between devices, layer(): lax.all_to_all(result, Z, split_axis=0, concat_axis=0, tiled=True)  24.8 us
    all_gather x1, blocking collectives, layer(): gathered = lax.all_gather(gathered, 'near', axis=0)  20.8 us
    ppermute x6, starting transfers between devices, swap(): return lax.ppermute(block, 'core', [(0, 1), (1, 0)])  12.2 us
    pallas_call x8, Pallas kernels, weighted_sum(): pl.pallas_call(body, in_specs=[pl.BlockSpec(memory_space=pltpu.SMEM)] + [...  10.5 us
    all_to_all x1, starting transfers between devices, layer(): lax.all_to_all(result, Z, split_axis=0, concat_axis=0, tiled=True)  10.1 us
  transfers between devices with their start and end apart: 21, of which 11 were waited for; matrix products, arithmetic and copies ran while one was open for 0% of the time, Pallas kernels for 4%

profile of v7, /device:TPU:70, one launch (start us, length us, event | category | flops | bytes accessed | tf_op | source)
XLA Modules:
  0.0 243.0 jit_solution(130649772007218140)
XLA Ops:
  1.6 49.1 %all-gather = bf16[320,256]{1,0:T(8,128)(2,1)S(1)} all-gather(bf16[80,256]{1,0:T(8,128)(2,1)S(1)} %shard_map.64), channel_id=2, replica_groups=mesh['groups'=2,'far'=4,'near'=4,'core'=2,'dp'=8] {'far'}, dimensions={0}, use_global_device_ids=true | all-gather | bytes 204800 | tf_op jit(solution)/shard_map/all_gather | solution.py:219
  50.7 20.8 %all-gather.1 = bf16[16,80,256]{2,1,0:T(8,128)(2,1)S(1)} all-gather(bf16[4,80,256]{2,1,0:T(8,128)(2,1)S(1)} %bitcast.28), channel_id=3, replica_groups=mesh['groups'=2,'far'=4,'near'=4,'core'=2,'dp'=8] {'near'}, dimensions={0}, use_global_device_ids=true | all-gather | bytes 819200 | tf_op jit(solution)/shard_map/all_gather | solution.py:220
  74.4 2.4 %collective-permute-start.4 = (bf16[2,192,2048]{2,1,0:T(8,128)(2,1)S(1)}, bf16[2,192,2048]{2,1,0:T(8,128)(2,1)S(1)}, u32[]{:S(2)}, u32[]{:S(2)}) collective-permute-start(bf16[2,192,2048]{2,1,0:T(8,128)(2,1)S(1)} %bitcast.12), channel_id=1, source_target_pairs={{0,8},{8,0},{1,9},{9,1},{2,10},{10,2},{3,11},{11,3},{4,12},{12,4},... | collective-permute-start | bytes 4718600 | tf_op jit(solution)/shard_map/ppermute | solution.py:14
  78.8 4.8 %collective-permute-start.7 = (bf16[4,256,256]{2,1,0:T(8,128)(2,1)S(1)}, bf16[4,256,256]{2,1,0:T(8,128)(2,1)S(1)}, u32[]{:S(2)}, u32[]{:S(2)}) collective-permute-start(bf16[4,256,256]{2,1,0:T(8,128)(2,1)S(1)} %collective-permute-done.6), channel_id=1, source_target_pairs={{0,1},{1,2},{2,3},{3,4},{4,5},{5,6},{6,7},{7,0},{8,15},{9,8},{10,9... | collective-permute-start | bytes 1572872 | tf_op jit(solution)/shard_map/ppermute | solution.py:21
  83.6 6.7 %collective-permute-done.7.refs_0_ = bf16[4,256,256]{2,1,0:T(8,128)(2,1)S(1)} collective-permute-done((bf16[4,256,256]{2,1,0:T(8,128)(2,1)S(1)}, bf16[4,256,256]{2,1,0:T(8,128)(2,1)S(1)}, u32[]{:S(2)}, u32[]{:S(2)}) %collective-permute-start.7) | collective-permute-done | bytes 524320 | tf_op jit(solution)/shard_map/ppermute | solution.py:21
  90.3 5.6 %collective-permute-start.8 = (bf16[4,256,256]{2,1,0:T(8,128)(2,1)S(1)}, bf16[4,256,256]{2,1,0:T(8,128)(2,1)S(1)}, u32[]{:S(2)}, u32[]{:S(2)}) collective-permute-start(bf16[4,256,256]{2,1,0:T(8,128)(2,1)S(1)} %collective-permute-done.7.refs_0_), channel_id=1, source_target_pairs={{0,1},{1,2},{2,3},{3,4},{4,5},{5,6},{6,7},{7,0},{8,15},{9,8},{10,9... | collective-permute-start | bytes 1572872 | tf_op jit(solution)/shard_map/ppermute | solution.py:21
  97.9 4.7 %collective-permute-done.8.refs_1_ = bf16[4,256,256]{2,1,0:T(8,128)(2,1)S(1)} collective-permute-done((bf16[4,256,256]{2,1,0:T(8,128)(2,1)S(1)}, bf16[4,256,256]{2,1,0:T(8,128)(2,1)S(1)}, u32[]{:S(2)}, u32[]{:S(2)}) %collective-permute-start.8) | collective-permute-done | bytes 524320 | tf_op jit(solution)/shard_map/ppermute | solution.py:21
  102.6 5.6 %collective-permute-start.9 = (bf16[4,256,256]{2,1,0:T(8,128)(2,1)S(1)}, bf16[4,256,256]{2,1,0:T(8,128)(2,1)S(1)}, u32[]{:S(2)}, u32[]{:S(2)}) collective-permute-start(bf16[4,256,256]{2,1,0:T(8,128)(2,1)S(1)} %collective-permute-done.8.refs_1_), channel_id=1, source_target_pairs={{0,1},{1,2},{2,3},{3,4},{4,5},{5,6},{6,7},{7,0},{8,15},{9,8},{10,9... | collective-permute-start | bytes 1572872 | tf_op jit(solution)/shard_map/ppermute | solution.py:21
  108.2 5.6 %collective-permute-start.1 = (bf16[4,256,256]{2,1,0:T(8,128)(2,1)S(1)}, bf16[4,256,256]{2,1,0:T(8,128)(2,1)S(1)}, u32[]{:S(2)}, u32[]{:S(2)}) collective-permute-start(bf16[4,256,256]{2,1,0:T(8,128)(2,1)S(1)} %collective-permute-done.refs_1_), channel_id=1, source_target_pairs={{0,1},{1,2},{2,3},{3,4},{4,5},{5,6},{6,7},{7,0},{8,15},{9,8},{10,9... | collective-permute-start | bytes 1572872 | tf_op jit(solution)/shard_map/ppermute | solution.py:21
  120.5 5.6 %collective-permute-start.2 = (bf16[4,256,256]{2,1,0:T(8,128)(2,1)S(1)}, bf16[4,256,256]{2,1,0:T(8,128)(2,1)S(1)}, u32[]{:S(2)}, u32[]{:S(2)}) collective-permute-start(bf16[4,256,256]{2,1,0:T(8,128)(2,1)S(1)} %collective-permute-done.1.refs_2_), channel_id=1, source_target_pairs={{0,1},{1,2},{2,3},{3,4},{4,5},{5,6},{6,7},{7,0},{8,15},{9,8},{10,9... | collective-permute-start | bytes 1572872 | tf_op jit(solution)/shard_map/ppermute | solution.py:21
  126.1 6.7 %collective-permute-done.2.refs_0_ = bf16[4,256,256]{2,1,0:T(8,128)(2,1)S(1)} collective-permute-done((bf16[4,256,256]{2,1,0:T(8,128)(2,1)S(1)}, bf16[4,256,256]{2,1,0:T(8,128)(2,1)S(1)}, u32[]{:S(2)}, u32[]{:S(2)}) %collective-permute-start.2) | collective-permute-done | bytes 524320 | tf_op jit(solution)/shard_map/ppermute | solution.py:21
  132.8 5.6 %collective-permute-start.3 = (bf16[4,256,256]{2,1,0:T(8,128)(2,1)S(1)}, bf16[4,256,256]{2,1,0:T(8,128)(2,1)S(1)}, u32[]{:S(2)}, u32[]{:S(2)}) collective-permute-start(bf16[4,256,256]{2,1,0:T(8,128)(2,1)S(1)} %collective-permute-done.2.refs_0_), channel_id=1, source_target_pairs={{0,1},{1,2},{2,3},{3,4},{4,5},{5,6},{6,7},{7,0},{8,15},{9,8},{10,9... | collective-permute-start | bytes 1572872 | tf_op jit(solution)/shard_map/ppermute | solution.py:21
  142.1 3.0 %collective-permute-done.3.refs_1_ = bf16[4,256,256]{2,1,0:T(8,128)(2,1)S(1)} collective-permute-done((bf16[4,256,256]{2,1,0:T(8,128)(2,1)S(1)}, bf16[4,256,256]{2,1,0:T(8,128)(2,1)S(1)}, u32[]{:S(2)}, u32[]{:S(2)}) %collective-permute-start.3) | collective-permute-done | bytes 524320 | tf_op jit(solution)/shard_map/ppermute | solution.py:21
  148.6 7.2 %collective-permute-done.16.refs_0_ = bf16[4,192,256]{2,1,0:T(8,128)(2,1)S(1)} collective-permute-done((bf16[4,192,256]{2,1,0:T(8,128)(2,1)S(1)}, bf16[4,192,256]{2,1,0:T(8,128)(2,1)S(1)}, u32[]{:S(2)}, u32[]{:S(2)}) %collective-permute-start.16) | collective-permute-done | bytes 393248 | tf_op jit(solution)/shard_map/ppermute | solution.py:28
  155.8 6.8 %collective-permute-start.17 = (bf16[4,192,256]{2,1,0:T(8,128)(2,1)S(1)}, bf16[4,192,256]{2,1,0:T(8,128)(2,1)S(1)}, u32[]{:S(2)}, u32[]{:S(2)}) collective-permute-start(bf16[4,192,256]{2,1,0:T(8,128)(2,1)S(1)} %collective-permute-done.16.refs_0_), channel_id=1, source_target_pairs={{0,1},{1,2},{2,3},{3,4},{4,5},{5,6},{6,7},{7,0},{8,15},{9,8},{10,9... | collective-permute-start | bytes 1179656 | tf_op jit(solution)/shard_map/ppermute | solution.py:21
  164.5 3.3 %collective-permute-done.17.refs_1_ = bf16[4,192,256]{2,1,0:T(8,128)(2,1)S(1)} collective-permute-done((bf16[4,192,256]{2,1,0:T(8,128)(2,1)S(1)}, bf16[4,192,256]{2,1,0:T(8,128)(2,1)S(1)}, u32[]{:S(2)}, u32[]{:S(2)}) %collective-permute-start.17) | collective-permute-done | bytes 393248 | tf_op jit(solution)/shard_map/ppermute | solution.py:21
  167.8 5.6 %collective-permute-start.18 = (bf16[4,192,256]{2,1,0:T(8,128)(2,1)S(1)}, bf16[4,192,256]{2,1,0:T(8,128)(2,1)S(1)}, u32[]{:S(2)}, u32[]{:S(2)}) collective-permute-start(bf16[4,192,256]{2,1,0:T(8,128)(2,1)S(1)} %collective-permute-done.17.refs_1_), channel_id=1, source_target_pairs={{0,1},{1,2},{2,3},{3,4},{4,5},{5,6},{6,7},{7,0},{8,15},{9,8},{10,9... | collective-permute-start | bytes 1179656 | tf_op jit(solution)/shard_map/ppermute | solution.py:21
  173.5 4.2 %collective-permute-start.12 = (bf16[4,192,256]{2,1,0:T(8,128)(2,1)S(1)}, bf16[4,192,256]{2,1,0:T(8,128)(2,1)S(1)}, u32[]{:S(2)}, u32[]{:S(2)}) collective-permute-start(bf16[4,192,256]{2,1,0:T(8,128)(2,1)S(1)} %collective-permute-done.11.refs_1_), channel_id=1, source_target_pairs={{0,1},{1,2},{2,3},{3,4},{4,5},{5,6},{6,7},{7,0},{8,15},{9,8},{10,9... | collective-permute-start | bytes 1179656 | tf_op jit(solution)/shard_map/ppermute | solution.py:21
  183.2 5.4 %collective-permute-start.13 = (bf16[4,192,256]{2,1,0:T(8,128)(2,1)S(1)}, bf16[4,192,256]{2,1,0:T(8,128)(2,1)S(1)}, u32[]{:S(2)}, u32[]{:S(2)}) collective-permute-start(bf16[4,192,256]{2,1,0:T(8,128)(2,1)S(1)} %collective-permute-done.12.refs_2_), channel_id=1, source_target_pairs={{0,1},{1,2},{2,3},{3,4},{4,5},{5,6},{6,7},{7,0},{8,15},{9,8},{10,9... | collective-permute-start | bytes 1179656 | tf_op jit(solution)/shard_map/ppermute | solution.py:21
  188.6 5.3 %collective-permute-done.13.refs_0_ = bf16[4,192,256]{2,1,0:T(8,128)(2,1)S(1)} collective-permute-done((bf16[4,192,256]{2,1,0:T(8,128)(2,1)S(1)}, bf16[4,192,256]{2,1,0:T(8,128)(2,1)S(1)}, u32[]{:S(2)}, u32[]{:S(2)}) %collective-permute-start.13) | collective-permute-done | bytes 393248 | tf_op jit(solution)/shard_map/ppermute | solution.py:21
  193.9 5.6 %collective-permute-start.14 = (bf16[4,192,256]{2,1,0:T(8,128)(2,1)S(1)}, bf16[4,192,256]{2,1,0:T(8,128)(2,1)S(1)}, u32[]{:S(2)}, u32[]{:S(2)}) collective-permute-start(bf16[4,192,256]{2,1,0:T(8,128)(2,1)S(1)} %collective-permute-done.13.refs_0_), channel_id=1, source_target_pairs={{0,1},{1,2},{2,3},{3,4},{4,5},{5,6},{6,7},{7,0},{8,15},{9,8},{10,9... | collective-permute-start | bytes 1179656 | tf_op jit(solution)/shard_map/ppermute | solution.py:21
  200.7 4.1 %collective-permute-done.14.refs_1_ = bf16[4,192,256]{2,1,0:T(8,128)(2,1)S(1)} collective-permute-done((bf16[4,192,256]{2,1,0:T(8,128)(2,1)S(1)}, bf16[4,192,256]{2,1,0:T(8,128)(2,1)S(1)}, u32[]{:S(2)}, u32[]{:S(2)}) %collective-permute-start.14) | collective-permute-done | bytes 393248 | tf_op jit(solution)/shard_map/ppermute | solution.py:21
  206.6 10.1 %all-to-all-start = ((bf16[16,4,16,256]{3,2,1,0:T(8,128)(2,1)}), bf16[16,4,16,256]{3,2,1,0:T(8,128)(2,1)S(1)}, u32[]{:S(2)}, u32[]{:S(2)}) async-start(bf16[16,4,16,256]{3,2,1,0:T(8,128)(2,1)} %shard_map.73), calls=%async_computation | async-start | bytes 1048576 | tf_op jit(solution)/shard_map/all_to_all | solution.py:255
  217.4 24.8 %all-to-all-done = bf16[16,4,16,256]{3,2,1,0:T(8,128)(2,1)S(1)} async-done(((bf16[16,4,16,256]{3,2,1,0:T(8,128)(2,1)}), bf16[16,4,16,256]{3,2,1,0:T(8,128)(2,1)S(1)}, u32[]{:S(2)}, u32[]{:S(2)}) %all-to-all-start) | async-done | bytes 524320 | tf_op jit(solution)/shard_map/all_to_all | solution.py:255
  (54 shorter events, 34.1 us)
Async XLA Ops:
  0.0 74.4 %copy-start = (bf16[2,2048,192]{1,2,0:T(8,128)(2,1)S(1)}, bf16[2,2048,192]{1,2,0:T(8,128)(2,1)}, u32[]{:S(2)}) copy-start(bf16[2,2048,192]{1,2,0:T(8,128)(2,1)} %param.9) | copy-start | bytes 4718596
  72.4 6.4 %collective-permute-start.6 = (bf16[4,256,256]{2,1,0:T(8,128)(2,1)S(1)}, bf16[4,256,256]{2,1,0:T(8,128)(2,1)S(1)}, u32[]{:S(2)}, u32[]{:S(2)}) collective-permute-start(bf16[4,256,256]{2,1,0:T(8,128)(2,1)S(1)} %shard_map.65.refs_0_), channel_id=1, source_target_pairs={{0,8},{8,0},{1,9},{9,1},{2,10},{10,2},{3,11},{11,3},{4,12},{12,4},... | collective-permute-start | bytes 1572872 | tf_op jit(solution)/shard_map/ppermute | solution.py:14
  74.4 39.4 %collective-permute-start.4 = (bf16[2,192,2048]{2,1,0:T(8,128)(2,1)S(1)}, bf16[2,192,2048]{2,1,0:T(8,128)(2,1)S(1)}, u32[]{:S(2)}, u32[]{:S(2)}) collective-permute-start(bf16[2,192,2048]{2,1,0:T(8,128)(2,1)S(1)} %bitcast.12), channel_id=1, source_target_pairs={{0,8},{8,0},{1,9},{9,1},{2,10},{10,2},{3,11},{11,3},{4,12},{12,4},... | collective-permute-start | bytes 4718600 | tf_op jit(solution)/shard_map/ppermute | solution.py:14
  76.9 37.0 %collective-permute-start.5 = (bf16[2,192,2048]{2,1,0:T(8,128)(2,1)}, bf16[2,192,2048]{2,1,0:T(8,128)(2,1)S(1)}, u32[]{:S(2)}, u32[]{:S(2)}) collective-permute-start(bf16[2,192,2048]{2,1,0:T(8,128)(2,1)} %bitcast.17), channel_id=1, source_target_pairs={{0,8},{8,0},{1,9},{9,1},{2,10},{10,2},{3,11},{11,3},{4,12},{12,4},... | collective-permute-start | bytes 4718600 | tf_op jit(solution)/shard_map/ppermute | solution.py:14
  78.8 11.5 %collective-permute-start.7 = (bf16[4,256,256]{2,1,0:T(8,128)(2,1)S(1)}, bf16[4,256,256]{2,1,0:T(8,128)(2,1)S(1)}, u32[]{:S(2)}, u32[]{:S(2)}) collective-permute-start(bf16[4,256,256]{2,1,0:T(8,128)(2,1)S(1)} %collective-permute-done.6), channel_id=1, source_target_pairs={{0,1},{1,2},{2,3},{3,4},{4,5},{5,6},{6,7},{7,0},{8,15},{9,8},{10,9... | collective-permute-start | bytes 1572872 | tf_op jit(solution)/shard_map/ppermute | solution.py:21
  90.3 12.3 %collective-permute-start.8 = (bf16[4,256,256]{2,1,0:T(8,128)(2,1)S(1)}, bf16[4,256,256]{2,1,0:T(8,128)(2,1)S(1)}, u32[]{:S(2)}, u32[]{:S(2)}) collective-permute-start(bf16[4,256,256]{2,1,0:T(8,128)(2,1)S(1)} %collective-permute-done.7.refs_0_), channel_id=1, source_target_pairs={{0,1},{1,2},{2,3},{3,4},{4,5},{5,6},{6,7},{7,0},{8,15},{9,8},{10,9... | collective-permute-start | bytes 1572872 | tf_op jit(solution)/shard_map/ppermute | solution.py:21
  95.9 12.3 %collective-permute-start = (bf16[4,256,256]{2,1,0:T(8,128)(2,1)S(1)}, bf16[4,256,256]{2,1,0:T(8,128)(2,1)S(1)}, u32[]{:S(2)}, u32[]{:S(2)}) collective-permute-start(bf16[4,256,256]{2,1,0:T(8,128)(2,1)S(1)} %shard_map.65.refs_0_), channel_id=1, source_target_pairs={{0,1},{1,2},{2,3},{3,4},{4,5},{5,6},{6,7},{7,0},{8,15},{9,8},{10,9... | collective-permute-start | bytes 1572872 | tf_op jit(solution)/shard_map/ppermute | solution.py:21
  102.6 14.1 %collective-permute-start.9 = (bf16[4,256,256]{2,1,0:T(8,128)(2,1)S(1)}, bf16[4,256,256]{2,1,0:T(8,128)(2,1)S(1)}, u32[]{:S(2)}, u32[]{:S(2)}) collective-permute-start(bf16[4,256,256]{2,1,0:T(8,128)(2,1)S(1)} %collective-permute-done.8.refs_1_), channel_id=1, source_target_pairs={{0,1},{1,2},{2,3},{3,4},{4,5},{5,6},{6,7},{7,0},{8,15},{9,8},{10,9... | collective-permute-start | bytes 1572872 | tf_op jit(solution)/shard_map/ppermute | solution.py:21
  108.2 12.3 %collective-permute-start.1 = (bf16[4,256,256]{2,1,0:T(8,128)(2,1)S(1)}, bf16[4,256,256]{2,1,0:T(8,128)(2,1)S(1)}, u32[]{:S(2)}, u32[]{:S(2)}) collective-permute-start(bf16[4,256,256]{2,1,0:T(8,128)(2,1)S(1)} %collective-permute-done.refs_1_), channel_id=1, source_target_pairs={{0,1},{1,2},{2,3},{3,4},{4,5},{5,6},{6,7},{7,0},{8,15},{9,8},{10,9... | collective-permute-start | bytes 1572872 | tf_op jit(solution)/shard_map/ppermute | solution.py:21
  116.6 21.8 %copy-start.3 = (bf16[2,1536,256]{2,1,0:T(8,128)(2,1)S(1)}, bf16[2,1536,256]{2,1,0:T(8,128)(2,1)}, u32[]{:S(2)}) copy-start(bf16[2,1536,256]{2,1,0:T(8,128)(2,1)} %refs_2_.3) | copy-start | bytes 4718596
  116.7 23.8 %copy-start.2 = (bf16[2,2048,192]{1,2,0:T(8,128)(2,1)S(1)}, bf16[2,2048,192]{1,2,0:T(8,128)(2,1)}, u32[]{:S(2)}) copy-start(bf16[2,2048,192]{1,2,0:T(8,128)(2,1)} %param.10) | copy-start | bytes 4718596
  117.7 27.4 %collective-permute-start.10 = (f32[4,384,256]{2,1,0:T(8,128)S(1)}, f32[4,384,256]{2,1,0:T(8,128)S(1)}, u32[]{:S(2)}, u32[]{:S(2)}) collective-permute-start(f32[4,384,256]{2,1,0:T(8,128)S(1)} %shard_map.68), channel_id=1, source_target_pairs={{0,8},{8,0},{1,9},{9,1},{2,10},{10,2},{3,11},{11,3},{4,12},{12,4},... | collective-permute-start | bytes 4718600 | tf_op jit(solution)/shard_map/ppermute | solution.py:14
  120.5 12.3 %collective-permute-start.2 = (bf16[4,256,256]{2,1,0:T(8,128)(2,1)S(1)}, bf16[4,256,256]{2,1,0:T(8,128)(2,1)S(1)}, u32[]{:S(2)}, u32[]{:S(2)}) collective-permute-start(bf16[4,256,256]{2,1,0:T(8,128)(2,1)S(1)} %collective-permute-done.1.refs_2_), channel_id=1, source_target_pairs={{0,1},{1,2},{2,3},{3,4},{4,5},{5,6},{6,7},{7,0},{8,15},{9,8},{10,9... | collective-permute-start | bytes 1572872 | tf_op jit(solution)/shard_map/ppermute | solution.py:21
  132.8 12.3 %collective-permute-start.3 = (bf16[4,256,256]{2,1,0:T(8,128)(2,1)S(1)}, bf16[4,256,256]{2,1,0:T(8,128)(2,1)S(1)}, u32[]{:S(2)}, u32[]{:S(2)}) collective-permute-start(bf16[4,256,256]{2,1,0:T(8,128)(2,1)S(1)} %collective-permute-done.2.refs_0_), channel_id=1, source_target_pairs={{0,1},{1,2},{2,3},{3,4},{4,5},{5,6},{6,7},{7,0},{8,15},{9,8},{10,9... | collective-permute-start | bytes 1572872 | tf_op jit(solution)/shard_map/ppermute | solution.py:21
  138.5 39.2 %collective-permute-start.15 = (bf16[2,1536,256]{2,1,0:T(8,128)(2,1)S(1)}, bf16[2,1536,256]{2,1,0:T(8,128)(2,1)S(1)}, u32[]{:S(2)}, u32[]{:S(2)}) collective-permute-start(bf16[2,1536,256]{2,1,0:T(8,128)(2,1)S(1)} %copy-done.3), channel_id=1, source_target_pairs={{0,8},{8,0},{1,9},{9,1},{2,10},{10,2},{3,11},{11,3},{4,12},{12,4},... | collective-permute-start | bytes 4718600 | tf_op jit(solution)/shard_map/ppermute | solution.py:14
  146.6 9.1 %collective-permute-start.16 = (bf16[4,192,256]{2,1,0:T(8,128)(2,1)S(1)}, bf16[4,192,256]{2,1,0:T(8,128)(2,1)S(1)}, u32[]{:S(2)}, u32[]{:S(2)}) collective-permute-start(bf16[4,192,256]{2,1,0:T(8,128)(2,1)S(1)} %shard_map.69.refs_0_), channel_id=1, source_target_pairs={{8,1},{9,2},{10,3},{11,4},{12,5},{13,6},{14,7},{15,0},{0,15},{1,8}... | collective-permute-start | bytes 1179656 | tf_op jit(solution)/shard_map/ppermute | solution.py:28
  155.8 12.1 %collective-permute-start.17 = (bf16[4,192,256]{2,1,0:T(8,128)(2,1)S(1)}, bf16[4,192,256]{2,1,0:T(8,128)(2,1)S(1)}, u32[]{:S(2)}, u32[]{:S(2)}) collective-permute-start(bf16[4,192,256]{2,1,0:T(8,128)(2,1)S(1)} %collective-permute-done.16.refs_0_), channel_id=1, source_target_pairs={{0,1},{1,2},{2,3},{3,4},{4,5},{5,6},{6,7},{7,0},{8,15},{9,8},{10,9... | collective-permute-start | bytes 1179656 | tf_op jit(solution)/shard_map/ppermute | solution.py:21
  162.6 10.9 %collective-permute-start.11 = (bf16[4,192,256]{2,1,0:T(8,128)(2,1)S(1)}, bf16[4,192,256]{2,1,0:T(8,128)(2,1)S(1)}, u32[]{:S(2)}, u32[]{:S(2)}) collective-permute-start(bf16[4,192,256]{2,1,0:T(8,128)(2,1)S(1)} %shard_map.69.refs_0_), channel_id=1, source_target_pairs={{0,1},{1,2},{2,3},{3,4},{4,5},{5,6},{6,7},{7,0},{8,15},{9,8},{10,9... | collective-permute-start | bytes 1179656 | tf_op jit(solution)/shard_map/ppermute | solution.py:21
  167.8 10.9 %collective-permute-start.18 = (bf16[4,192,256]{2,1,0:T(8,128)(2,1)S(1)}, bf16[4,192,256]{2,1,0:T(8,128)(2,1)S(1)}, u32[]{:S(2)}, u32[]{:S(2)}) collective-permute-start(bf16[4,192,256]{2,1,0:T(8,128)(2,1)S(1)} %collective-permute-done.17.refs_1_), channel_id=1, source_target_pairs={{0,1},{1,2},{2,3},{3,4},{4,5},{5,6},{6,7},{7,0},{8,15},{9,8},{10,9... | collective-permute-start | bytes 1179656 | tf_op jit(solution)/shard_map/ppermute | solution.py:21
  173.5 9.7 %collective-permute-start.12 = (bf16[4,192,256]{2,1,0:T(8,128)(2,1)S(1)}, bf16[4,192,256]{2,1,0:T(8,128)(2,1)S(1)}, u32[]{:S(2)}, u32[]{:S(2)}) collective-permute-start(bf16[4,192,256]{2,1,0:T(8,128)(2,1)S(1)} %collective-permute-done.11.refs_1_), channel_id=1, source_target_pairs={{0,1},{1,2},{2,3},{3,4},{4,5},{5,6},{6,7},{7,0},{8,15},{9,8},{10,9... | collective-permute-start | bytes 1179656 | tf_op jit(solution)/shard_map/ppermute | solution.py:21
  179.6 25.1 %collective-permute-start.19 = (f32[4,256,256]{2,1,0:T(8,128)S(1)}, f32[4,256,256]{2,1,0:T(8,128)S(1)}, u32[]{:S(2)}, u32[]{:S(2)}) collective-permute-start(f32[4,256,256]{2,1,0:T(8,128)S(1)} %shard_map.72), channel_id=1, source_target_pairs={{0,8},{8,0},{1,9},{9,1},{2,10},{10,2},{3,11},{11,3},{4,12},{12,4},... | collective-permute-start | bytes 3145736 | tf_op jit(solution)/shard_map/ppermute | solution.py:14
  183.2 10.7 %collective-permute-start.13 = (bf16[4,192,256]{2,1,0:T(8,128)(2,1)S(1)}, bf16[4,192,256]{2,1,0:T(8,128)(2,1)S(1)}, u32[]{:S(2)}, u32[]{:S(2)}) collective-permute-start(bf16[4,192,256]{2,1,0:T(8,128)(2,1)S(1)} %collective-permute-done.12.refs_2_), channel_id=1, source_target_pairs={{0,1},{1,2},{2,3},{3,4},{4,5},{5,6},{6,7},{7,0},{8,15},{9,8},{10,9... | collective-permute-start | bytes 1179656 | tf_op jit(solution)/shard_map/ppermute | solution.py:21
  193.9 10.9 %collective-permute-start.14 = (bf16[4,192,256]{2,1,0:T(8,128)(2,1)S(1)}, bf16[4,192,256]{2,1,0:T(8,128)(2,1)S(1)}, u32[]{:S(2)}, u32[]{:S(2)}) collective-permute-start(bf16[4,192,256]{2,1,0:T(8,128)(2,1)S(1)} %collective-permute-done.13.refs_0_), channel_id=1, source_target_pairs={{0,1},{1,2},{2,3},{3,4},{4,5},{5,6},{6,7},{7,0},{8,15},{9,8},{10,9... | collective-permute-start | bytes 1179656 | tf_op jit(solution)/shard_map/ppermute | solution.py:21
  206.6 35.6 %all-to-all-start = ((bf16[16,4,16,256]{3,2,1,0:T(8,128)(2,1)}), bf16[16,4,16,256]{3,2,1,0:T(8,128)(2,1)S(1)}, u32[]{:S(2)}, u32[]{:S(2)}) async-start(bf16[16,4,16,256]{3,2,1,0:T(8,128)(2,1)} %shard_map.73), calls=%async_computation | async-start | bytes 1048576 | tf_op jit(solution)/shard_map/all_to_all | solution.py:255
  (5 other events, 35.3 us)

commit v8 on v6

--- a/solution.py
+++ b/solution.py
@@ -41,18 +41,30 @@
     tok_dev, width = tokens.shape
     picks = ids.shape[0]
 
-    def body(tokens_ref, ids_ref, out_ref):
-        out_ref[:tok_dev] = tokens_ref[...]
-        found = ids_ref[...].astype(jnp.float32)
+    def body(tokens_ref, ids_ref, out_ref, held_ref, sems):
+        ids_copy = pltpu.make_async_copy(ids_ref, held_ref, sems.at[0])
+        tokens_copy = pltpu.make_async_copy(tokens_ref, out_ref.at[:tok_dev], sems.at[1])
+        ids_copy.start()
+        tokens_copy.start()
+        ids_copy.wait()
+        found = held_ref[...].astype(jnp.float32)
         tall = jnp.concatenate([found, jnp.zeros((picks, tok_dev), jnp.float32)], axis=0)
         wide = jnp.concatenate([tall, jnp.zeros((2 * picks, width - tok_dev), jnp.float32)], axis=1)
         out_ref[tok_dev:] = wide.astype(jnp.bfloat16)
+        tokens_copy.wait()
 
     return pl.pallas_call(
         body,
+        in_specs=[pl.BlockSpec(memory_space=pl.ANY)] * 2,
+        out_specs=pl.BlockSpec(memory_space=pltpu.VMEM),
         out_shape=jax.ShapeDtypeStruct((tok_dev + 2 * picks, width), jnp.bfloat16),
-        compiler_params=pltpu.CompilerParams(vmem_limit_bytes=4 * 2**20),
-        cost_estimate=pl.CostEstimate(flops=2 * tokens.size, bytes_accessed=4 * tokens.size, transcendentals=0),
+        scratch_shapes=[
+            pltpu.VMEM((picks, tok_dev), jnp.int32),
+            pltpu.SemaphoreType.DMA((2,)),
+        ],
+        cost_estimate=pl.CostEstimate(
+            flops=2 * tokens.size, bytes_accessed=4 * tokens.size, transcendentals=0
+        ),
     )(tokens, ids)
 
 

time: 240 us -> 240 us (level)
  the two profiles are of different devices: /device:TPU:86 before, /device:TPU:70 now
where the time goes in v8:
time: 240 us; the launch traced here: 239 us
  starting transfers between devices  82.5 us (34%)
  blocking collectives  71.8 us (30%)
  waiting for transfers between devices  68.7 us (29%)
  Pallas kernels  13 us (5%)
    all_gather x1, blocking collectives, layer(): gathered = lax.all_gather(payload, 'z', axis=0)  71.8 us
    ppermute x13, starting transfers between devices, onward(): return lax.ppermute(block, ('core', 'dp'), up + down)  64.4 us
    ppermute x13, waiting for transfers between devices, onward(): return lax.ppermute(block, ('core', 'dp'), up + down)  36.2 us
    all_to_all x1, waiting for transfers between devices, layer(): lax.all_to_all(result, 'z', split_axis=0, concat_axis=0, tiled=True)  25.3 us
    ppermute x6, starting transfers between devices, swap(): return lax.ppermute(block, 'core', [(0, 1), (1, 0)])  12.2 us
    pallas_call x8, Pallas kernels, weighted_sum(): pl.pallas_call(body, in_specs=[pl.BlockSpec(memory_space=pltpu.SMEM)] + [...  10.5 us
    ppermute x1, waiting for transfers between devices, across(): return lax.ppermute(block, ('core', 'dp'), up + down)  7.17 us
  transfers between devices with their start and end apart: 21, of which 11 were waited for; matrix products, arithmetic and copies ran while one was open for 0% of the time, Pallas kernels for 4%

profile of v8, /device:TPU:70, one launch (start us, length us, event | category | flops | bytes accessed | tf_op | source)
XLA Modules:
  0.0 239.4 jit_solution(13912388094348697291)
XLA Ops:
  1.5 71.8 %all-gather = bf16[1280,256]{1,0:T(8,128)(2,1)S(1)} all-gather(bf16[80,256]{1,0:T(8,128)(2,1)} %shard_map.64), channel_id=2, replica_groups=mesh['groups'=2,'z'=16,'core'=2,'dp'=8] {'z'}, dimensions={0}, use_global_device_ids=true | all-gather | bytes 696320 | tf_op jit(solution)/shard_map/all_gather | solution.py:229
  76.3 2.4 %collective-permute-start.4 = (bf16[2,192,2048]{2,1,0:T(8,128)(2,1)S(1)}, bf16[2,192,2048]{2,1,0:T(8,128)(2,1)S(1)}, u32[]{:S(2)}, u32[]{:S(2)}) collective-permute-start(bf16[2,192,2048]{2,1,0:T(8,128)(2,1)S(1)} %bitcast.11), channel_id=1, source_target_pairs={{0,8},{8,0},{1,9},{9,1},{2,10},{10,2},{3,11},{11,3},{4,12},{12,4},... | collective-permute-start | bytes 4718600 | tf_op jit(solution)/shard_map/ppermute | solution.py:13
  78.8 2.0 collective-permute-start.5
  80.7 4.8 %collective-permute-start.7 = (bf16[4,256,256]{2,1,0:T(8,128)(2,1)S(1)}, bf16[4,256,256]{2,1,0:T(8,128)(2,1)S(1)}, u32[]{:S(2)}, u32[]{:S(2)}) collective-permute-start(bf16[4,256,256]{2,1,0:T(8,128)(2,1)S(1)} %collective-permute-done.6), channel_id=1, source_target_pairs={{0,1},{1,2},{2,3},{3,4},{4,5},{5,6},{6,7},{7,0},{8,15},{9,8},{10,9... | collective-permute-start | bytes 1572872 | tf_op jit(solution)/shard_map/ppermute | solution.py:20
  85.5 6.7 %collective-permute-done.7.refs_0_ = bf16[4,256,256]{2,1,0:T(8,128)(2,1)S(1)} collective-permute-done((bf16[4,256,256]{2,1,0:T(8,128)(2,1)S(1)}, bf16[4,256,256]{2,1,0:T(8,128)(2,1)S(1)}, u32[]{:S(2)}, u32[]{:S(2)}) %collective-permute-start.7) | collective-permute-done | bytes 524320 | tf_op jit(solution)/shard_map/ppermute | solution.py:20
  92.2 5.6 %collective-permute-start.8 = (bf16[4,256,256]{2,1,0:T(8,128)(2,1)S(1)}, bf16[4,256,256]{2,1,0:T(8,128)(2,1)S(1)}, u32[]{:S(2)}, u32[]{:S(2)}) collective-permute-start(bf16[4,256,256]{2,1,0:T(8,128)(2,1)S(1)} %collective-permute-done.7.refs_0_), channel_id=1, source_target_pairs={{0,1},{1,2},{2,3},{3,4},{4,5},{5,6},{6,7},{7,0},{8,15},{9,8},{10,9... | collective-permute-start | bytes 1572872 | tf_op jit(solution)/shard_map/ppermute | solution.py:20
  99.8 4.7 %collective-permute-done.8.refs_1_ = bf16[4,256,256]{2,1,0:T(8,128)(2,1)S(1)} collective-permute-done((bf16[4,256,256]{2,1,0:T(8,128)(2,1)S(1)}, bf16[4,256,256]{2,1,0:T(8,128)(2,1)S(1)}, u32[]{:S(2)}, u32[]{:S(2)}) %collective-permute-start.8) | collective-permute-done | bytes 524320 | tf_op jit(solution)/shard_map/ppermute | solution.py:20
  104.5 5.6 %collective-permute-start.9 = (bf16[4,256,256]{2,1,0:T(8,128)(2,1)S(1)}, bf16[4,256,256]{2,1,0:T(8,128)(2,1)S(1)}, u32[]{:S(2)}, u32[]{:S(2)}) collective-permute-start(bf16[4,256,256]{2,1,0:T(8,128)(2,1)S(1)} %collective-permute-done.8.refs_1_), channel_id=1, source_target_pairs={{0,1},{1,2},{2,3},{3,4},{4,5},{5,6},{6,7},{7,0},{8,15},{9,8},{10,9... | collective-permute-start | bytes 1572872 | tf_op jit(solution)/shard_map/ppermute | solution.py:20
  110.1 5.6 %collective-permute-start.1 = (bf16[4,256,256]{2,1,0:T(8,128)(2,1)S(1)}, bf16[4,256,256]{2,1,0:T(8,128)(2,1)S(1)}, u32[]{:S(2)}, u32[]{:S(2)}) collective-permute-start(bf16[4,256,256]{2,1,0:T(8,128)(2,1)S(1)} %collective-permute-done.refs_1_), channel_id=1, source_target_pairs={{0,1},{1,2},{2,3},{3,4},{4,5},{5,6},{6,7},{7,0},{8,15},{9,8},{10,9... | collective-permute-start | bytes 1572872 | tf_op jit(solution)/shard_map/ppermute | solution.py:20
  122.4 5.6 %collective-permute-start.2 = (bf16[4,256,256]{2,1,0:T(8,128)(2,1)S(1)}, bf16[4,256,256]{2,1,0:T(8,128)(2,1)S(1)}, u32[]{:S(2)}, u32[]{:S(2)}) collective-permute-start(bf16[4,256,256]{2,1,0:T(8,128)(2,1)S(1)} %collective-permute-done.1.refs_2_), channel_id=1, source_target_pairs={{0,1},{1,2},{2,3},{3,4},{4,5},{5,6},{6,7},{7,0},{8,15},{9,8},{10,9... | collective-permute-start | bytes 1572872 | tf_op jit(solution)/shard_map/ppermute | solution.py:20
  128.1 6.7 %collective-permute-done.2.refs_0_ = bf16[4,256,256]{2,1,0:T(8,128)(2,1)S(1)} collective-permute-done((bf16[4,256,256]{2,1,0:T(8,128)(2,1)S(1)}, bf16[4,256,256]{2,1,0:T(8,128)(2,1)S(1)}, u32[]{:S(2)}, u32[]{:S(2)}) %collective-permute-start.2) | collective-permute-done | bytes 524320 | tf_op jit(solution)/shard_map/ppermute | solution.py:20
  134.7 5.6 %collective-permute-start.3 = (bf16[4,256,256]{2,1,0:T(8,128)(2,1)S(1)}, bf16[4,256,256]{2,1,0:T(8,128)(2,1)S(1)}, u32[]{:S(2)}, u32[]{:S(2)}) collective-permute-start(bf16[4,256,256]{2,1,0:T(8,128)(2,1)S(1)} %collective-permute-done.2.refs_0_), channel_id=1, source_target_pairs={{0,1},{1,2},{2,3},{3,4},{4,5},{5,6},{6,7},{7,0},{8,15},{9,8},{10,9... | collective-permute-start | bytes 1572872 | tf_op jit(solution)/shard_map/ppermute | solution.py:20
  144.1 3.0 %collective-permute-done.3.refs_1_ = bf16[4,256,256]{2,1,0:T(8,128)(2,1)S(1)} collective-permute-done((bf16[4,256,256]{2,1,0:T(8,128)(2,1)S(1)}, bf16[4,256,256]{2,1,0:T(8,128)(2,1)S(1)}, u32[]{:S(2)}, u32[]{:S(2)}) %collective-permute-start.3) | collective-permute-done | bytes 524320 | tf_op jit(solution)/shard_map/ppermute | solution.py:20
  150.5 7.2 %collective-permute-done.16.refs_0_ = bf16[4,192,256]{2,1,0:T(8,128)(2,1)S(1)} collective-permute-done((bf16[4,192,256]{2,1,0:T(8,128)(2,1)S(1)}, bf16[4,192,256]{2,1,0:T(8,128)(2,1)S(1)}, u32[]{:S(2)}, u32[]{:S(2)}) %collective-permute-start.16) | collective-permute-done | bytes 393248 | tf_op jit(solution)/shard_map/ppermute | solution.py:27
  157.7 6.8 %collective-permute-start.17 = (bf16[4,192,256]{2,1,0:T(8,128)(2,1)S(1)}, bf16[4,192,256]{2,1,0:T(8,128)(2,1)S(1)}, u32[]{:S(2)}, u32[]{:S(2)}) collective-permute-start(bf16[4,192,256]{2,1,0:T(8,128)(2,1)S(1)} %collective-permute-done.16.refs_0_), channel_id=1, source_target_pairs={{0,1},{1,2},{2,3},{3,4},{4,5},{5,6},{6,7},{7,0},{8,15},{9,8},{10,9... | collective-permute-start | bytes 1179656 | tf_op jit(solution)/shard_map/ppermute | solution.py:20
  166.4 3.3 %collective-permute-done.17.refs_1_ = bf16[4,192,256]{2,1,0:T(8,128)(2,1)S(1)} collective-permute-done((bf16[4,192,256]{2,1,0:T(8,128)(2,1)S(1)}, bf16[4,192,256]{2,1,0:T(8,128)(2,1)S(1)}, u32[]{:S(2)}, u32[]{:S(2)}) %collective-permute-start.17) | collective-permute-done | bytes 393248 | tf_op jit(solution)/shard_map/ppermute | solution.py:20
  169.8 5.6 %collective-permute-start.18 = (bf16[4,192,256]{2,1,0:T(8,128)(2,1)S(1)}, bf16[4,192,256]{2,1,0:T(8,128)(2,1)S(1)}, u32[]{:S(2)}, u32[]{:S(2)}) collective-permute-start(bf16[4,192,256]{2,1,0:T(8,128)(2,1)S(1)} %collective-permute-done.17.refs_1_), channel_id=1, source_target_pairs={{0,1},{1,2},{2,3},{3,4},{4,5},{5,6},{6,7},{7,0},{8,15},{9,8},{10,9... | collective-permute-start | bytes 1179656 | tf_op jit(solution)/shard_map/ppermute | solution.py:20
  175.4 4.2 %collective-permute-start.12 = (bf16[4,192,256]{2,1,0:T(8,128)(2,1)S(1)}, bf16[4,192,256]{2,1,0:T(8,128)(2,1)S(1)}, u32[]{:S(2)}, u32[]{:S(2)}) collective-permute-start(bf16[4,192,256]{2,1,0:T(8,128)(2,1)S(1)} %collective-permute-done.11.refs_1_), channel_id=1, source_target_pairs={{0,1},{1,2},{2,3},{3,4},{4,5},{5,6},{6,7},{7,0},{8,15},{9,8},{10,9... | collective-permute-start | bytes 1179656 | tf_op jit(solution)/shard_map/ppermute | solution.py:20
  185.1 5.4 %collective-permute-start.13 = (bf16[4,192,256]{2,1,0:T(8,128)(2,1)S(1)}, bf16[4,192,256]{2,1,0:T(8,128)(2,1)S(1)}, u32[]{:S(2)}, u32[]{:S(2)}) collective-permute-start(bf16[4,192,256]{2,1,0:T(8,128)(2,1)S(1)} %collective-permute-done.12.refs_2_), channel_id=1, source_target_pairs={{0,1},{1,2},{2,3},{3,4},{4,5},{5,6},{6,7},{7,0},{8,15},{9,8},{10,9... | collective-permute-start | bytes 1179656 | tf_op jit(solution)/shard_map/ppermute | solution.py:20
  190.5 5.3 %collective-permute-done.13.refs_0_ = bf16[4,192,256]{2,1,0:T(8,128)(2,1)S(1)} collective-permute-done((bf16[4,192,256]{2,1,0:T(8,128)(2,1)S(1)}, bf16[4,192,256]{2,1,0:T(8,128)(2,1)S(1)}, u32[]{:S(2)}, u32[]{:S(2)}) %collective-permute-start.13) | collective-permute-done | bytes 393248 | tf_op jit(solution)/shard_map/ppermute | solution.py:20
  195.8 5.6 %collective-permute-start.14 = (bf16[4,192,256]{2,1,0:T(8,128)(2,1)S(1)}, bf16[4,192,256]{2,1,0:T(8,128)(2,1)S(1)}, u32[]{:S(2)}, u32[]{:S(2)}) collective-permute-start(bf16[4,192,256]{2,1,0:T(8,128)(2,1)S(1)} %collective-permute-done.13.refs_0_), channel_id=1, source_target_pairs={{0,1},{1,2},{2,3},{3,4},{4,5},{5,6},{6,7},{7,0},{8,15},{9,8},{10,9... | collective-permute-start | bytes 1179656 | tf_op jit(solution)/shard_map/ppermute | solution.py:20
  202.6 4.1 %collective-permute-done.14.refs_1_ = bf16[4,192,256]{2,1,0:T(8,128)(2,1)S(1)} collective-permute-done((bf16[4,192,256]{2,1,0:T(8,128)(2,1)S(1)}, bf16[4,192,256]{2,1,0:T(8,128)(2,1)S(1)}, u32[]{:S(2)}, u32[]{:S(2)}) %collective-permute-start.14) | collective-permute-done | bytes 393248 | tf_op jit(solution)/shard_map/ppermute | solution.py:20
  208.5 4.0 %all-to-all-start = ((bf16[16,4,16,256]{3,2,1,0:T(8,128)(2,1)}), bf16[16,4,16,256]{3,2,1,0:T(8,128)(2,1)S(1)}, u32[]{:S(2)}, u32[]{:S(2)}) async-start(bf16[16,4,16,256]{3,2,1,0:T(8,128)(2,1)} %shard_map.73), calls=%async_computation | async-start | bytes 1048576 | tf_op jit(solution)/shard_map/all_to_all | solution.py:264
  213.2 25.3 %all-to-all-done = bf16[16,4,16,256]{3,2,1,0:T(8,128)(2,1)S(1)} async-done(((bf16[16,4,16,256]{3,2,1,0:T(8,128)(2,1)}), bf16[16,4,16,256]{3,2,1,0:T(8,128)(2,1)S(1)}, u32[]{:S(2)}, u32[]{:S(2)}) %all-to-all-start) | async-done | bytes 524320 | tf_op jit(solution)/shard_map/all_to_all | solution.py:264
  (49 shorter events, 32.1 us)
Async XLA Ops:
  0.0 76.3 %copy-start = (bf16[2,2048,192]{1,2,0:T(8,128)(2,1)S(1)}, bf16[2,2048,192]{1,2,0:T(8,128)(2,1)}, u32[]{:S(2)}) copy-start(bf16[2,2048,192]{1,2,0:T(8,128)(2,1)} %param.9) | copy-start | bytes 4718596
  74.4 6.4 %collective-permute-start.6 = (bf16[4,256,256]{2,1,0:T(8,128)(2,1)S(1)}, bf16[4,256,256]{2,1,0:T(8,128)(2,1)S(1)}, u32[]{:S(2)}, u32[]{:S(2)}) collective-permute-start(bf16[4,256,256]{2,1,0:T(8,128)(2,1)S(1)} %shard_map.65.refs_0_), channel_id=1, source_target_pairs={{0,8},{8,0},{1,9},{9,1},{2,10},{10,2},{3,11},{11,3},{4,12},{12,4},... | collective-permute-start | bytes 1572872 | tf_op jit(solution)/shard_map/ppermute | solution.py:13
  76.3 39.4 %collective-permute-start.4 = (bf16[2,192,2048]{2,1,0:T(8,128)(2,1)S(1)}, bf16[2,192,2048]{2,1,0:T(8,128)(2,1)S(1)}, u32[]{:S(2)}, u32[]{:S(2)}) collective-permute-start(bf16[2,192,2048]{2,1,0:T(8,128)(2,1)S(1)} %bitcast.11), channel_id=1, source_target_pairs={{0,8},{8,0},{1,9},{9,1},{2,10},{10,2},{3,11},{11,3},{4,12},{12,4},... | collective-permute-start | bytes 4718600 | tf_op jit(solution)/shard_map/ppermute | solution.py:13
  78.8 37.0 %collective-permute-start.5 = (bf16[2,192,2048]{2,1,0:T(8,128)(2,1)}, bf16[2,192,2048]{2,1,0:T(8,128)(2,1)S(1)}, u32[]{:S(2)}, u32[]{:S(2)}) collective-permute-start(bf16[2,192,2048]{2,1,0:T(8,128)(2,1)} %bitcast.16), channel_id=1, source_target_pairs={{0,8},{8,0},{1,9},{9,1},{2,10},{10,2},{3,11},{11,3},{4,12},{12,4},... | collective-permute-start | bytes 4718600 | tf_op jit(solution)/shard_map/ppermute | solution.py:13
  80.7 11.5 %collective-permute-start.7 = (bf16[4,256,256]{2,1,0:T(8,128)(2,1)S(1)}, bf16[4,256,256]{2,1,0:T(8,128)(2,1)S(1)}, u32[]{:S(2)}, u32[]{:S(2)}) collective-permute-start(bf16[4,256,256]{2,1,0:T(8,128)(2,1)S(1)} %collective-permute-done.6), channel_id=1, source_target_pairs={{0,1},{1,2},{2,3},{3,4},{4,5},{5,6},{6,7},{7,0},{8,15},{9,8},{10,9... | collective-permute-start | bytes 1572872 | tf_op jit(solution)/shard_map/ppermute | solution.py:20
  92.2 12.3 %collective-permute-start.8 = (bf16[4,256,256]{2,1,0:T(8,128)(2,1)S(1)}, bf16[4,256,256]{2,1,0:T(8,128)(2,1)S(1)}, u32[]{:S(2)}, u32[]{:S(2)}) collective-permute-start(bf16[4,256,256]{2,1,0:T(8,128)(2,1)S(1)} %collective-permute-done.7.refs_0_), channel_id=1, source_target_pairs={{0,1},{1,2},{2,3},{3,4},{4,5},{5,6},{6,7},{7,0},{8,15},{9,8},{10,9... | collective-permute-start | bytes 1572872 | tf_op jit(solution)/shard_map/ppermute | solution.py:20
  97.8 12.3 %collective-permute-start = (bf16[4,256,256]{2,1,0:T(8,128)(2,1)S(1)}, bf16[4,256,256]{2,1,0:T(8,128)(2,1)S(1)}, u32[]{:S(2)}, u32[]{:S(2)}) collective-permute-start(bf16[4,256,256]{2,1,0:T(8,128)(2,1)S(1)} %shard_map.65.refs_0_), channel_id=1, source_target_pairs={{0,1},{1,2},{2,3},{3,4},{4,5},{5,6},{6,7},{7,0},{8,15},{9,8},{10,9... | collective-permute-start | bytes 1572872 | tf_op jit(solution)/shard_map/ppermute | solution.py:20
  104.5 14.1 %collective-permute-start.9 = (bf16[4,256,256]{2,1,0:T(8,128)(2,1)S(1)}, bf16[4,256,256]{2,1,0:T(8,128)(2,1)S(1)}, u32[]{:S(2)}, u32[]{:S(2)}) collective-permute-start(bf16[4,256,256]{2,1,0:T(8,128)(2,1)S(1)} %collective-permute-done.8.refs_1_), channel_id=1, source_target_pairs={{0,1},{1,2},{2,3},{3,4},{4,5},{5,6},{6,7},{7,0},{8,15},{9,8},{10,9... | collective-permute-start | bytes 1572872 | tf_op jit(solution)/shard_map/ppermute | solution.py:20
  110.1 12.3 %collective-permute-start.1 = (bf16[4,256,256]{2,1,0:T(8,128)(2,1)S(1)}, bf16[4,256,256]{2,1,0:T(8,128)(2,1)S(1)}, u32[]{:S(2)}, u32[]{:S(2)}) collective-permute-start(bf16[4,256,256]{2,1,0:T(8,128)(2,1)S(1)} %collective-permute-done.refs_1_), channel_id=1, source_target_pairs={{0,1},{1,2},{2,3},{3,4},{4,5},{5,6},{6,7},{7,0},{8,15},{9,8},{10,9... | collective-permute-start | bytes 1572872 | tf_op jit(solution)/shard_map/ppermute | solution.py:20
  118.6 21.8 %copy-start.3 = (bf16[2,1536,256]{2,1,0:T(8,128)(2,1)S(1)}, bf16[2,1536,256]{2,1,0:T(8,128)(2,1)}, u32[]{:S(2)}) copy-start(bf16[2,1536,256]{2,1,0:T(8,128)(2,1)} %refs_2_.3) | copy-start | bytes 4718596
  118.6 23.8 %copy-start.2 = (bf16[2,2048,192]{1,2,0:T(8,128)(2,1)S(1)}, bf16[2,2048,192]{1,2,0:T(8,128)(2,1)}, u32[]{:S(2)}) copy-start(bf16[2,2048,192]{1,2,0:T(8,128)(2,1)} %param.10) | copy-start | bytes 4718596
  119.6 27.4 %collective-permute-start.10 = (f32[4,384,256]{2,1,0:T(8,128)S(1)}, f32[4,384,256]{2,1,0:T(8,128)S(1)}, u32[]{:S(2)}, u32[]{:S(2)}) collective-permute-start(f32[4,384,256]{2,1,0:T(8,128)S(1)} %shard_map.68), channel_id=1, source_target_pairs={{0,8},{8,0},{1,9},{9,1},{2,10},{10,2},{3,11},{11,3},{4,12},{12,4},... | collective-permute-start | bytes 4718600 | tf_op jit(solution)/shard_map/ppermute | solution.py:13
  122.4 12.3 %collective-permute-start.2 = (bf16[4,256,256]{2,1,0:T(8,128)(2,1)S(1)}, bf16[4,256,256]{2,1,0:T(8,128)(2,1)S(1)}, u32[]{:S(2)}, u32[]{:S(2)}) collective-permute-start(bf16[4,256,256]{2,1,0:T(8,128)(2,1)S(1)} %collective-permute-done.1.refs_2_), channel_id=1, source_target_pairs={{0,1},{1,2},{2,3},{3,4},{4,5},{5,6},{6,7},{7,0},{8,15},{9,8},{10,9... | collective-permute-start | bytes 1572872 | tf_op jit(solution)/shard_map/ppermute | solution.py:20
  134.7 12.3 %collective-permute-start.3 = (bf16[4,256,256]{2,1,0:T(8,128)(2,1)S(1)}, bf16[4,256,256]{2,1,0:T(8,128)(2,1)S(1)}, u32[]{:S(2)}, u32[]{:S(2)}) collective-permute-start(bf16[4,256,256]{2,1,0:T(8,128)(2,1)S(1)} %collective-permute-done.2.refs_0_), channel_id=1, source_target_pairs={{0,1},{1,2},{2,3},{3,4},{4,5},{5,6},{6,7},{7,0},{8,15},{9,8},{10,9... | collective-permute-start | bytes 1572872 | tf_op jit(solution)/shard_map/ppermute | solution.py:20
  140.4 39.2 %collective-permute-start.15 = (bf16[2,1536,256]{2,1,0:T(8,128)(2,1)S(1)}, bf16[2,1536,256]{2,1,0:T(8,128)(2,1)S(1)}, u32[]{:S(2)}, u32[]{:S(2)}) collective-permute-start(bf16[2,1536,256]{2,1,0:T(8,128)(2,1)S(1)} %copy-done.3), channel_id=1, source_target_pairs={{0,8},{8,0},{1,9},{9,1},{2,10},{10,2},{3,11},{11,3},{4,12},{12,4},... | collective-permute-start | bytes 4718600 | tf_op jit(solution)/shard_map/ppermute | solution.py:13
  148.5 9.1 %collective-permute-start.16 = (bf16[4,192,256]{2,1,0:T(8,128)(2,1)S(1)}, bf16[4,192,256]{2,1,0:T(8,128)(2,1)S(1)}, u32[]{:S(2)}, u32[]{:S(2)}) collective-permute-start(bf16[4,192,256]{2,1,0:T(8,128)(2,1)S(1)} %shard_map.69.refs_0_), channel_id=1, source_target_pairs={{8,1},{9,2},{10,3},{11,4},{12,5},{13,6},{14,7},{15,0},{0,15},{1,8}... | collective-permute-start | bytes 1179656 | tf_op jit(solution)/shard_map/ppermute | solution.py:27
  157.7 12.1 %collective-permute-start.17 = (bf16[4,192,256]{2,1,0:T(8,128)(2,1)S(1)}, bf16[4,192,256]{2,1,0:T(8,128)(2,1)S(1)}, u32[]{:S(2)}, u32[]{:S(2)}) collective-permute-start(bf16[4,192,256]{2,1,0:T(8,128)(2,1)S(1)} %collective-permute-done.16.refs_0_), channel_id=1, source_target_pairs={{0,1},{1,2},{2,3},{3,4},{4,5},{5,6},{6,7},{7,0},{8,15},{9,8},{10,9... | collective-permute-start | bytes 1179656 | tf_op jit(solution)/shard_map/ppermute | solution.py:20
  164.5 10.9 %collective-permute-start.11 = (bf16[4,192,256]{2,1,0:T(8,128)(2,1)S(1)}, bf16[4,192,256]{2,1,0:T(8,128)(2,1)S(1)}, u32[]{:S(2)}, u32[]{:S(2)}) collective-permute-start(bf16[4,192,256]{2,1,0:T(8,128)(2,1)S(1)} %shard_map.69.refs_0_), channel_id=1, source_target_pairs={{0,1},{1,2},{2,3},{3,4},{4,5},{5,6},{6,7},{7,0},{8,15},{9,8},{10,9... | collective-permute-start | bytes 1179656 | tf_op jit(solution)/shard_map/ppermute | solution.py:20
  169.8 10.9 %collective-permute-start.18 = (bf16[4,192,256]{2,1,0:T(8,128)(2,1)S(1)}, bf16[4,192,256]{2,1,0:T(8,128)(2,1)S(1)}, u32[]{:S(2)}, u32[]{:S(2)}) collective-permute-start(bf16[4,192,256]{2,1,0:T(8,128)(2,1)S(1)} %collective-permute-done.17.refs_1_), channel_id=1, source_target_pairs={{0,1},{1,2},{2,3},{3,4},{4,5},{5,6},{6,7},{7,0},{8,15},{9,8},{10,9... | collective-permute-start | bytes 1179656 | tf_op jit(solution)/shard_map/ppermute | solution.py:20
  175.4 9.7 %collective-permute-start.12 = (bf16[4,192,256]{2,1,0:T(8,128)(2,1)S(1)}, bf16[4,192,256]{2,1,0:T(8,128)(2,1)S(1)}, u32[]{:S(2)}, u32[]{:S(2)}) collective-permute-start(bf16[4,192,256]{2,1,0:T(8,128)(2,1)S(1)} %collective-permute-done.11.refs_1_), channel_id=1, source_target_pairs={{0,1},{1,2},{2,3},{3,4},{4,5},{5,6},{6,7},{7,0},{8,15},{9,8},{10,9... | collective-permute-start | bytes 1179656 | tf_op jit(solution)/shard_map/ppermute | solution.py:20
  181.6 25.1 %collective-permute-start.19 = (f32[4,256,256]{2,1,0:T(8,128)S(1)}, f32[4,256,256]{2,1,0:T(8,128)S(1)}, u32[]{:S(2)}, u32[]{:S(2)}) collective-permute-start(f32[4,256,256]{2,1,0:T(8,128)S(1)} %shard_map.72), channel_id=1, source_target_pairs={{0,8},{8,0},{1,9},{9,1},{2,10},{10,2},{3,11},{11,3},{4,12},{12,4},... | collective-permute-start | bytes 3145736 | tf_op jit(solution)/shard_map/ppermute | solution.py:13
  185.1 10.7 %collective-permute-start.13 = (bf16[4,192,256]{2,1,0:T(8,128)(2,1)S(1)}, bf16[4,192,256]{2,1,0:T(8,128)(2,1)S(1)}, u32[]{:S(2)}, u32[]{:S(2)}) collective-permute-start(bf16[4,192,256]{2,1,0:T(8,128)(2,1)S(1)} %collective-permute-done.12.refs_2_), channel_id=1, source_target_pairs={{0,1},{1,2},{2,3},{3,4},{4,5},{5,6},{6,7},{7,0},{8,15},{9,8},{10,9... | collective-permute-start | bytes 1179656 | tf_op jit(solution)/shard_map/ppermute | solution.py:20
  195.8 10.9 %collective-permute-start.14 = (bf16[4,192,256]{2,1,0:T(8,128)(2,1)S(1)}, bf16[4,192,256]{2,1,0:T(8,128)(2,1)S(1)}, u32[]{:S(2)}, u32[]{:S(2)}) collective-permute-start(bf16[4,192,256]{2,1,0:T(8,128)(2,1)S(1)} %collective-permute-done.13.refs_0_), channel_id=1, source_target_pairs={{0,1},{1,2},{2,3},{3,4},{4,5},{5,6},{6,7},{7,0},{8,15},{9,8},{10,9... | collective-permute-start | bytes 1179656 | tf_op jit(solution)/shard_map/ppermute | solution.py:20
  208.5 30.0 %all-to-all-start = ((bf16[16,4,16,256]{3,2,1,0:T(8,128)(2,1)}), bf16[16,4,16,256]{3,2,1,0:T(8,128)(2,1)S(1)}, u32[]{:S(2)}, u32[]{:S(2)}) async-start(bf16[16,4,16,256]{3,2,1,0:T(8,128)(2,1)} %shard_map.73), calls=%async_computation | async-start | bytes 1048576 | tf_op jit(solution)/shard_map/all_to_all | solution.py:264
  (3 other events, 21.5 us)
